TPU v7x, 128 devices: a whole 4x4x4 slice. The times are simulated.
128 devices in a mesh: dp: 16 (over y, z), tensor: 8 (over x, core).
Axes of the slice: x: 4, y: 4, z: 4, core: 2. Of those that a mesh axis runs over, the one named last changes fastest.
Arguments:
- patches: bfloat16 [16384, 1280], P(('dp', 'tensor')), may hold values from -12 to 12
- ln_gain: float32 [1280], replicated, may hold values from 0.5 to 1.5
- ln_bias: float32 [1280], replicated, may hold values from -1.8 to 1.8
- fc1_weight: bfloat16 [5120, 2560], P(None, 'tensor'), may hold values from -0.078125 to 0.078125
- fc1_bias: float32 [2560], P('tensor'), may hold values from -3 to 3
- fc2_weight: bfloat16 [2560, 8192], P('tensor'), may hold values from -0.125 to 0.125
- fc2_bias: float32 [8192], replicated, may hold values from -3 to 3
- image_counts: int32 [128, 4], P(('dp', 'tensor')), may hold values from 0 to 32, as said below
- image_positions: int32 [4096], P(('dp', 'tensor')), may hold values from 0 to 16383, as said below
- text_embeds: bfloat16 [16384, 8192], P(('dp', 'tensor')), may hold values from -6 to 6
- keep_mask: int32 [16384, 8192], P(('dp', 'tensor')), may hold values 0 or 1
- norm_gain: float32 [8192], replicated, may hold values from 0.25 to 1.75
- qkv_weight: bfloat16 [8192, 10240], P('dp', 'tensor'), may hold values from -0.0625 to 0.0625
- qkv_bias: float32 [10240], P('tensor'), may hold values from -3 to 3
Outputs:
- stream: bfloat16 [16384, 8192], P(('dp', 'tensor'))
- queries: bfloat16 [16384, 8192], P('dp', 'tensor')
- keys: bfloat16 [16384, 1024], P('dp', 'tensor')
- values: bfloat16 [16384, 1024], P('dp', 'tensor')
Inputs may be any that keep to these rules, and one draw needn't show every extreme that they name: `image_counts`: A multiple of 4. In a shard, the images after its first empty one are empty. The counts of one shard sum to at most 128, which one shard reaches in every draw. `image_positions`: all slots name distinct positions. Position p lies on the device of index p // 128 of dp+tensor. The slots of a shard name positions only on devices with the shard's tensor index, exactly 2 on each of them, so every such device receives 2 slots from each shard.
All inputs are finite; a program needn't handle non-finite values. No bound on the sum of `keep_mask` on one device may be relied on, other than what follows from the above.
Results may differ from a plain program's by a relative error of at most 0.0075.
Values may be sent and summed in bfloat16 or wider, within the bound.
No kernel may reach another device: no remote copies, remote signals or barrier semaphores. Data moves between devices by JAX's collectives and lax.ppermute only.
A program may use at most 128 MiB of HBM per device.

v0:
```python
import jax
import jax.numpy as jnp
from jax import lax
from jax.sharding import PartitionSpec as P

HEADS = 64
KV_HEADS = 8
HEAD_DIM = 128


KEEP_SCALE = 1.0 / 0.9


def layer_norm(inputs, gain, bias):
    widened = inputs.astype(jnp.float32)
    center = jnp.mean(widened, axis=-1, keepdims=True)
    spread = jnp.mean((widened - center) * (widened - center), axis=-1, keepdims=True)
    return (widened - center) * lax.rsqrt(spread + 1e-06) * gain + bias


def rms_norm(inputs, gain):
    widened = inputs.astype(jnp.float32)
    inverse = lax.rsqrt(jnp.mean(widened * widened, axis=-1, keepdims=True) + 1e-06)
    return (widened * inverse * gain).astype(jnp.bfloat16)


def merger(rows_in, fc1_weight, fc1_bias, fc2_weight, fc2_bias):
    product = (
        jnp.dot(
            lax.all_gather(rows_in, "tensor", axis=0, tiled=True),
            fc1_weight,
            preferred_element_type=jnp.float32,
        )
        + fc1_bias
    )
    hidden = jax.nn.gelu(product, approximate=False).astype(jnp.bfloat16)
    summed = lax.psum_scatter(
        jnp.dot(hidden, fc2_weight, preferred_element_type=jnp.float32).astype(jnp.bfloat16),
        "tensor",
        scatter_dimension=0,
        tiled=True,
    ).astype(jnp.float32)
    return (summed + fc2_bias).astype(jnp.bfloat16)


def route_plan(image_counts, image_positions, rows_here, groups, tensor_devs):
    slot_total = image_positions.shape[0]
    per_peer = slot_total // groups
    live_slots = jnp.sum(image_counts) // 4
    usable = jnp.arange(slot_total, dtype=jnp.int32) < live_slots
    owner_dev = image_positions // rows_here
    owner_group = owner_dev // tensor_devs
    owner_row = jnp.where(usable, image_positions % rows_here, -1)
    member = (owner_group[:, None] == jnp.arange(groups, dtype=jnp.int32)[None, :]).astype(
        jnp.int32
    )
    slot_rank = jnp.sum(member * (jnp.cumsum(member, axis=0) - 1), axis=1)
    out_slot = owner_group * per_peer + slot_rank
    chooser = out_slot[None, :] == jnp.arange(slot_total, dtype=jnp.int32)[:, None]
    send_rows = jnp.sum(jnp.where(chooser, owner_row[None, :], 0), axis=1)
    return (chooser.astype(jnp.bfloat16), send_rows.reshape(groups, per_peer))


def arrange(payload, chooser, groups):
    ordered = jnp.dot(chooser, payload, preferred_element_type=jnp.float32).astype(jnp.bfloat16)
    return ordered.reshape(groups, payload.shape[0] // groups, payload.shape[1])


def land(arrived, arrived_rows, text_rows):
    landing = arrived_rows[None, :] == jnp.arange(text_rows.shape[0], dtype=jnp.int32)[:, None]
    covered = jnp.any(landing, axis=1)
    placed = jnp.dot(
        landing.astype(jnp.bfloat16), arrived, preferred_element_type=jnp.float32
    ).astype(jnp.bfloat16)
    return jnp.where(covered[:, None], placed, text_rows)


def shards(
    patches,
    ln_gain,
    ln_bias,
    fc1_weight,
    fc1_bias,
    fc2_weight,
    fc2_bias,
    image_counts,
    image_positions,
    text_embeds,
    keep_mask,
    norm_gain,
    qkv_weight,
    qkv_bias,
):
    groups = lax.axis_size("dp")
    rows_here = text_embeds.shape[0]
    patch_normed = layer_norm(patches, ln_gain, ln_bias).astype(jnp.bfloat16)
    merged_in = patch_normed.reshape(-1, 4 * patches.shape[1])
    chooser, send_rows = route_plan(
        image_counts, image_positions, rows_here, groups, lax.axis_size("tensor")
    )
    merged_tokens = merger(merged_in, fc1_weight, fc1_bias, fc2_weight, fc2_bias)
    outgoing = arrange(merged_tokens, chooser, groups)
    arrived, arrived_rows = (
        lax.all_to_all(outgoing, "dp", split_axis=0, concat_axis=0, tiled=True),
        lax.all_to_all(send_rows, "dp", split_axis=0, concat_axis=0, tiled=True),
    )
    images = arrived.reshape(-1, arrived.shape[-1])
    placed = land(images, arrived_rows.reshape(-1), text_embeds)
    stream = (placed.astype(jnp.float32) * keep_mask.astype(jnp.float32) * KEEP_SCALE).astype(
        jnp.bfloat16
    )
    normed = lax.all_gather(rms_norm(stream, norm_gain), "tensor", axis=0, tiled=True)
    projected = (
        jnp.dot(
            normed,
            lax.all_gather(qkv_weight, "dp", axis=0, tiled=True),
            preferred_element_type=jnp.float32,
        )
        + qkv_bias
    )
    group_width = (HEADS // KV_HEADS + 2) * HEAD_DIM
    grouped = projected.reshape(normed.shape[0], -1, group_width)
    query_width = HEADS // KV_HEADS * HEAD_DIM
    queries = grouped[:, :, :query_width].reshape(normed.shape[0], -1).astype(jnp.bfloat16)
    keys = (
        grouped[:, :, query_width : query_width + HEAD_DIM]
        .reshape(normed.shape[0], -1)
        .astype(jnp.bfloat16)
    )
    values = (
        grouped[:, :, query_width + HEAD_DIM :].reshape(normed.shape[0], -1).astype(jnp.bfloat16)
    )
    return (stream, queries, keys, values)


def solution(mesh):
    placed = (
        P(("dp", "tensor"), None),
        P(),
        P(),
        P(None, "tensor"),
        P("tensor"),
        P("tensor", None),
        P(),
        P(("dp", "tensor"), None),
        P(("dp", "tensor")),
        P(("dp", "tensor"), None),
        P(("dp", "tensor"), None),
        P(),
        P("dp", "tensor"),
        P("tensor"),
    )
    return jax.shard_map(
        shards,
        mesh=mesh,
        in_specs=placed,
        out_specs=(
            P(("dp", "tensor"), None),
            P("dp", "tensor"),
            P("dp", "tensor"),
            P("dp", "tensor"),
        ),
        check_vma=False,
    )
```

profile of v0, /device:TPU:1, one launch (start us, length us, event | category | flops | bytes accessed | tf_op | source)
XLA Modules:
  0.0 318.2 jit_solution(12399917112263050034)
XLA Ops:
  8.0 0.0 copy-start
  8.0 0.0 all-gather.4.cloned.1.call-start
  8.1 1.2 convert_reduce_fusion
  9.3 1.2 fusion.11
  10.5 2.0 fusion.14
  12.5 1.9 reshape.62
  14.4 0.0 all-gather.4.cloned.1.call-update
  14.4 0.0 reduce-scatter.2.cloned.1.call-start
  14.5 29.7 %all-gather.4.cloned.1.call-done = bf16[256,5120]{1,0:T(8,128)(2,1)} async-done(((bf16[32,5120]{1,0:T(8,128)(2,1)}), bf16[256,5120]{1,0:T(8,128)(2,1)}) %all-gather.4.cloned.1.call-update) | async-done | bytes 2621456 | tf_op jit(solution)/shard_map/all_gather | solution.py:30
  44.2 0.0 copy-done
  44.2 11.0 %convolution_convert_fusion = bf16[256,8192]{1,0:T(8,128)(2,1)} fusion(bf16[320,8192]{1,0:T(8,128)(2,1)} %param.19, bf16[256,5120]{1,0:T(8,128)(2,1)} %all-gather.4.cloned.1.call-done, bf16[5120,320]{0,1:T(8,128)(2,1)S(1)} %copy-done, f32[320]{0:T(512)} %param.18), kind=kOutput, calls=%fused_computation | convolution fusion | flops 2188541952 | bytes 15336704 | tf_op jit(solution)/shard_map/dot_general | solution.py:38
  55.1 0.0 copy-start.7
  55.1 0.0 copy-start.5
  55.1 0.0 copy-start.4
  55.1 0.0 reduce-scatter.2.cloned.1.call-update
  55.1 0.0 all-gather.8.cloned.1.call-start
  55.2 0.5 all-gather.8.cloned.1.call-update
  55.7 0.0 copy-done.7
  55.8 0.6 reduce_sum.55
  59.0 0.0 copy-done.5
  59.0 0.1 fusion.52
  59.1 0.1 reduce_window_sum.11
  59.2 0.2 select_reduce_fusion.1
  59.4 0.1 select_reduce_fusion
  59.5 0.7 all_to_all.9
  60.2 6.7 %all-to-all-start = ((s32[16,1,2]{2,1,0:T(1,128)}), s32[16,1,2]{2,1,0:T(1,128)S(1)}, u32[]{:S(2)}, u32[]{:S(2)}) async-start(s32[16,1,2]{2,1,0:T(1,128)} %bitcast), calls=%async_computation | async-start | bytes 16384 | tf_op jit(solution)/shard_map/all_to_all | solution.py:105
  66.9 24.2 %reduce-scatter.2.cloned.1.call-done = bf16[32,8192]{1,0:T(8,128)(2,1)} async-done(((bf16[256,8192]{1,0:T(8,128)(2,1)}), bf16[32,8192]{1,0:T(8,128)(2,1)}) %reduce-scatter.2.cloned.1.call-update) | async-done | bytes 524304 | tf_op jit(solution)/shard_map/reduce_scatter | solution.py:37
  91.0 0.0 copy-done.4
  91.0 1.3 convolution_convert_fusion.2
  92.4 1.1 reshape.63
  93.5 0.0 all-to-all-done
  93.5 6.6 %all-to-all-start.1 = ((bf16[16,2,8192]{2,1,0:T(2,128)(2,1)}), bf16[16,2,8192]{2,1,0:T(2,128)(2,1)S(1)}, u32[]{:S(2)}, u32[]{:S(2)}) async-start(bf16[16,2,8192]{2,1,0:T(2,128)(2,1)} %reshape.63), calls=%async_computation.2 | async-start | bytes 1048576 | tf_op jit(solution)/shard_map/all_to_all | solution.py:104
  100.1 0.2 all-gather.6.cloned.1.call-start
  100.4 0.5 broadcast.106
  100.9 0.7 reduce.3
  101.6 0.1 eq.49
  101.6 0.1 fusion.51
  101.7 7.2 %all-to-all-done.1 = bf16[16,2,8192]{2,1,0:T(2,128)(2,1)S(1)} async-done(((bf16[16,2,8192]{2,1,0:T(2,128)(2,1)}), bf16[16,2,8192]{2,1,0:T(2,128)(2,1)S(1)}, u32[]{:S(2)}, u32[]{:S(2)}) %all-to-all-start.1) | async-done | bytes 524320 | tf_op jit(solution)/shard_map/all_to_all | solution.py:104
  108.9 0.2 reshape.64
  109.1 0.0 copy-start.3
  109.2 4.4 %fusion.5 = (f32[128]{0:T(128)S(1)}, bf16[128,8192]{1,0:T(8,128)(2,1)S(1)}) fusion(s32[128,8192]{1,0:T(8,128)} %param.24, bf16[128,8192]{1,0:T(8,128)(2,1)} %param.23, bf16[32,8192]{1,0:T(8,128)(2,1)S(1)} %reshape.64, s32[32]{0:T(128)S(1)} %eq.49, pred[128]{0:T(512)(128)(4,1)S(1)} %fusion.51), kind=kOutput, calls=%fused_computation.11 | convolution fusion | flops 77598592 | bytes 8913664 | tf_op jit(solution)/shard_map/dot_general | solution.py:72
  113.6 0.0 copy-start.2
  113.6 0.0 copy-start.6
  113.6 1.3 copy-done.2
  114.9 0.0 copy-done.3
  114.9 1.9 fusion.7
  116.8 0.0 all-gather.6.cloned.1.call-update
  116.9 78.6 %all-gather.8.cloned.1.call-done = bf16[8192,1280]{1,0:T(8,128)(2,1)} async-done(((bf16[512,1280]{1,0:T(8,128)(2,1)}), bf16[8192,1280]{1,0:T(8,128)(2,1)}) %all-gather.8.cloned.1.call-update) | async-done | bytes 20971536 | tf_op jit(solution)/shard_map/all_gather | solution.py:116
  195.4 86.3 %all-gather.6.cloned.1.call-done = bf16[1024,8192]{1,0:T(8,128)(2,1)} async-done(((bf16[128,8192]{1,0:T(8,128)(2,1)}), bf16[1024,8192]{1,0:T(8,128)(2,1)}) %all-gather.6.cloned.1.call-update) | async-done | bytes 16777232 | tf_op jit(solution)/shard_map/all_gather | solution.py:112
  281.8 0.0 copy-done.6
  281.8 0.0 copy-start.1
  281.8 26.6 %fusion.8 = bf16[1024,1,1280]{2,0,1:T(8,128)(2,1)S(1)} fusion(bf16[1024,8192]{1,0:T(8,128)(2,1)} %all-gather.6.cloned.1.call-done, bf16[8192,1280]{1,0:T(8,128)(2,1)} %all-gather.8.cloned.1.call-done, f32[1280]{0:T(1024)S(1)} %copy-done.6), kind=kOutput, calls=%fused_computation.14 | convolution fusion | flops 21477457920 | bytes 40375296 | tf_op jit(solution)/shard_map/dot_general | solution.py:114
  308.4 0.8 slice_bitcast_fusion.1
  309.2 1.6 slice_bitcast_fusion
  310.8 0.0 copy-done.1
  (5 shorter events, 0.0 us)
Async XLA Ops:
  8.0 36.2 %copy-start = (bf16[5120,320]{0,1:T(8,128)(2,1)S(1)}, bf16[5120,320]{0,1:T(8,128)(2,1)}, u32[]{:S(2)}) copy-start(bf16[5120,320]{0,1:T(8,128)(2,1)} %param.17) | copy-start | bytes 9830404
  8.0 36.1 %all-gather.4.cloned.1.call-start = ((), (), s32[]{:S(2)}) async-start(), calls=%async_computation.3 | async-start | bytes 2949120 | tf_op jit(solution)/shard_map/all_gather | solution.py:30
  14.4 76.6 %reduce-scatter.2.cloned.1.call-start = ((), (), s32[]{:S(2)}) async-start(), calls=%async_computation.4 | async-start | bytes 4718592 | tf_op jit(solution)/shard_map/reduce_scatter | solution.py:37
  55.1 0.7 copy-start.7
  55.1 3.9 %copy-start.5 = (s32[32]{0:T(128)S(1)}, s32[32]{0:T(128)}, u32[]{:S(2)}) copy-start(s32[32]{0:T(128)} %param.22) | copy-start | bytes 388
  55.1 35.9 %copy-start.4 = (f32[8192]{0:T(1024)S(1)}, f32[8192]{0:T(1024)}, u32[]{:S(2)}) copy-start(f32[8192]{0:T(1024)} %param.20) | copy-start | bytes 98308
  55.1 140.3 %all-gather.8.cloned.1.call-start = ((), (), s32[]{:S(2)}) async-start(), calls=%async_computation.6 | async-start | bytes 22282240 | tf_op jit(solution)/shard_map/all_gather | solution.py:116
  60.2 33.3 %all-to-all-start = ((s32[16,1,2]{2,1,0:T(1,128)}), s32[16,1,2]{2,1,0:T(1,128)S(1)}, u32[]{:S(2)}, u32[]{:S(2)}) async-start(s32[16,1,2]{2,1,0:T(1,128)} %bitcast), calls=%async_computation | async-start | bytes 16384 | tf_op jit(solution)/shard_map/all_to_all | solution.py:105
  93.5 15.4 %all-to-all-start.1 = ((bf16[16,2,8192]{2,1,0:T(2,128)(2,1)}), bf16[16,2,8192]{2,1,0:T(2,128)(2,1)S(1)}, u32[]{:S(2)}, u32[]{:S(2)}) async-start(bf16[16,2,8192]{2,1,0:T(2,128)(2,1)} %reshape.63), calls=%async_computation.2 | async-start | bytes 1048576 | tf_op jit(solution)/shard_map/all_to_all | solution.py:104
  100.1 181.6 %all-gather.6.cloned.1.call-start = ((), (), s32[]{:S(2)}) async-start(), calls=%async_computation.5 | async-start | bytes 18874368 | tf_op jit(solution)/shard_map/all_gather | solution.py:112
  109.1 5.8 %copy-start.3 = (f32[8192]{0:T(1024)S(1)}, f32[8192]{0:T(1024)}, u32[]{:S(2)}) copy-start(f32[8192]{0:T(1024)} %param.25) | copy-start | bytes 98308
  113.6 1.3 copy-start.2
  113.6 168.1 %copy-start.6 = (f32[1280]{0:T(1024)S(1)}, f32[1280]{0:T(1024)}, u32[]{:S(2)}) copy-start(f32[1280]{0:T(1024)} %param.27) | copy-start | bytes 15364
  281.8 29.1 %copy-start.1 = (bf16[5120,320]{0,1:T(8,128)(2,1)S(1)}, bf16[5120,320]{0,1:T(8,128)(2,1)}, u32[]{:S(2)}) copy-start(bf16[5120,320]{0,1:T(8,128)(2,1)} %param.17) | copy-start | bytes 9830404
Sparse Core Ops, SparseCore 0:
  14.6 29.5 all-gather.3
  55.3 35.7 reduce-scatter.1
Sparse Core Ops, SparseCore 1:
  57.8 137.6 all-gather.7
  197.6 84.1 all-gather.5
where the time goes:
time: 319 us; the launch traced here: 318 us
  waiting for transfers between devices  226 us (71%)
  matrix products  43.3 us (14%)
  between operations  18.2 us (6%)
  starting transfers between devices  13.7 us (4%)
  local copies, waits for them, and re-layouts  8.34 us (3%)
  other arithmetic  8.2 us (3%)
    all_gather x1, waiting for transfers between devices, shards(): lax.all_gather(rms_norm(stream, norm_gain), 'tensor', axis=0, tiled=True)  86.3 us
    all_gather x1, waiting for transfers between devices, shards(): lax.all_gather(qkv_weight, 'dp', axis=0, tiled=True)  78.6 us
    all_gather x1, waiting for transfers between devices, merger(): lax.all_gather(rows_in, 'tensor', axis=0, tiled=True)  29.7 us
    dot_general x1, matrix products, shards(): jnp.dot(normed, lax.all_gather(qkv_weight, 'dp', axis=0, tiled=True), pre...  26.6 us
    reduce_scatter x1, waiting for transfers between devices, merger(): lax.psum_scatter(jnp.dot(hidden, fc2_weight, preferred_element_type=jnp.f...  24.2 us
    dot_general x1, matrix products, merger(): jnp.dot(hidden, fc2_weight, preferred_element_type=jnp.float32)  11 us
    all_to_all x1, waiting for transfers between devices, shards(): lax.all_to_all(outgoing, 'dp', split_axis=0, concat_axis=0, tiled=True)  7.21 us
    all_to_all x1, starting transfers between devices, shards(): lax.all_to_all(send_rows, 'dp', split_axis=0, concat_axis=0, tiled=True)  6.7 us
  transfers between devices with their start and end apart: 6, of which 5 were waited for; matrix products, arithmetic and copies ran while one was open for 4% of the time, Pallas kernels for 0%

commit v1 on v0

v1 whole, which is shorter than its diff:
```python
import jax
import jax.numpy as jnp
from jax import lax
from jax.experimental import pallas as pl
from jax.experimental.pallas import tpu as pltpu
from jax.sharding import PartitionSpec as P


HEAD_DIM = 128
KEEP_SCALE = 1.0 / 0.9
CHUNKS = 4
K_BLOCKS = 8
TILE = 256

UP = [(t, (t + 2) % 8) for t in range(8)]
DOWN = [(t, (t - 2) % 8) for t in range(8)]
ACROSS = [(t, t ^ 1) for t in range(8)]


def layer_norm(inputs, gain, bias):
    widened = inputs.astype(jnp.float32)
    center = jnp.mean(widened, axis=-1, keepdims=True)
    spread = jnp.mean((widened - center) * (widened - center), axis=-1, keepdims=True)
    return (widened - center) * lax.rsqrt(spread + 1e-06) * gain + bias


def rms_norm(inputs, gain):
    widened = inputs.astype(jnp.float32)
    inverse = lax.rsqrt(jnp.mean(widened * widened, axis=-1, keepdims=True) + 1e-06)
    return (widened * inverse * gain).astype(jnp.bfloat16)


def after(value, *others):
    return lax.optimization_barrier((value,) + others)[0]


def shift(value, perm):
    return lax.ppermute(value, "tensor", perm)


def gather_near(rows):
    return shift(rows, UP), shift(rows, DOWN)


def gather_far(rows, near):
    below, above = near
    half = rows.shape[0] // 2
    far_low = shift(below[:half], UP)
    far_high = shift(above[half:], DOWN)
    mine = jnp.concatenate([rows, below, above, far_low, far_high], axis=0)
    return mine, shift(mine, ACROSS)


def outgoing_rows(merged_in, image_counts, image_positions, rows_here, groups, tensor_devs):
    slots = image_positions.shape[0]
    live_slots = jnp.sum(image_counts) // 4
    usable = jnp.arange(slots, dtype=jnp.int32) < live_slots
    group = image_positions // (rows_here * tensor_devs)
    row = image_positions % rows_here
    mark = jnp.where(usable, row + 1, 0).astype(jnp.bfloat16)
    order = jnp.arange(slots, dtype=jnp.int32)
    earlier = (group[:, None] == group[None, :]) & (order[:, None] < order[None, :])
    out_slot = group * (slots // groups) + jnp.sum(earlier.astype(jnp.int32), axis=0)
    chooser = (out_slot[None, :] == order[:, None]).astype(jnp.bfloat16)
    payload = jnp.concatenate([merged_in, jnp.broadcast_to(mark[:, None], (slots, 128))], axis=1)
    return jnp.dot(chooser, payload, preferred_element_type=jnp.float32).astype(jnp.bfloat16)


def project_body(owners, *refs):
    pieces = refs[: 2 * CHUNKS + 2]
    weight, bias, place, hit, queries, keys, values, rows, total, done, sems = refs[2 * CHUNKS + 2 :]
    tile = pl.program_id(0)
    height, depth = pieces[0].shape
    step = depth // K_BLOCKS
    count = len(pieces)
    live = 2 * CHUNKS * height
    per_owner = height // 4

    def copy(piece, block):
        span = pl.ds(pl.multiple_of(block * step, step), step)
        return pltpu.make_async_copy(
            pieces[piece].at[:, span], rows.at[pl.ds(piece * height, height), span], sems.at[block, piece]
        )

    @pl.when(tile == 0)
    def _():
        for block in range(K_BLOCKS):
            for piece in range(count):
                copy(piece, block).start()

    total[...] = jnp.broadcast_to(bias[...], total.shape)

    def accumulate(block, carry):
        @pl.when(tile == 0)
        def _():
            for piece in range(count):
                copy(piece, block).wait()

        span = pl.ds(pl.multiple_of(block * step, step), step)
        total[...] += jnp.dot(rows[:, span], weight[span, :], preferred_element_type=jnp.float32)
        return carry

    lax.fori_loop(0, K_BLOCKS, accumulate, 0)
    tokens = total[live:, :].astype(jnp.bfloat16)

    for chunk in range(CHUNKS):
        lower = chunk * 2 * height
        part = slice(lower, lower + 2 * height)
        moved = jnp.dot(place[part, :], tokens, preferred_element_type=jnp.float32)
        done[part, :] = jnp.where(hit[part, :1] > 0.5, moved, total[part, :]).astype(jnp.bfloat16)

    def write(store):
        for chunk in range(CHUNKS):
            for owner in range(8):
                source = chunk * 2 * height + owner * per_owner
                target = pl.multiple_of(owners[owner] * (CHUNKS * per_owner) + chunk * per_owner, per_owner)
                store(source, target)

    @pl.when(tile < 4)
    def _():
        def store(source, target):
            queries[pl.ds(target, per_owner), :] = done[source : source + per_owner, :]

        write(store)

    @pl.when(tile == 4)
    def _():
        def store(source, target):
            keys[pl.ds(target, per_owner), :] = done[source : source + per_owner, :HEAD_DIM]
            values[pl.ds(target, per_owner), :] = done[source : source + per_owner, HEAD_DIM:]

        write(store)


def project(owners, pieces, weight, bias, place, hit):
    height, depth = pieces[0].shape
    total_rows = len(pieces) * height
    live = 2 * CHUNKS * height
    tiles = weight.shape[1] // TILE
    anywhere = pl.BlockSpec(memory_space=pl.ANY)
    return pl.pallas_call(
        project_body,
        name="project",
        grid_spec=pltpu.PrefetchScalarGridSpec(
            num_scalar_prefetch=1,
            grid=(tiles,),
            in_specs=[anywhere] * len(pieces)
            + [
                pl.BlockSpec((depth, TILE), lambda n, o: (0, n)),
                pl.BlockSpec((1, TILE), lambda n, o: (0, n)),
                pl.BlockSpec(place.shape, lambda n, o: (0, 0)),
                pl.BlockSpec(hit.shape, lambda n, o: (0, 0)),
            ],
            out_specs=[
                pl.BlockSpec((live, TILE), lambda n, o: (0, jnp.minimum(n, 3))),
                pl.BlockSpec((live, HEAD_DIM), lambda n, o: (0, 0)),
                pl.BlockSpec((live, HEAD_DIM), lambda n, o: (0, 0)),
            ],
            scratch_shapes=[
                pltpu.VMEM((total_rows, depth), jnp.bfloat16),
                pltpu.VMEM((total_rows, TILE), jnp.float32),
                pltpu.VMEM((live, TILE), jnp.bfloat16),
                pltpu.SemaphoreType.DMA((K_BLOCKS, len(pieces))),
            ],
        ),
        out_shape=[
            jax.ShapeDtypeStruct((live, 8 * HEAD_DIM), jnp.bfloat16),
            jax.ShapeDtypeStruct((live, HEAD_DIM), jnp.bfloat16),
            jax.ShapeDtypeStruct((live, HEAD_DIM), jnp.bfloat16),
        ],
        compiler_params=pltpu.CompilerParams(
            dimension_semantics=("arbitrary",), vmem_limit_bytes=56 * 1024 * 1024
        ),
        cost_estimate=pl.CostEstimate(
            flops=2 * total_rows * depth * weight.shape[1], bytes_accessed=50_000_000, transcendentals=0
        ),
    )(owners, *pieces, weight, bias[None, :], place, hit)


def shards(
    patches, ln_gain, ln_bias, fc1_weight, fc1_bias, fc2_weight, fc2_bias, image_counts, image_positions,
    text_embeds, keep_mask, norm_gain, qkv_weight, qkv_bias,
):
    groups = lax.axis_size("dp")
    tensor_devs = lax.axis_size("tensor")
    device = lax.axis_index("tensor")
    rows_here, _ = text_embeds.shape
    weight = lax.all_gather(qkv_weight, "dp", axis=0, tiled=True)

    patch_normed = layer_norm(patches, ln_gain, ln_bias).astype(jnp.bfloat16)
    merged_in = patch_normed.reshape(-1, 4 * patches.shape[1])
    slots, features = merged_in.shape
    outgoing = outgoing_rows(merged_in, image_counts, image_positions, rows_here, groups, tensor_devs)
    arrived = lax.all_to_all(
        outgoing.reshape(groups, slots // groups, -1), "dp", split_axis=0, concat_axis=0, tiled=True
    ).reshape(slots, -1)

    text_stream = (text_embeds.astype(jnp.float32) * keep_mask.astype(jnp.float32) * KEEP_SCALE).astype(jnp.bfloat16)
    text_normed = rms_norm(text_stream, norm_gain)
    per_chunk = rows_here // CHUNKS
    chunks = [text_normed[c * per_chunk : (c + 1) * per_chunk] for c in range(CHUNKS)]
    near0 = gather_near(chunks[0])

    mine, other = gather_far(arrived, gather_near(arrived))
    together = jnp.concatenate([mine, other], axis=0)
    far0 = gather_far(chunks[0], (after(near0[0], together), near0[1]))
    chunk1 = after(chunks[1], together)
    near1 = gather_near(chunk1)

    product = jnp.dot(together[:, :features], fc1_weight, preferred_element_type=jnp.float32) + fc1_bias
    hidden = jax.nn.gelu(product, approximate=False).astype(jnp.bfloat16)
    partial = jnp.dot(hidden, fc2_weight, preferred_element_type=jnp.float32).astype(jnp.bfloat16)
    theirs = shift(partial[4 * slots :], ACROSS)
    paired = (partial[: 4 * slots].astype(jnp.float32) + theirs.astype(jnp.float32)).astype(jnp.bfloat16)
    half = slots // 2
    low = shift(paired[3 * slots : 3 * slots + half], UP)
    high = shift(paired[3 * slots + half : 4 * slots], DOWN)
    zeros = jnp.zeros_like(low)
    to_above = paired[2 * slots : 3 * slots].astype(jnp.float32) + jnp.concatenate([low, zeros], axis=0).astype(jnp.float32)
    to_below = paired[slots : 2 * slots].astype(jnp.float32) + jnp.concatenate([zeros, high], axis=0).astype(jnp.float32)
    from_below = shift(to_above.astype(jnp.bfloat16), UP)
    from_above = shift(to_below.astype(jnp.bfloat16), DOWN)
    summed = paired[:slots].astype(jnp.float32) + from_below.astype(jnp.float32) + from_above.astype(jnp.float32)
    tokens = (summed + fc2_bias).astype(jnp.bfloat16)

    far1 = gather_far(chunk1, (after(near1[0], tokens), near1[1]))
    chunk2 = after(chunks[2], tokens)
    near2 = gather_near(chunk2)

    own_row = arrived[:, features].astype(jnp.int32) - 1
    landing = own_row[None, :] == jnp.arange(rows_here, dtype=jnp.int32)[:, None]
    covered = jnp.any(landing, axis=1)
    token_mask = lax.dot_general(
        landing.astype(jnp.bfloat16), keep_mask.astype(jnp.bfloat16), (((0,), (0,)), ((), ())),
        preferred_element_type=jnp.float32,
    )
    token_stream = (tokens.astype(jnp.float32) * token_mask * KEEP_SCALE).astype(jnp.bfloat16)
    token_normed = rms_norm(token_stream, norm_gain)
    token_all = gather_far(token_normed, gather_near(token_normed))
    far2 = gather_far(chunk2, (after(near2[0], token_all[0]), near2[1]))
    chunk3 = after(chunks[3], token_all[0])
    far3 = gather_far(chunk3, gather_near(chunk3))

    landed = jnp.dot(landing.astype(jnp.bfloat16), token_stream, preferred_element_type=jnp.float32)
    stream = jnp.where(covered[:, None], landed.astype(jnp.bfloat16), text_stream)

    slot_row = together[:, features].astype(jnp.int32) - 1
    row = jnp.arange(rows_here * tensor_devs, dtype=jnp.int32)
    row_owner = row // per_chunk % tensor_devs
    row_index = row // (per_chunk * tensor_devs) * per_chunk + row % per_chunk
    slot_owner = jnp.arange(slots * tensor_devs, dtype=jnp.int32) // slots
    place = (row_owner[:, None] == slot_owner[None, :]) & (row_index[:, None] == slot_row[None, :])
    hit = jnp.broadcast_to(jnp.any(place, axis=1)[:, None], (row.shape[0], 128)).astype(jnp.float32)
    owners = jnp.stack([(base + step) % tensor_devs for base in (device, device ^ 1) for step in (0, -2, 2, 4)])
    queries, keys, values = project(
        owners.astype(jnp.int32), [*far0, *far1, *far2, *far3, *token_all], weight, qkv_bias,
        place.astype(jnp.bfloat16), hit,
    )
    return (stream, queries, keys, values)


def solution(mesh):
    placed = (
        P(("dp", "tensor"), None), P(), P(), P(None, "tensor"), P("tensor"), P("tensor", None), P(),
        P(("dp", "tensor"), None), P(("dp", "tensor")), P(("dp", "tensor"), None), P(("dp", "tensor"), None),
        P(), P("dp", "tensor"), P("tensor"),
    )

    return jax.shard_map(
        shards, mesh=mesh, in_specs=placed,
        out_specs=(P(("dp", "tensor"), None), P("dp", "tensor"), P("dp", "tensor"), P("dp", "tensor")),
        check_vma=False,
    )
```

time: 319 us -> 288 us (0.903)
  waiting for transfers between devices: 226 us -> 78.7 us
  starting transfers between devices: 13.7 us -> 72.2 us
  Pallas kernels: 0 us -> 43.8 us
  local copies, waits for them, and re-layouts: 8.34 us -> 42 us
  matrix products: 43.3 us -> 16.1 us
  other arithmetic: 8.2 us -> 17.5 us
    all_gather x3 -> x1, waiting for transfers between devices: 195 us -> 0.02 us  [shards(): weight = lax.all_gather(qkv_weight, 'dp', axis=0, tiled=True)]
    ppermute x0 -> x35, waiting for transfers between devices: none -> 73.7 us  [shift(): return lax.ppermute(value, 'tensor', perm)]
    ppermute x0 -> x35, starting transfers between devices: none -> 63.5 us  [shift(): return lax.ppermute(value, 'tensor', perm)]
    pallas_call x0 -> x1, Pallas kernels: none -> 43.8 us  [project(): pl.pallas_call(project_body, name='project', grid_spec=pltpu.PrefetchScal...]
    dot_general x4, matrix products: 43.3 us -> 16.1 us  [the longest x1 11.3 us: shards(): jnp.dot(hidden, fc2_weight, preferred_element_type=jnp.float32)]
    reduce_scatter x1 -> x0, waiting for transfers between devices: 24.2 us -> none  [merger(): lax.psum_scatter(jnp.dot(hidden, fc2_weight, preferred_element_type=jnp.f...]
    unnamed x16 -> x56, local copies, waits for them, and re-layouts: 1.38 us -> 22.9 us
    slice x0 -> x15, local copies, waits for them, and re-layouts: none -> 7.32 us  [the longest x6 2.01 us: gather_far(): far_low = shift(below[:half], UP)]
  transfers between devices with their start and end apart: 6 -> 37, of which waited for: 5 -> 14; matrix products, arithmetic and copies ran while one was open for 4% -> 25% of each run, Pallas kernels for 0% -> 0%
where the time goes in v1:
time: 288 us; the launch traced here: 287 us
  waiting for transfers between devices  78.7 us (27%)
  starting transfers between devices  72.2 us (25%)
  Pallas kernels  43.8 us (15%)
  local copies, waits for them, and re-layouts  42 us (15%)
  other arithmetic  17.5 us (6%)
  between operations  17 us (6%)
  matrix products  16.1 us (6%)
    ppermute x35, waiting for transfers between devices, shift(): return lax.ppermute(value, 'tensor', perm)  73.7 us
    ppermute x35, starting transfers between devices, shift(): return lax.ppermute(value, 'tensor', perm)  63.5 us
    pallas_call x1, Pallas kernels, project(): pl.pallas_call(project_body, name='project', grid_spec=pltpu.PrefetchScal...  43.8 us
    unnamed x56, local copies, waits for them, and re-layouts  22.9 us
    dot_general x1, matrix products, shards(): jnp.dot(hidden, fc2_weight, preferred_element_type=jnp.float32)  11.3 us
    all_to_all x1, starting transfers between devices, shards(): lax.all_to_all(outgoing.reshape(groups, slots // groups, -1), 'dp', split...  8.68 us
  transfers between devices with their start and end apart: 37, of which 14 were waited for; matrix products, arithmetic and copies ran while one was open for 25% of the time, Pallas kernels for 0%

profile of v1, /device:TPU:1, one launch (start us, length us, event | category | flops | bytes accessed | tf_op | source)
XLA Modules:
  0.0 287.3 jit_solution(11126633857418511326)
XLA Ops:
  7.9 1.5 reduce_sum.57
  12.1 1.1 convert_reduce_fusion
  13.2 1.2 fusion.18
  15.2 2.0 fusion.21
  17.1 1.9 reshape.131
  19.1 1.9 convolution_convert_fusion.2
  21.0 1.8 reshape.132
  22.9 8.7 %all-to-all-start = ((bf16[16,2,5248]{2,1,0:T(2,128)(2,1)}), bf16[16,2,5248]{2,1,0:T(2,128)(2,1)}, u32[]{:S(2)}, u32[]{:S(2)}) async-start(bf16[16,2,5248]{2,1,0:T(2,128)(2,1)} %reshape.132), calls=%async_computation | async-start | bytes 671744 | tf_op jit(solution)/shard_map/all_to_all | solution.py:194
  31.6 4.0 %fusion.1 = (f32[128]{0:T(128)S(1)}, bf16[128,8192]{1,0:T(8,128)(2,1)S(1)}) fusion(s32[128,8192]{1,0:T(8,128)} %param.24, bf16[128,8192]{1,0:T(8,128)(2,1)} %param.23), kind=kLoop, calls=%fused_computation.6 | loop fusion | flops 8388480 | bytes 8389120 | tf_op jit(solution)/shard_map/reduce_sum | solution.py:29
  35.6 1.3 copy-done.2
  36.9 2.0 fusion.3
  38.8 4.3 %all-to-all-done = bf16[16,2,5248]{2,1,0:T(2,128)(2,1)} async-done(((bf16[16,2,5248]{2,1,0:T(2,128)(2,1)}), bf16[16,2,5248]{2,1,0:T(2,128)(2,1)}, u32[]{:S(2)}, u32[]{:S(2)}) %all-to-all-start) | async-done | bytes 335904 | tf_op jit(solution)/shard_map/all_to_all | solution.py:194
  43.1 1.9 reshape.133
  45.0 2.5 collective-permute-start.1
  47.5 1.1 constant_dynamic-update-slice_fusion.4
  48.6 4.3 %collective-permute-done.1 = bf16[32,5248]{1,0:T(8,128)(2,1)S(1)} collective-permute-done((bf16[32,5248]{1,0:T(8,128)(2,1)}, bf16[32,5248]{1,0:T(8,128)(2,1)S(1)}, u32[]{:S(2)}, u32[]{:S(2)}) %collective-permute-start.1) | collective-permute-done | bytes 335904 | tf_op jit(solution)/shard_map/ppermute | solution.py:38
  52.9 3.4 %collective-permute-start.3 = (bf16[16,5248]{1,0:T(8,128)(2,1)S(1)}, bf16[16,5248]{1,0:T(8,128)(2,1)S(1)}, u32[]{:S(2)}, u32[]{:S(2)}) collective-permute-start(bf16[16,5248]{1,0:T(8,128)(2,1)S(1)} %slice.106), channel_id=1, source_target_pairs={{0,6},{1,7},{2,0},{3,1},{4,2},{5,3},{6,4},{7,5},{8,14},{9,15},{10,... | collective-permute-start | bytes 503816 | tf_op jit(solution)/shard_map/ppermute | solution.py:38
  56.6 5.3 %collective-permute-done.2 = bf16[16,5248]{1,0:T(8,128)(2,1)S(1)} collective-permute-done((bf16[16,5248]{1,0:T(8,128)(2,1)S(1)}, bf16[16,5248]{1,0:T(8,128)(2,1)S(1)}, u32[]{:S(2)}, u32[]{:S(2)}) %collective-permute-start.2) | collective-permute-done | bytes 167968 | tf_op jit(solution)/shard_map/ppermute | solution.py:38
  61.9 4.5 %collective-permute-start.4 = (bf16[128,5248]{1,0:T(8,128)(2,1)S(1)}, bf16[128,5248]{1,0:T(8,128)(2,1)S(1)}, u32[]{:S(2)}, u32[]{:S(2)}) collective-permute-start(bf16[128,5248]{1,0:T(8,128)(2,1)S(1)} %get-tuple-element.41), channel_id=1, source_target_pairs={{0,1},{1,0},{2,3},{3,2},{4,5},{5,4},{6,7},{7,6},{8,9},{9,8},{10,11... | collective-permute-start | bytes 4030472 | tf_op jit(solution)/shard_map/ppermute | solution.py:38
  66.4 1.6 fusion.123
  67.9 1.5 collective-permute-start.10
  70.2 11.5 %collective-permute-done.11 = bf16[32,8192]{1,0:T(8,128)(2,1)S(1)} collective-permute-done((bf16[32,8192]{1,0:T(8,128)(2,1)}, bf16[32,8192]{1,0:T(8,128)(2,1)S(1)}, u32[]{:S(2)}, u32[]{:S(2)}) %collective-permute-start.11) | collective-permute-done | bytes 524320 | tf_op jit(solution)/shard_map/ppermute | solution.py:38
  82.5 1.4 collective-permute-start.13
  84.1 1.5 copy-done.13
  85.7 1.4 collective-permute-start.15
  87.1 11.3 %convolution_convert_fusion = bf16[256,8192]{1,0:T(8,128)(2,1)} fusion(bf16[320,8192]{1,0:T(8,128)(2,1)} %param.19, bf16[5120,320]{0,1:T(8,128)(2,1)S(1)} %copy-done, bf16[256,5248]{1,0:T(8,128)(2,1)} %copy-done.13, f32[320]{0:T(512)S(1)} %copy-done.16), kind=kOutput, calls=%fused_computation | convolution fusion | flops 2188541952 | bytes 15336704 | tf_op jit(solution)/shard_map/dot_general | solution.py:212
  98.4 1.9 slice.109
  100.3 1.5 collective-permute-start.5
  101.8 1.9 constant_dynamic-update-slice_fusion.20
  103.8 1.0 slice.90
  105.1 1.9 constant_dynamic-update-slice_fusion.14
  106.9 0.9 constant_dynamic-update-slice_fusion.13
  108.5 5.4 %collective-permute-done.12 = bf16[16,8192]{1,0:T(8,128)(2,1)S(1)} collective-permute-done((bf16[16,8192]{1,0:T(8,128)(2,1)S(1)}, bf16[16,8192]{1,0:T(8,128)(2,1)S(1)}, u32[]{:S(2)}, u32[]{:S(2)}) %collective-permute-start.12) | collective-permute-done | bytes 262176 | tf_op jit(solution)/shard_map/ppermute | solution.py:38
  114.6 4.9 %collective-permute-done.6 = bf16[16,8192]{1,0:T(8,128)(2,1)S(1)} collective-permute-done((bf16[16,8192]{1,0:T(8,128)(2,1)S(1)}, bf16[16,8192]{1,0:T(8,128)(2,1)S(1)}, u32[]{:S(2)}, u32[]{:S(2)}) %collective-permute-start.6) | collective-permute-done | bytes 262176 | tf_op jit(solution)/shard_map/ppermute | solution.py:38
  119.5 1.0 collective-permute-done.8
  120.7 2.7 collective-permute-start.9
  124.1 2.7 collective-permute-start.14
  126.8 1.0 slice.118
  127.8 5.5 %collective-permute-done.7 = bf16[32,8192]{1,0:T(8,128)(2,1)S(1)} collective-permute-done((bf16[32,8192]{1,0:T(8,128)(2,1)S(1)}, bf16[32,8192]{1,0:T(8,128)(2,1)S(1)}, u32[]{:S(2)}, u32[]{:S(2)}) %collective-permute-start.7) | collective-permute-done | bytes 524320 | tf_op jit(solution)/shard_map/ppermute | solution.py:38
  133.6 2.5 collective-permute-start.25
  136.1 1.0 slice.93
  137.8 0.9 constant_dynamic-update-slice_fusion.30
  138.7 1.9 constant_dynamic-update-slice_fusion.19
  140.6 1.0 constant_dynamic-update-slice_fusion.25
  141.6 1.9 constant_dynamic-update-slice_fusion.18
  143.5 6.6 %collective-permute-done.17 = bf16[16,8192]{1,0:T(8,128)(2,1)S(1)} collective-permute-done((bf16[16,8192]{1,0:T(8,128)(2,1)S(1)}, bf16[16,8192]{1,0:T(8,128)(2,1)S(1)}, u32[]{:S(2)}, u32[]{:S(2)}) %collective-permute-start.17) | collective-permute-done | bytes 262176 | tf_op jit(solution)/shard_map/ppermute | solution.py:38
  150.8 1.5 collective-permute-start.21
  153.0 9.9 %collective-permute-start.19 = (bf16[128,8192]{1,0:T(8,128)(2,1)}, bf16[128,8192]{1,0:T(8,128)(2,1)}, u32[]{:S(2)}, u32[]{:S(2)}) collective-permute-start(bf16[128,8192]{1,0:T(8,128)(2,1)} %constant_dynamic-update-slice_fusion.16.refs_2_), channel_id=1, source_target_pairs={{0,1},{1,0},{2,3},{3,2},{4,5},{5,4},{6,7},{7,6},{8,9},{9,8},{10,11... | collective-permute-start | bytes 6291464 | tf_op jit(solution)/shard_map/ppermute | solution.py:38
  162.9 1.0 collective-permute-start.27
  163.9 0.9 constant_dynamic-update-slice_fusion.24
  166.2 6.4 %collective-permute-done.23 = bf16[16,8192]{1,0:T(8,128)(2,1)S(1)} collective-permute-done((bf16[16,8192]{1,0:T(8,128)(2,1)S(1)}, bf16[16,8192]{1,0:T(8,128)(2,1)S(1)}, u32[]{:S(2)}, u32[]{:S(2)}) %collective-permute-start.23) | collective-permute-done | bytes 262176 | tf_op jit(solution)/shard_map/ppermute | solution.py:38
  173.3 7.1 %collective-permute-done.24 = bf16[16,8192]{1,0:T(8,128)(2,1)S(1)} collective-permute-done((bf16[16,8192]{1,0:T(8,128)(2,1)S(1)}, bf16[16,8192]{1,0:T(8,128)(2,1)S(1)}, u32[]{:S(2)}, u32[]{:S(2)}) %collective-permute-start.24) | collective-permute-done | bytes 262176 | tf_op jit(solution)/shard_map/ppermute | solution.py:38
  181.5 2.4 collective-permute-start.30
  186.4 1.2 collective-permute-done.26
  188.3 12.4 %collective-permute-start.34 = (bf16[128,8192]{1,0:T(8,128)(2,1)}, bf16[128,8192]{1,0:T(8,128)(2,1)}, u32[]{:S(2)}, u32[]{:S(2)}) collective-permute-start(bf16[128,8192]{1,0:T(8,128)(2,1)} %constant_dynamic-update-slice_fusion.21.refs_8_), channel_id=1, source_target_pairs={{0,1},{1,0},{2,3},{3,2},{4,5},{5,4},{6,7},{7,6},{8,9},{9,8},{10,11... | collective-permute-start | bytes 6291464 | tf_op jit(solution)/shard_map/ppermute | solution.py:38
  201.5 8.9 %collective-permute-start.28 = (bf16[128,8192]{1,0:T(8,128)(2,1)}, bf16[128,8192]{1,0:T(8,128)(2,1)}, u32[]{:S(2)}, u32[]{:S(2)}) collective-permute-start(bf16[128,8192]{1,0:T(8,128)(2,1)} %constant_dynamic-update-slice_fusion.26.refs_4_), channel_id=1, source_target_pairs={{0,1},{1,0},{2,3},{3,2},{4,5},{5,4},{6,7},{7,6},{8,9},{9,8},{10,11... | collective-permute-start | bytes 6291464 | tf_op jit(solution)/shard_map/ppermute | solution.py:38
  212.2 8.2 %collective-permute-done.31 = bf16[16,8192]{1,0:T(8,128)(2,1)S(1)} collective-permute-done((bf16[16,8192]{1,0:T(8,128)(2,1)S(1)}, bf16[16,8192]{1,0:T(8,128)(2,1)S(1)}, u32[]{:S(2)}, u32[]{:S(2)}) %collective-permute-start.31) | collective-permute-done | bytes 262176 | tf_op jit(solution)/shard_map/ppermute | solution.py:38
  221.2 6.3 %collective-permute-done.32 = bf16[16,8192]{1,0:T(8,128)(2,1)S(1)} collective-permute-done((bf16[16,8192]{1,0:T(8,128)(2,1)S(1)}, bf16[16,8192]{1,0:T(8,128)(2,1)S(1)}, u32[]{:S(2)}, u32[]{:S(2)}) %collective-permute-start.32) | collective-permute-done | bytes 262176 | tf_op jit(solution)/shard_map/ppermute | solution.py:38
  228.1 1.7 collective-permute-start.33
  231.2 1.0 add_reduce_fusion
  232.2 1.2 fusion.14
  233.4 2.1 fusion
  235.6 1.0 broadcast_in_dim.16.refs_13_
  236.6 43.8 %project.1 = (bf16[1024,1024]{1,0:T(8,128)(2,1)}, bf16[1024,128]{1,0:T(8,128)(2,1)}, bf16[1024,128]{1,0:T(8,128)(2,1)}) custom-call(s32[8]{0:T(128)} %stack.35.owners, bf16[128,8192]{1,0:T(8,128)(2,1)} %constant_dynamic-update-slice_fusion.11.refs_0_, bf16[128,8192]{1,0:T(8,128)(2,1)} %collective-permute-done.14.refs_1_, ...), custom_call_target="tpu_custom_call" | custom-call | flops 26843545600 | bytes 50000000 | tf_op jit(solution)/shard_map/project/pallas_call | solution.py:141
  (125 shorter events, 20.8 us)
Async XLA Ops:
  7.2 79.9 %copy-start = (bf16[5120,320]{0,1:T(8,128)(2,1)S(1)}, bf16[5120,320]{0,1:T(8,128)(2,1)}, u32[]{:S(2)}) copy-start(bf16[5120,320]{0,1:T(8,128)(2,1)} %param.17) | copy-start | bytes 9830404
  7.2 228.4 %all-gather.2.cloned.1.call-start = ((), (), s32[]{:S(2)}) async-start(), calls=%async_computation.1 | async-start | bytes 22282240 | tf_op jit(solution)/shard_map/all_gather | solution.py:188
  22.9 20.3 %all-to-all-start = ((bf16[16,2,5248]{2,1,0:T(2,128)(2,1)}), bf16[16,2,5248]{2,1,0:T(2,128)(2,1)}, u32[]{:S(2)}, u32[]{:S(2)}) async-start(bf16[16,2,5248]{2,1,0:T(2,128)(2,1)} %reshape.132), calls=%async_computation | async-start | bytes 671744 | tf_op jit(solution)/shard_map/all_to_all | solution.py:194
  31.6 5.3 %copy-start.11 = (f32[8192]{0:T(1024)S(1)}, f32[8192]{0:T(1024)}, u32[]{:S(2)}) copy-start(f32[8192]{0:T(1024)} %param.25) | copy-start | bytes 98308
  35.5 1.3 copy-start.2
  45.0 7.9 %collective-permute-start.1 = (bf16[32,5248]{1,0:T(8,128)(2,1)}, bf16[32,5248]{1,0:T(8,128)(2,1)S(1)}, u32[]{:S(2)}, u32[]{:S(2)}) collective-permute-start(bf16[32,5248]{1,0:T(8,128)(2,1)} %reshape.133), channel_id=1, source_target_pairs={{0,6},{1,7},{2,0},{3,1},{4,2},{5,3},{6,4},{7,5},{8,14},{9,15},{10,... | collective-permute-start | bytes 1007624 | tf_op jit(solution)/shard_map/ppermute | solution.py:38
  47.5 8.9 %collective-permute-start = (bf16[32,5248]{1,0:T(8,128)(2,1)}, bf16[32,5248]{1,0:T(8,128)(2,1)S(1)}, u32[]{:S(2)}, u32[]{:S(2)}) collective-permute-start(bf16[32,5248]{1,0:T(8,128)(2,1)} %reshape.133), channel_id=1, source_target_pairs={{0,2},{1,3},{2,4},{3,5},{4,6},{5,7},{6,0},{7,1},{8,10},{9,11},{10,... | collective-permute-start | bytes 1007624 | tf_op jit(solution)/shard_map/ppermute | solution.py:38
  48.6 17.8 %copy-start.5 = (bf16[128,8192]{1,0:T(8,128)(2,1)S(1)}, bf16[128,8192]{1,0:T(8,128)(2,1)}, u32[]{:S(2)}) copy-start(bf16[128,8192]{1,0:T(8,128)(2,1)} %fusion.3) | copy-start | bytes 6291460
  52.9 9.0 %collective-permute-start.3 = (bf16[16,5248]{1,0:T(8,128)(2,1)S(1)}, bf16[16,5248]{1,0:T(8,128)(2,1)S(1)}, u32[]{:S(2)}, u32[]{:S(2)}) collective-permute-start(bf16[16,5248]{1,0:T(8,128)(2,1)S(1)} %slice.106), channel_id=1, source_target_pairs={{0,6},{1,7},{2,0},{3,1},{4,2},{5,3},{6,4},{7,5},{8,14},{9,15},{10,... | collective-permute-start | bytes 503816 | tf_op jit(solution)/shard_map/ppermute | solution.py:38
  56.4 5.5 %collective-permute-start.2 = (bf16[16,5248]{1,0:T(8,128)(2,1)S(1)}, bf16[16,5248]{1,0:T(8,128)(2,1)S(1)}, u32[]{:S(2)}, u32[]{:S(2)}) collective-permute-start(bf16[16,5248]{1,0:T(8,128)(2,1)S(1)} %slice.105), channel_id=1, source_target_pairs={{0,2},{1,3},{2,4},{3,5},{4,6},{5,7},{6,0},{7,1},{8,10},{9,11},{10,... | collective-permute-start | bytes 503816 | tf_op jit(solution)/shard_map/ppermute | solution.py:38
  61.9 22.0 %collective-permute-start.4 = (bf16[128,5248]{1,0:T(8,128)(2,1)S(1)}, bf16[128,5248]{1,0:T(8,128)(2,1)S(1)}, u32[]{:S(2)}, u32[]{:S(2)}) collective-permute-start(bf16[128,5248]{1,0:T(8,128)(2,1)S(1)} %get-tuple-element.41), channel_id=1, source_target_pairs={{0,1},{1,0},{2,3},{3,2},{4,5},{5,4},{6,7},{7,6},{8,9},{9,8},{10,11... | collective-permute-start | bytes 4030472 | tf_op jit(solution)/shard_map/ppermute | solution.py:38
  67.9 19.1 %copy-start.16 = (f32[320]{0:T(512)S(1)}, f32[320]{0:T(512)}, u32[]{:S(2)}) copy-start(f32[320]{0:T(512)} %param.18) | copy-start | bytes 3844
  67.9 13.8 %collective-permute-start.11 = (bf16[32,8192]{1,0:T(8,128)(2,1)}, bf16[32,8192]{1,0:T(8,128)(2,1)S(1)}, u32[]{:S(2)}, u32[]{:S(2)}) collective-permute-start(bf16[32,8192]{1,0:T(8,128)(2,1)} %get-tuple-element.30), channel_id=1, source_target_pairs={{0,6},{1,7},{2,0},{3,1},{4,2},{5,3},{6,4},{7,5},{8,14},{9,15},{10,... | collective-permute-start | bytes 1572872 | tf_op jit(solution)/shard_map/ppermute | solution.py:38
  67.9 35.8 %collective-permute-start.10 = (bf16[32,8192]{1,0:T(8,128)(2,1)}, bf16[32,8192]{1,0:T(8,128)(2,1)}, u32[]{:S(2)}, u32[]{:S(2)}) collective-permute-start(bf16[32,8192]{1,0:T(8,128)(2,1)} %get-tuple-element.30), channel_id=1, source_target_pairs={{0,2},{1,3},{2,4},{3,5},{4,6},{5,7},{6,0},{7,1},{8,10},{9,11},{10,... | collective-permute-start | bytes 1572872 | tf_op jit(solution)/shard_map/ppermute | solution.py:38
  81.7 2.2 copy-start.9
  82.5 40.9 %collective-permute-start.13 = (bf16[16,8192]{1,0:T(8,128)(2,1)}, bf16[16,8192]{1,0:T(8,128)(2,1)S(1)}, u32[]{:S(2)}, u32[]{:S(2)}) collective-permute-start(bf16[16,8192]{1,0:T(8,128)(2,1)} %slice.116), channel_id=1, source_target_pairs={{0,6},{1,7},{2,0},{3,1},{4,2},{5,3},{6,4},{7,5},{8,14},{9,15},{10,... | collective-permute-start | bytes 786440 | tf_op jit(solution)/shard_map/ppermute | solution.py:38
  84.1 1.5 copy-start.13
  85.6 41.2 %collective-permute-start.16 = (bf16[32,8192]{1,0:T(8,128)(2,1)}, bf16[32,8192]{1,0:T(8,128)(2,1)}, u32[]{:S(2)}, u32[]{:S(2)}) collective-permute-start(bf16[32,8192]{1,0:T(8,128)(2,1)} %get-tuple-element.14), channel_id=1, source_target_pairs={{0,6},{1,7},{2,0},{3,1},{4,2},{5,3},{6,4},{7,5},{8,14},{9,15},{10,... | collective-permute-start | bytes 1572872 | tf_op jit(solution)/shard_map/ppermute | solution.py:38
  85.7 50.4 %collective-permute-start.15 = (bf16[32,8192]{1,0:T(8,128)(2,1)}, bf16[32,8192]{1,0:T(8,128)(2,1)}, u32[]{:S(2)}, u32[]{:S(2)}) collective-permute-start(bf16[32,8192]{1,0:T(8,128)(2,1)} %get-tuple-element.14), channel_id=1, source_target_pairs={{0,2},{1,3},{2,4},{3,5},{4,6},{5,7},{6,0},{7,1},{8,10},{9,11},{10,... | collective-permute-start | bytes 1572872 | tf_op jit(solution)/shard_map/ppermute | solution.py:38
  98.4 9.4 %copy-start.6 = (bf16[256,8192]{1,0:T(8,128)(2,1)S(1)}, bf16[256,8192]{1,0:T(8,128)(2,1)}, u32[]{:S(2)}) copy-start(bf16[256,8192]{1,0:T(8,128)(2,1)} %convolution_convert_fusion) | copy-start | bytes 12582916
  100.3 6.6 %copy-start.10 = (bf16[32,8192]{1,0:T(8,128)(2,1)S(1)}, bf16[32,8192]{1,0:T(8,128)(2,1)}, u32[]{:S(2)}) copy-start(bf16[32,8192]{1,0:T(8,128)(2,1)} %copy-done.9) | copy-start | bytes 1572868
  100.3 7.5 %collective-permute-start.5 = (bf16[128,8192]{1,0:T(8,128)(2,1)S(1)}, bf16[128,8192]{1,0:T(8,128)(2,1)S(1)}, u32[]{:S(2)}, u32[]{:S(2)}) collective-permute-start(bf16[128,8192]{1,0:T(8,128)(2,1)S(1)} %slice.109), channel_id=1, source_target_pairs={{0,1},{1,0},{2,3},{3,2},{4,5},{5,4},{6,7},{7,6},{8,9},{9,8},{10,11... | collective-permute-start | bytes 6291464 | tf_op jit(solution)/shard_map/ppermute | solution.py:38
  104.7 9.2 %collective-permute-start.12 = (bf16[16,8192]{1,0:T(8,128)(2,1)S(1)}, bf16[16,8192]{1,0:T(8,128)(2,1)S(1)}, u32[]{:S(2)}, u32[]{:S(2)}) collective-permute-start(bf16[16,8192]{1,0:T(8,128)(2,1)S(1)} %slice.90), channel_id=1, source_target_pairs={{0,2},{1,3},{2,4},{3,5},{4,6},{5,7},{6,0},{7,1},{8,10},{9,11},{10,... | collective-permute-start | bytes 786440 | tf_op jit(solution)/shard_map/ppermute | solution.py:38
  108.4 11.1 %collective-permute-start.6 = (bf16[16,8192]{1,0:T(8,128)(2,1)S(1)}, bf16[16,8192]{1,0:T(8,128)(2,1)S(1)}, u32[]{:S(2)}, u32[]{:S(2)}) collective-permute-start(bf16[16,8192]{1,0:T(8,128)(2,1)S(1)} %get-tuple-element.33), channel_id=1, source_target_pairs={{0,2},{1,3},{2,4},{3,5},{4,6},{5,7},{6,0},{7,1},{8,10},{9,11},{10,... | collective-permute-start | bytes 786440 | tf_op jit(solution)/shard_map/ppermute | solution.py:38
  113.9 19.4 %copy-start.14 = (f32[8192]{0:T(1024)S(1)}, f32[8192]{0:T(1024)}, u32[]{:S(2)}) copy-start(f32[8192]{0:T(1024)} %param.20) | copy-start | bytes 98308
  113.9 6.6 %collective-permute-start.8 = (bf16[16,8192]{1,0:T(8,128)(2,1)S(1)}, bf16[16,8192]{1,0:T(8,128)(2,1)S(1)}, u32[]{:S(2)}, u32[]{:S(2)}) collective-permute-start(bf16[16,8192]{1,0:T(8,128)(2,1)S(1)} %get-tuple-element.34), channel_id=1, source_target_pairs={{0,6},{1,7},{2,0},{3,1},{4,2},{5,3},{6,4},{7,5},{8,14},{9,15},{10,... | collective-permute-start | bytes 786440 | tf_op jit(solution)/shard_map/ppermute | solution.py:38
  120.5 16.6 %copy-start.4 = (s32[128,8192]{1,0:T(8,128)S(1)}, s32[128,8192]{1,0:T(8,128)}, u32[]{:S(2)}) copy-start(s32[128,8192]{1,0:T(8,128)} %param.24) | copy-start | bytes 12582916
  120.6 13.0 %copy-start.8 = (bf16[32,8192]{1,0:T(8,128)(2,1)S(1)}, bf16[32,8192]{1,0:T(8,128)(2,1)}, u32[]{:S(2)}) copy-start(bf16[32,8192]{1,0:T(8,128)(2,1)} %get-tuple-element.16) | copy-start | bytes 1572868
  120.6 12.7 %collective-permute-start.7 = (bf16[32,8192]{1,0:T(8,128)(2,1)S(1)}, bf16[32,8192]{1,0:T(8,128)(2,1)S(1)}, u32[]{:S(2)}, u32[]{:S(2)}) collective-permute-start(bf16[32,8192]{1,0:T(8,128)(2,1)S(1)} %get-tuple-element.31), channel_id=1, source_target_pairs={{0,2},{1,3},{2,4},{3,5},{4,6},{5,7},{6,0},{7,1},{8,10},{9,11},{10,... | collective-permute-start | bytes 1572872 | tf_op jit(solution)/shard_map/ppermute | solution.py:38
  120.7 12.6 %collective-permute-start.9 = (bf16[32,8192]{1,0:T(8,128)(2,1)S(1)}, bf16[32,8192]{1,0:T(8,128)(2,1)S(1)}, u32[]{:S(2)}, u32[]{:S(2)}) collective-permute-start(bf16[32,8192]{1,0:T(8,128)(2,1)S(1)} %get-tuple-element.32), channel_id=1, source_target_pairs={{0,6},{1,7},{2,0},{3,1},{4,2},{5,3},{6,4},{7,5},{8,14},{9,15},{10,... | collective-permute-start | bytes 1572872 | tf_op jit(solution)/shard_map/ppermute | solution.py:38
  124.1 111.5 %collective-permute-start.14 = (bf16[128,8192]{1,0:T(8,128)(2,1)}, bf16[128,8192]{1,0:T(8,128)(2,1)}, u32[]{:S(2)}, u32[]{:S(2)}) collective-permute-start(bf16[128,8192]{1,0:T(8,128)(2,1)} %constant_dynamic-update-slice_fusion.11.refs_0_), channel_id=1, source_target_pairs={{0,1},{1,0},{2,3},{3,2},{4,5},{5,4},{6,7},{7,6},{8,9},{9,8},{10,11... | collective-permute-start | bytes 6291464 | tf_op jit(solution)/shard_map/ppermute | solution.py:38
  127.8 23.0 %collective-permute-start.18 = (bf16[16,8192]{1,0:T(8,128)(2,1)S(1)}, bf16[16,8192]{1,0:T(8,128)(2,1)S(1)}, u32[]{:S(2)}, u32[]{:S(2)}) collective-permute-start(bf16[16,8192]{1,0:T(8,128)(2,1)S(1)} %slice.118), channel_id=1, source_target_pairs={{0,6},{1,7},{2,0},{3,1},{4,2},{5,3},{6,4},{7,5},{8,14},{9,15},{10,... | collective-permute-start | bytes 786440 | tf_op jit(solution)/shard_map/ppermute | solution.py:38
  133.6 19.4 %collective-permute-start.25 = (bf16[32,8192]{1,0:T(8,128)(2,1)S(1)}, bf16[32,8192]{1,0:T(8,128)(2,1)S(1)}, u32[]{:S(2)}, u32[]{:S(2)}) collective-permute-start(bf16[32,8192]{1,0:T(8,128)(2,1)S(1)} %copy-done.8), channel_id=1, source_target_pairs={{0,6},{1,7},{2,0},{3,1},{4,2},{5,3},{6,4},{7,5},{8,14},{9,15},{10,... | collective-permute-start | bytes 1572872 | tf_op jit(solution)/shard_map/ppermute | solution.py:38
  136.1 45.0 %collective-permute-start.20 = (bf16[32,8192]{1,0:T(8,128)(2,1)S(1)}, bf16[32,8192]{1,0:T(8,128)(2,1)S(1)}, u32[]{:S(2)}, u32[]{:S(2)}) collective-permute-start(bf16[32,8192]{1,0:T(8,128)(2,1)S(1)} %copy-done.8), channel_id=1, source_target_pairs={{0,2},{1,3},{2,4},{3,5},{4,6},{5,7},{6,0},{7,1},{8,10},{9,11},{10,... | collective-permute-start | bytes 1572872 | tf_op jit(solution)/shard_map/ppermute | solution.py:38
  137.0 13.0 %collective-permute-start.17 = (bf16[16,8192]{1,0:T(8,128)(2,1)S(1)}, bf16[16,8192]{1,0:T(8,128)(2,1)S(1)}, u32[]{:S(2)}, u32[]{:S(2)}) collective-permute-start(bf16[16,8192]{1,0:T(8,128)(2,1)S(1)} %slice.93), channel_id=1, source_target_pairs={{0,2},{1,3},{2,4},{3,5},{4,6},{5,7},{6,0},{7,1},{8,10},{9,11},{10,... | collective-permute-start | bytes 786440 | tf_op jit(solution)/shard_map/ppermute | solution.py:38
  137.8 2.7 copy-start.12
  150.0 14.8 %collective-permute-start.22 = (bf16[32,8192]{1,0:T(8,128)(2,1)S(1)}, bf16[32,8192]{1,0:T(8,128)(2,1)S(1)}, u32[]{:S(2)}, u32[]{:S(2)}) collective-permute-start(bf16[32,8192]{1,0:T(8,128)(2,1)S(1)} %get-tuple-element.23), channel_id=1, source_target_pairs={{0,6},{1,7},{2,0},{3,1},{4,2},{5,3},{6,4},{7,5},{8,14},{9,15},{10,... | collective-permute-start | bytes 1572872 | tf_op jit(solution)/shard_map/ppermute | solution.py:38
  150.8 12.1 %collective-permute-start.21 = (bf16[32,8192]{1,0:T(8,128)(2,1)S(1)}, bf16[32,8192]{1,0:T(8,128)(2,1)S(1)}, u32[]{:S(2)}, u32[]{:S(2)}) collective-permute-start(bf16[32,8192]{1,0:T(8,128)(2,1)S(1)} %get-tuple-element.23), channel_id=1, source_target_pairs={{0,2},{1,3},{2,4},{3,5},{4,6},{5,7},{6,0},{7,1},{8,10},{9,11},{10,... | collective-permute-start | bytes 1572872 | tf_op jit(solution)/shard_map/ppermute | solution.py:38
  153.0 82.6 %collective-permute-start.19 = (bf16[128,8192]{1,0:T(8,128)(2,1)}, bf16[128,8192]{1,0:T(8,128)(2,1)}, u32[]{:S(2)}, u32[]{:S(2)}) collective-permute-start(bf16[128,8192]{1,0:T(8,128)(2,1)} %constant_dynamic-update-slice_fusion.16.refs_2_), channel_id=1, source_target_pairs={{0,1},{1,0},{2,3},{3,2},{4,5},{5,4},{6,7},{7,6},{8,9},{9,8},{10,11... | collective-permute-start | bytes 6291464 | tf_op jit(solution)/shard_map/ppermute | solution.py:38
  162.9 25.5 %collective-permute-start.27 = (bf16[16,8192]{1,0:T(8,128)(2,1)S(1)}, bf16[16,8192]{1,0:T(8,128)(2,1)S(1)}, u32[]{:S(2)}, u32[]{:S(2)}) collective-permute-start(bf16[16,8192]{1,0:T(8,128)(2,1)S(1)} %slice.122), channel_id=1, source_target_pairs={{0,6},{1,7},{2,0},{3,1},{4,2},{5,3},{6,4},{7,5},{8,14},{9,15},{10,... | collective-permute-start | bytes 786440 | tf_op jit(solution)/shard_map/ppermute | solution.py:38
  163.9 17.6 %copy-start.7 = (bf16[32,8192]{1,0:T(8,128)(2,1)S(1)}, bf16[32,8192]{1,0:T(8,128)(2,1)}, u32[]{:S(2)}) copy-start(bf16[32,8192]{1,0:T(8,128)(2,1)} %get-tuple-element.18) | copy-start | bytes 1572868
  164.8 7.8 %collective-permute-start.23 = (bf16[16,8192]{1,0:T(8,128)(2,1)S(1)}, bf16[16,8192]{1,0:T(8,128)(2,1)S(1)}, u32[]{:S(2)}, u32[]{:S(2)}) collective-permute-start(bf16[16,8192]{1,0:T(8,128)(2,1)S(1)} %slice.120), channel_id=1, source_target_pairs={{0,2},{1,3},{2,4},{3,5},{4,6},{5,7},{6,0},{7,1},{8,10},{9,11},{10,... | collective-permute-start | bytes 786440 | tf_op jit(solution)/shard_map/ppermute | solution.py:38
  172.6 7.8 %collective-permute-start.24 = (bf16[16,8192]{1,0:T(8,128)(2,1)S(1)}, bf16[16,8192]{1,0:T(8,128)(2,1)S(1)}, u32[]{:S(2)}, u32[]{:S(2)}) collective-permute-start(bf16[16,8192]{1,0:T(8,128)(2,1)S(1)} %slice.121), channel_id=1, source_target_pairs={{0,6},{1,7},{2,0},{3,1},{4,2},{5,3},{6,4},{7,5},{8,14},{9,15},{10,... | collective-permute-start | bytes 786440 | tf_op jit(solution)/shard_map/ppermute | solution.py:38
  181.1 6.5 %collective-permute-start.26 = (bf16[16,8192]{1,0:T(8,128)(2,1)S(1)}, bf16[16,8192]{1,0:T(8,128)(2,1)S(1)}, u32[]{:S(2)}, u32[]{:S(2)}) collective-permute-start(bf16[16,8192]{1,0:T(8,128)(2,1)S(1)} %slice.98), channel_id=1, source_target_pairs={{0,2},{1,3},{2,4},{3,5},{4,6},{5,7},{6,0},{7,1},{8,10},{9,11},{10,... | collective-permute-start | bytes 786440 | tf_op jit(solution)/shard_map/ppermute | solution.py:38
  181.5 29.8 %collective-permute-start.30 = (bf16[32,8192]{1,0:T(8,128)(2,1)S(1)}, bf16[32,8192]{1,0:T(8,128)(2,1)S(1)}, u32[]{:S(2)}, u32[]{:S(2)}) collective-permute-start(bf16[32,8192]{1,0:T(8,128)(2,1)S(1)} %copy-done.7), channel_id=1, source_target_pairs={{0,6},{1,7},{2,0},{3,1},{4,2},{5,3},{6,4},{7,5},{8,14},{9,15},{10,... | collective-permute-start | bytes 1572872 | tf_op jit(solution)/shard_map/ppermute | solution.py:38
  187.6 13.9 %collective-permute-start.29 = (bf16[32,8192]{1,0:T(8,128)(2,1)S(1)}, bf16[32,8192]{1,0:T(8,128)(2,1)S(1)}, u32[]{:S(2)}, u32[]{:S(2)}) collective-permute-start(bf16[32,8192]{1,0:T(8,128)(2,1)S(1)} %copy-done.7), channel_id=1, source_target_pairs={{0,2},{1,3},{2,4},{3,5},{4,6},{5,7},{6,0},{7,1},{8,10},{9,11},{10,... | collective-permute-start | bytes 1572872 | tf_op jit(solution)/shard_map/ppermute | solution.py:38
  188.3 47.2 %collective-permute-start.34 = (bf16[128,8192]{1,0:T(8,128)(2,1)}, bf16[128,8192]{1,0:T(8,128)(2,1)}, u32[]{:S(2)}, u32[]{:S(2)}) collective-permute-start(bf16[128,8192]{1,0:T(8,128)(2,1)} %constant_dynamic-update-slice_fusion.21.refs_8_), channel_id=1, source_target_pairs={{0,1},{1,0},{2,3},{3,2},{4,5},{5,4},{6,7},{7,6},{8,9},{9,8},{10,11... | collective-permute-start | bytes 6291464 | tf_op jit(solution)/shard_map/ppermute | solution.py:38
  201.5 28.3 %copy-start.15 = (f32[1280]{0:T(1024)S(1)}, f32[1280]{0:T(1024)}, u32[]{:S(2)}) copy-start(f32[1280]{0:T(1024)} %param.27) | copy-start | bytes 15364
  201.5 34.0 %collective-permute-start.28 = (bf16[128,8192]{1,0:T(8,128)(2,1)}, bf16[128,8192]{1,0:T(8,128)(2,1)}, u32[]{:S(2)}, u32[]{:S(2)}) collective-permute-start(bf16[128,8192]{1,0:T(8,128)(2,1)} %constant_dynamic-update-slice_fusion.26.refs_4_), channel_id=1, source_target_pairs={{0,1},{1,0},{2,3},{3,2},{4,5},{5,4},{6,7},{7,6},{8,9},{9,8},{10,11... | collective-permute-start | bytes 6291464 | tf_op jit(solution)/shard_map/ppermute | solution.py:38
  210.5 22.9 %copy-start.3 = (bf16[128,8192]{1,0:T(8,128)(2,1)S(1)}, bf16[128,8192]{1,0:T(8,128)(2,1)}, u32[]{:S(2)}) copy-start(bf16[128,8192]{1,0:T(8,128)(2,1)} %copy-done.2) | copy-start | bytes 6291460
  211.3 9.1 %collective-permute-start.31 = (bf16[16,8192]{1,0:T(8,128)(2,1)S(1)}, bf16[16,8192]{1,0:T(8,128)(2,1)S(1)}, u32[]{:S(2)}, u32[]{:S(2)}) collective-permute-start(bf16[16,8192]{1,0:T(8,128)(2,1)S(1)} %slice.124), channel_id=1, source_target_pairs={{0,2},{1,3},{2,4},{3,5},{4,6},{5,7},{6,0},{7,1},{8,10},{9,11},{10,... | collective-permute-start | bytes 786440 | tf_op jit(solution)/shard_map/ppermute | solution.py:38
  220.4 7.0 %collective-permute-start.32 = (bf16[16,8192]{1,0:T(8,128)(2,1)S(1)}, bf16[16,8192]{1,0:T(8,128)(2,1)S(1)}, u32[]{:S(2)}, u32[]{:S(2)}) collective-permute-start(bf16[16,8192]{1,0:T(8,128)(2,1)S(1)} %slice.125), channel_id=1, source_target_pairs={{0,6},{1,7},{2,0},{3,1},{4,2},{5,3},{6,4},{7,5},{8,14},{9,15},{10,... | collective-permute-start | bytes 786440 | tf_op jit(solution)/shard_map/ppermute | solution.py:38
  228.1 7.4 %collective-permute-start.33 = (bf16[128,8192]{1,0:T(8,128)(2,1)}, bf16[128,8192]{1,0:T(8,128)(2,1)}, u32[]{:S(2)}, u32[]{:S(2)}) collective-permute-start(bf16[128,8192]{1,0:T(8,128)(2,1)} %constant_dynamic-update-slice_fusion.31.refs_6_), channel_id=1, source_target_pairs={{0,1},{1,0},{2,3},{3,2},{4,5},{5,4},{6,7},{7,6},{8,9},{9,8},{10,11... | collective-permute-start | bytes 6291464 | tf_op jit(solution)/shard_map/ppermute | solution.py:38
  236.6 43.8 %copy-start.1 = (bf16[5120,320]{0,1:T(8,128)(2,1)S(1)}, bf16[5120,320]{0,1:T(8,128)(2,1)}, u32[]{:S(2)}) copy-start(bf16[5120,320]{0,1:T(8,128)(2,1)} %param.17) | copy-start | bytes 9830404
Sparse Core Ops, SparseCore 0:
  10.2 139.3 all-gather.1

commit v2 on v1

v2 whole, which is shorter than its diff:
```python
import jax
import jax.numpy as jnp
from jax import lax
from jax.experimental import pallas as pl
from jax.experimental.pallas import tpu as pltpu
from jax.sharding import PartitionSpec as P


HEAD_DIM = 128
KEEP_SCALE = 1.0 / 0.9
K_BLOCKS = 8

UP = [(t, (t + 2) % 8) for t in range(8)]
DOWN = [(t, (t - 2) % 8) for t in range(8)]
ACROSS = [(t, t ^ 1) for t in range(8)]


def layer_norm(inputs, gain, bias):
    widened = inputs.astype(jnp.float32)
    center = jnp.mean(widened, axis=-1, keepdims=True)
    spread = jnp.mean((widened - center) * (widened - center), axis=-1, keepdims=True)
    return (widened - center) * lax.rsqrt(spread + 1e-06) * gain + bias


def rms_norm(inputs, gain):
    widened = inputs.astype(jnp.float32)
    inverse = lax.rsqrt(jnp.mean(widened * widened, axis=-1, keepdims=True) + 1e-06)
    return (widened * inverse * gain).astype(jnp.bfloat16)


def after(value, *others):
    return lax.optimization_barrier((value,) + others)[0]


def shift(value, perm):
    return lax.ppermute(value, "tensor", perm)


def gather_near(rows):
    return shift(rows, UP), shift(rows, DOWN)


def gather_far(near):
    half = near[0].shape[0] // 2
    return shift(near[0][:half], UP), shift(near[1][half:], DOWN)


def outgoing_rows(merged_in, image_counts, image_positions, rows_here, groups, tensor_devs):
    slots = image_positions.shape[0]
    live_slots = jnp.sum(image_counts) // 4
    usable = jnp.arange(slots, dtype=jnp.int32) < live_slots
    group = image_positions // (rows_here * tensor_devs)
    row = image_positions % rows_here
    mark = jnp.where(usable, row + 1, -1 - row).astype(jnp.bfloat16)
    order = jnp.arange(slots, dtype=jnp.int32)
    earlier = (group[:, None] == group[None, :]) & (order[:, None] < order[None, :])
    out_slot = group * (slots // groups) + jnp.sum(earlier.astype(jnp.int32), axis=0)
    chooser = (out_slot[None, :] == order[:, None]).astype(jnp.bfloat16)
    payload = jnp.concatenate([merged_in, jnp.broadcast_to(mark[:, None], (slots, 128))], axis=1)
    return jnp.dot(chooser, payload, preferred_element_type=jnp.float32).astype(jnp.bfloat16)


def project_body(owners, *refs):
    weight, bias, place, queries, keys, values, rows, total, sems = refs[-9:]
    pieces = refs[:-9]
    block = pl.program_id(0)
    step = weight.shape[0]
    owner_rows = place.shape[1]

    def copies(at):
        span = pl.ds(pl.multiple_of(at * step, step), step)
        lower = 0
        for index, piece in enumerate(pieces):
            height = piece.shape[0]
            yield pltpu.make_async_copy(piece.at[:, span], rows.at[pl.ds(lower, height), span], sems.at[at, index])
            lower += height

    @pl.when(block == 0)
    def _():
        for at in range(rows.shape[1] // step):
            for copy in copies(at):
                copy.start()

    for copy in copies(block):
        copy.wait()
    product = jnp.dot(
        rows[:, pl.ds(pl.multiple_of(block * step, step), step)], weight[...], preferred_element_type=jnp.float32
    )

    @pl.when(block == 0)
    def _():
        total[...] = product + bias[...]

    @pl.when(block > 0)
    def _():
        total[...] += product

    @pl.when(block == pl.num_programs(0) - 1)
    def _():
        wide = queries.shape[1]
        for owner in range(place.shape[0]):
            found = total[owner * owner_rows : (owner + 1) * owner_rows, :].astype(jnp.bfloat16)
            moved = jnp.dot(place[owner], found, preferred_element_type=jnp.float32).astype(jnp.bfloat16)
            at = pl.ds(pl.multiple_of(owners[owner] * owner_rows, owner_rows), owner_rows)
            queries[at, :] = moved[:, :wide]
            keys[at, :] = moved[:, wide : wide + HEAD_DIM]
            values[at, :] = moved[:, wide + HEAD_DIM :]


def project(owners, pieces, weight, bias, place):
    depth, width = weight.shape
    total_rows = sum(piece.shape[0] for piece in pieces)
    wide = width - 2 * HEAD_DIM
    outs = (wide, HEAD_DIM, HEAD_DIM)
    return pl.pallas_call(
        project_body,
        name="project",
        grid_spec=pltpu.PrefetchScalarGridSpec(
            num_scalar_prefetch=1,
            grid=(K_BLOCKS,),
            in_specs=[pl.BlockSpec(memory_space=pl.ANY)] * len(pieces)
            + [
                pl.BlockSpec((depth // K_BLOCKS, width), lambda k, o: (k, 0)),
                pl.BlockSpec((1, width), lambda k, o: (0, 0)),
                pl.BlockSpec(place.shape, lambda k, o: (0, 0, 0)),
            ],
            out_specs=[pl.BlockSpec((total_rows, columns), lambda k, o: (0, 0)) for columns in outs],
            scratch_shapes=[
                pltpu.VMEM((total_rows, depth), jnp.bfloat16),
                pltpu.VMEM((total_rows, width), jnp.float32),
                pltpu.SemaphoreType.DMA((K_BLOCKS, len(pieces))),
            ],
        ),
        out_shape=[jax.ShapeDtypeStruct((total_rows, columns), jnp.bfloat16) for columns in outs],
        compiler_params=pltpu.CompilerParams(
            dimension_semantics=("arbitrary",), vmem_limit_bytes=56 * 1024 * 1024
        ),
        cost_estimate=pl.CostEstimate(
            flops=2 * total_rows * depth * width, bytes_accessed=45_000_000, transcendentals=0
        ),
    )(owners, *pieces, weight, bias[None, :], place)


def shards(
    patches, ln_gain, ln_bias, fc1_weight, fc1_bias, fc2_weight, fc2_bias, image_counts, image_positions,
    text_embeds, keep_mask, norm_gain, qkv_weight, qkv_bias,
):
    groups = lax.axis_size("dp")
    tensor_devs = lax.axis_size("tensor")
    device = lax.axis_index("tensor")
    rows_here, _ = text_embeds.shape
    weight = lax.all_gather(qkv_weight, "dp", axis=0, tiled=True)

    patch_normed = layer_norm(patches, ln_gain, ln_bias).astype(jnp.bfloat16)
    merged_in = patch_normed.reshape(-1, 4 * patches.shape[1])
    slots, features = merged_in.shape
    outgoing = outgoing_rows(merged_in, image_counts, image_positions, rows_here, groups, tensor_devs)
    arrived = lax.all_to_all(
        outgoing.reshape(groups, slots // groups, -1), "dp", split_axis=0, concat_axis=0, tiled=True
    ).reshape(slots, -1)
    text_stream = (text_embeds.astype(jnp.float32) * keep_mask.astype(jnp.float32) * KEEP_SCALE).astype(jnp.bfloat16)
    text_normed = rms_norm(text_stream, norm_gain)
    arrived = after(arrived, text_normed)

    mark = arrived[:, features].astype(jnp.int32)
    own_row = jnp.abs(mark) - 1
    index = jnp.arange(rows_here, dtype=jnp.int32)
    lookup = own_row[:, None] == index[None, :]
    named = jnp.any(lookup, axis=0)
    rank = index - jnp.sum((own_row[:, None] < index[None, :]).astype(jnp.int32), axis=0)
    kept = rows_here - slots
    keep = (jnp.arange(kept, dtype=jnp.int32)[:, None] == rank[None, :]) & ~named[None, :]
    text_kept = jnp.dot(keep.astype(jnp.bfloat16), text_normed, preferred_element_type=jnp.float32).astype(jnp.bfloat16)

    near = gather_near(arrived)
    far = gather_far((after(near[0], text_kept), near[1]))
    mine = jnp.concatenate([arrived, *near, *far], axis=0)
    together = jnp.concatenate([mine, shift(mine, ACROSS)], axis=0)
    text_kept = after(text_kept, *far)
    x_near = gather_near(text_kept)

    product = jnp.dot(together[:, :features], fc1_weight, preferred_element_type=jnp.float32) + fc1_bias
    hidden = jax.nn.gelu(product, approximate=False).astype(jnp.bfloat16)
    for_other = jnp.dot(hidden[4 * slots :], fc2_weight, preferred_element_type=jnp.float32).astype(jnp.bfloat16)
    theirs = shift(for_other, ACROSS)
    partial = jnp.dot(hidden[: 4 * slots], fc2_weight, preferred_element_type=jnp.float32).astype(jnp.bfloat16)
    partial = lax.optimization_barrier(partial)
    paired = (partial.astype(jnp.float32) + theirs.astype(jnp.float32)).astype(jnp.bfloat16)
    half = slots // 2
    low = shift(paired[3 * slots : 3 * slots + half], UP)
    high = shift(paired[3 * slots + half : 4 * slots], DOWN)
    zeros = jnp.zeros_like(low)
    to_above = paired[2 * slots : 3 * slots].astype(jnp.float32) + jnp.concatenate([low, zeros], axis=0).astype(jnp.float32)
    to_below = paired[slots : 2 * slots].astype(jnp.float32) + jnp.concatenate([zeros, high], axis=0).astype(jnp.float32)
    from_below = shift(to_above.astype(jnp.bfloat16), UP)
    from_above = shift(to_below.astype(jnp.bfloat16), DOWN)
    summed = paired[:slots].astype(jnp.float32) + from_below.astype(jnp.float32) + from_above.astype(jnp.float32)
    tokens = (summed + fc2_bias).astype(jnp.bfloat16)

    token_mask = jnp.dot(
        lookup.astype(jnp.bfloat16), keep_mask.astype(jnp.bfloat16), preferred_element_type=jnp.float32
    )
    unused = jnp.dot(lookup.astype(jnp.bfloat16), text_stream, preferred_element_type=jnp.float32)
    token_stream = jnp.where(mark[:, None] > 0, tokens.astype(jnp.float32) * token_mask * KEEP_SCALE, unused)
    token_stream = token_stream.astype(jnp.bfloat16)
    token_normed = rms_norm(token_stream, norm_gain)
    t_near = gather_near(token_normed)
    landed = lax.dot_general(
        lookup.astype(jnp.bfloat16), token_stream, (((0,), (0,)), ((), ())), preferred_element_type=jnp.float32
    )
    stream = jnp.where(named[:, None], landed.astype(jnp.bfloat16), text_stream)

    slot_row = (jnp.abs(together[:, features].astype(jnp.int32)) - 1).reshape(tensor_devs, 1, slots)
    at_slot = slot_row == index[None, :, None]
    ranks = index[None, :] - jnp.sum((slot_row < index[None, :, None]).astype(jnp.int32), axis=2)
    at_kept = (ranks[:, :, None] == jnp.arange(kept, dtype=jnp.int32)) & ~jnp.any(at_slot, axis=2)[:, :, None]
    place = jnp.concatenate([at_kept, at_slot], axis=2).astype(jnp.bfloat16)
    owners = jnp.stack([(base + step) & 7 for base in (device, device ^ 1) for step in (0, -2, 2, 4)])
    owners = owners.astype(jnp.int32)

    x_far = gather_far((after(x_near[0], place, owners), x_near[1]))
    t_far = gather_far((after(t_near[0], stream), t_near[1]))
    pieces = [text_kept, token_normed, x_near[0], t_near[0], x_near[1], t_near[1], *x_far, *t_far]
    pieces = pieces + [shift(piece, ACROSS) for piece in pieces]
    queries, keys, values = project(owners, pieces, weight, qkv_bias, place)
    return (stream, queries, keys, values)


def solution(mesh):
    placed = (
        P(("dp", "tensor"), None), P(), P(), P(None, "tensor"), P("tensor"), P("tensor", None), P(),
        P(("dp", "tensor"), None), P(("dp", "tensor")), P(("dp", "tensor"), None), P(("dp", "tensor"), None),
        P(), P("dp", "tensor"), P("tensor"),
    )

    return jax.shard_map(
        shards, mesh=mesh, in_specs=placed,
        out_specs=(P(("dp", "tensor"), None), P("dp", "tensor"), P("dp", "tensor"), P("dp", "tensor")),
        check_vma=False,
    )
```

time: 288 us -> 227 us (0.79)
  starting transfers between devices: 72.2 us -> 42.7 us
  local copies, waits for them, and re-layouts: 42 us -> 16.1 us
  Pallas kernels: 43.8 us -> 35.6 us
  matrix products: 16.1 us -> 20.5 us
  waiting for transfers between devices: 78.7 us -> 75.6 us
    ppermute x35 -> x28, starting transfers between devices: 63.5 us -> 34 us  [shift(): return lax.ppermute(value, 'tensor', perm)]
    unnamed x56 -> x62, local copies, waits for them, and re-layouts: 22.9 us -> 6.45 us
    pallas_call x1, Pallas kernels: 43.8 us -> 35.6 us  [project(): pl.pallas_call(project_body, name='project', grid_spec=pltpu.PrefetchScal...]
    slice x14 -> x6, local copies, waits for them, and re-layouts: 7.29 us -> 2.44 us  [gather_far(): return (shift(near[0][:half], UP), shift(near[1][half:], DOWN))]
    dot_general x3 -> x7, matrix products: 14.2 us -> 18.5 us  [the longest x1 4 us: shards(): jnp.dot(hidden[:4 * slots], fc2_weight, preferred_element_type=jnp.float32)]
    concatenate x7 -> x2, local copies, waits for them, and re-layouts: 3.78 us -> 0.2 us  [the longest x1 0.17 us: shards(): together = jnp.concatenate([mine, shift(mine, ACROSS)], axis=0)]
    ppermute x35 -> x28, waiting for transfers between devices: 73.7 us -> 70.6 us  [shift(): return lax.ppermute(value, 'tensor', perm)]
  transfers between devices with their start and end apart: 37 -> 30, of which waited for: 14 -> 11; matrix products, arithmetic and copies ran while one was open for 25% -> 22% of each run, Pallas kernels for 0% -> 0%
where the time goes in v2:
time: 227 us; the launch traced here: 226 us
  waiting for transfers between devices  75.6 us (33%)
  starting transfers between devices  42.7 us (19%)
  Pallas kernels  35.6 us (16%)
  matrix products  20.5 us (9%)
  other arithmetic  18.7 us (8%)
  between operations  17.1 us (8%)
  local copies, waits for them, and re-layouts  16.1 us (7%)
    ppermute x28, waiting for transfers between devices, shift(): return lax.ppermute(value, 'tensor', perm)  70.6 us
    pallas_call x1, Pallas kernels, project(): pl.pallas_call(project_body, name='project', grid_spec=pltpu.PrefetchScal...  35.6 us
    ppermute x28, starting transfers between devices, shift(): return lax.ppermute(value, 'tensor', perm)  34 us
    all_to_all x1, starting transfers between devices, shards(): lax.all_to_all(outgoing.reshape(groups, slots // groups, -1), 'dp', split...  8.67 us
    unnamed x62, local copies, waits for them, and re-layouts  6.45 us
  transfers between devices with their start and end apart: 30, of which 11 were waited for; matrix products, arithmetic and copies ran while one was open for 22% of the time, Pallas kernels for 0%

profile of v2, /device:TPU:1, one launch (start us, length us, event | category | flops | bytes accessed | tf_op | source)
XLA Modules:
  0.0 226.3 jit_solution(6784262064660152147)
XLA Ops:
  7.2 0.7 all-gather.2.cloned.1.call-update
  7.9 1.4 reduce_sum.75
  12.0 1.1 convert_reduce_fusion
  13.1 1.2 fusion.17
  14.3 2.0 fusion.20
  16.3 1.9 reshape.90
  18.4 1.9 convolution_convert_fusion.4
  20.3 1.8 reshape.91
  22.1 8.7 %all-to-all-start = ((bf16[16,2,5248]{2,1,0:T(2,128)(2,1)}), bf16[16,2,5248]{2,1,0:T(2,128)(2,1)}, u32[]{:S(2)}, u32[]{:S(2)}) async-start(bf16[16,2,5248]{2,1,0:T(2,128)(2,1)} %reshape.91), calls=%async_computation | async-start | bytes 671744 | tf_op jit(solution)/shard_map/all_to_all | solution.py:158
  30.8 4.0 %fusion.2 = (f32[128]{0:T(128)S(1)}, bf16[128,8192]{1,0:T(8,128)(2,1)S(1)}) fusion(s32[128,8192]{1,0:T(8,128)} %param.24, bf16[128,8192]{1,0:T(8,128)(2,1)} %param.23), kind=kLoop, calls=%fused_computation.10 | loop fusion | flops 8388480 | bytes 8389120 | tf_op jit(solution)/shard_map/reduce_sum | solution.py:27
  34.8 1.3 copy-done.2
  36.1 2.0 fusion.4
  38.1 4.3 %all-to-all-done = bf16[16,2,5248]{2,1,0:T(2,128)(2,1)} async-done(((bf16[16,2,5248]{2,1,0:T(2,128)(2,1)}), bf16[16,2,5248]{2,1,0:T(2,128)(2,1)}, u32[]{:S(2)}, u32[]{:S(2)}) %all-to-all-start) | async-done | bytes 335904 | tf_op jit(solution)/shard_map/all_to_all | solution.py:158
  42.4 1.8 reshape.92
  44.2 1.2 collective-permute-start
  45.5 1.5 collective-permute-start.1
  46.9 0.8 fusion.44
  47.9 1.0 constant_dynamic-update-slice_fusion.4
  49.0 3.3 %convolution_convert_fusion.3.refs_0_ = bf16[96,8192]{1,0:T(8,128)(2,1)} fusion(bf16[128,8192]{1,0:T(8,128)(2,1)} %fusion.4, s32[128]{0:T(128)S(1)} %iota_subtract_fusion.1, pred[128]{0:T(512)(128)(4,1)S(1)} %not.16), kind=kOutput, calls=%fused_computation.3 | convolution fusion | flops 202137600 | bytes 3670656 | tf_op jit(solution)/shard_map/dot_general | solution.py:173
  52.3 0.8 collective-permute-done
  53.3 2.7 %collective-permute-start.3 = (bf16[16,5248]{1,0:T(8,128)(2,1)S(1)}, bf16[16,5248]{1,0:T(8,128)(2,1)S(1)}, u32[]{:S(2)}, u32[]{:S(2)}) collective-permute-start(bf16[16,5248]{1,0:T(8,128)(2,1)S(1)} %slice.64), channel_id=1, source_target_pairs={{0,6},{1,7},{2,0},{3,1},{4,2},{5,3},{6,4},{7,5},{8,14},{9,15},{10,... | collective-permute-start | bytes 503816 | tf_op jit(solution)/shard_map/ppermute | solution.py:36
  56.1 2.5 %collective-permute-done.2 = bf16[16,5248]{1,0:T(8,128)(2,1)S(1)} collective-permute-done((bf16[16,5248]{1,0:T(8,128)(2,1)S(1)}, bf16[16,5248]{1,0:T(8,128)(2,1)S(1)}, u32[]{:S(2)}, u32[]{:S(2)}) %collective-permute-start.2) | collective-permute-done | bytes 167968 | tf_op jit(solution)/shard_map/ppermute | solution.py:36
  58.7 4.1 %collective-permute-start.4 = (bf16[128,5248]{1,0:T(8,128)(2,1)S(1)}, bf16[128,5248]{1,0:T(8,128)(2,1)S(1)}, u32[]{:S(2)}, u32[]{:S(2)}) collective-permute-start(bf16[128,5248]{1,0:T(8,128)(2,1)S(1)} %get-tuple-element.32), channel_id=1, source_target_pairs={{0,1},{1,0},{2,3},{3,2},{4,5},{5,4},{6,7},{7,6},{8,9},{9,8},{10,11... | collective-permute-start | bytes 4030472 | tf_op jit(solution)/shard_map/ppermute | solution.py:36
  62.8 2.7 %collective-permute-done.4 = bf16[128,5248]{1,0:T(8,128)(2,1)S(1)} collective-permute-done((bf16[128,5248]{1,0:T(8,128)(2,1)S(1)}, bf16[128,5248]{1,0:T(8,128)(2,1)S(1)}, u32[]{:S(2)}, u32[]{:S(2)}) %collective-permute-start.4) | collective-permute-done | bytes 1343520 | tf_op jit(solution)/shard_map/ppermute | solution.py:36
  65.7 1.7 fusion.27
  67.4 1.2 slice-done
  69.0 2.6 %convolution_convert_fusion.1 = bf16[128,8192]{1,0:T(8,128)(2,1)} fusion(bf16[320,8192]{1,0:T(8,128)(2,1)S(1)} %bitcast.15, bf16[256,320]{0,1:T(8,128)(2,1)S(1)} %fusion.27), kind=kOutput, calls=%fused_computation.1 | convolution fusion | flops 672137216 | bytes 7421952 | tf_op jit(solution)/shard_map/dot_general | solution.py:184
  71.6 0.4 collective-permute-start.5
  72.0 0.6 stack.35.owners
  72.6 0.8 fusion.47
  73.4 3.8 %fusion.7 = f32[32,8192]{1,0:T(8,128)} fusion(s32[128,8192]{1,0:T(8,128)} %param.24, s32[32]{0:T(128)S(1)} %fusion.44), kind=kOutput, calls=%fused_computation.17 | convolution fusion | flops 68161536 | bytes 5243008 | tf_op jit(solution)/shard_map/dot_general | solution.py:200
  77.2 0.4 collective-permute-start.10
  77.6 2.6 %collective-permute-start.12 = (bf16[96,8192]{1,0:T(8,128)(2,1)}, bf16[96,8192]{1,0:T(8,128)(2,1)}, u32[]{:S(2)}, u32[]{:S(2)}) collective-permute-start(bf16[96,8192]{1,0:T(8,128)(2,1)} %convolution_convert_fusion.3.refs_0_), channel_id=1, source_target_pairs={{0,6},{1,7},{2,0},{3,1},{4,2},{5,3},{6,4},{7,5},{8,14},{9,15},{10,... | collective-permute-start | bytes 4718600 | tf_op jit(solution)/shard_map/ppermute | solution.py:36
  80.2 0.4 collective-permute-start.18
  80.6 4.0 %convolution_convert_fusion.2 = bf16[128,8192]{1,0:T(8,128)(2,1)S(1)} fusion(bf16[320,8192]{1,0:T(8,128)(2,1)} %param.19, bf16[256,320]{0,1:T(8,128)(2,1)S(1)} %fusion.27), kind=kOutput, calls=%fused_computation.2 | convolution fusion | flops 672137216 | bytes 7421952 | tf_op jit(solution)/shard_map/dot_general | solution.py:186
  84.6 1.0 add_reduce_fusion
  85.7 2.1 add_convert_fusion
  87.9 2.7 %collective-permute-start.8 = (bf16[16,8192]{1,0:T(8,128)(2,1)S(1)}, bf16[16,8192]{1,0:T(8,128)(2,1)S(1)}, u32[]{:S(2)}, u32[]{:S(2)}) collective-permute-start(bf16[16,8192]{1,0:T(8,128)(2,1)S(1)} %get-tuple-element.25), channel_id=1, source_target_pairs={{0,6},{1,7},{2,0},{3,1},{4,2},{5,3},{6,4},{7,5},{8,14},{9,15},{10,... | collective-permute-start | bytes 786440 | tf_op jit(solution)/shard_map/ppermute | solution.py:36
  91.0 29.8 %collective-permute-done.6 = bf16[16,8192]{1,0:T(8,128)(2,1)S(1)} collective-permute-done((bf16[16,8192]{1,0:T(8,128)(2,1)S(1)}, bf16[16,8192]{1,0:T(8,128)(2,1)S(1)}, u32[]{:S(2)}, u32[]{:S(2)}) %collective-permute-start.6) | collective-permute-done | bytes 262176 | tf_op jit(solution)/shard_map/ppermute | solution.py:36
  120.9 0.7 collective-permute-start.7
  121.6 2.1 collective-permute-start.9
  123.7 0.3 fusion.21
  124.0 0.9 add_convert_fusion.4.refs_22_
  125.0 1.2 slice.60
  126.2 1.2 slice.74
  127.4 2.7 %collective-permute-start.15 = (bf16[48,8192]{1,0:T(8,128)(2,1)S(1)}, bf16[48,8192]{1,0:T(8,128)(2,1)S(1)}, u32[]{:S(2)}, u32[]{:S(2)}) collective-permute-start(bf16[48,8192]{1,0:T(8,128)(2,1)S(1)} %slice.74), channel_id=1, source_target_pairs={{0,6},{1,7},{2,0},{3,1},{4,2},{5,3},{6,4},{7,5},{8,14},{9,15},{10,... | collective-permute-start | bytes 2359304 | tf_op jit(solution)/shard_map/ppermute | solution.py:36
  130.2 5.0 %collective-permute-done.7 = bf16[32,8192]{1,0:T(8,128)(2,1)S(1)} collective-permute-done((bf16[32,8192]{1,0:T(8,128)(2,1)S(1)}, bf16[32,8192]{1,0:T(8,128)(2,1)S(1)}, u32[]{:S(2)}, u32[]{:S(2)}) %collective-permute-start.7) | collective-permute-done | bytes 524320 | tf_op jit(solution)/shard_map/ppermute | solution.py:36
  135.2 2.4 %collective-permute-start.20 = (bf16[96,8192]{1,0:T(8,128)(2,1)}, bf16[96,8192]{1,0:T(8,128)(2,1)S(1)}, u32[]{:S(2)}, u32[]{:S(2)}) collective-permute-start(bf16[96,8192]{1,0:T(8,128)(2,1)} %collective-permute-done.10.refs_2_), channel_id=1, source_target_pairs={{0,1},{1,0},{2,3},{3,2},{4,5},{5,4},{6,7},{7,6},{8,9},{9,8},{10,11... | collective-permute-start | bytes 4718600 | tf_op jit(solution)/shard_map/ppermute | solution.py:36
  137.6 0.9 fusion.12
  138.8 13.1 %collective-permute-done.14.refs_6_ = bf16[48,8192]{1,0:T(8,128)(2,1)S(1)} collective-permute-done((bf16[48,8192]{1,0:T(8,128)(2,1)S(1)}, bf16[48,8192]{1,0:T(8,128)(2,1)S(1)}, u32[]{:S(2)}, u32[]{:S(2)}) %collective-permute-start.14) | collective-permute-done | bytes 786464 | tf_op jit(solution)/shard_map/ppermute | solution.py:36
  152.0 2.7 %collective-permute-start.13 = (bf16[32,8192]{1,0:T(8,128)(2,1)S(1)}, bf16[32,8192]{1,0:T(8,128)(2,1)S(1)}, u32[]{:S(2)}, u32[]{:S(2)}) collective-permute-start(bf16[32,8192]{1,0:T(8,128)(2,1)S(1)} %fusion.14.refs_1_), channel_id=1, source_target_pairs={{0,6},{1,7},{2,0},{3,1},{4,2},{5,3},{6,4},{7,5},{8,14},{9,15},{10,... | collective-permute-start | bytes 1572872 | tf_op jit(solution)/shard_map/ppermute | solution.py:36
  154.6 10.6 %collective-permute-done.11.refs_3_ = bf16[32,8192]{1,0:T(8,128)(2,1)S(1)} collective-permute-done((bf16[32,8192]{1,0:T(8,128)(2,1)S(1)}, bf16[32,8192]{1,0:T(8,128)(2,1)S(1)}, u32[]{:S(2)}, u32[]{:S(2)}) %collective-permute-start.11) | collective-permute-done | bytes 524320 | tf_op jit(solution)/shard_map/ppermute | solution.py:36
  165.2 2.3 %collective-permute-start.24 = (bf16[48,8192]{1,0:T(8,128)(2,1)S(1)}, bf16[48,8192]{1,0:T(8,128)(2,1)S(1)}, u32[]{:S(2)}, u32[]{:S(2)}) collective-permute-start(bf16[48,8192]{1,0:T(8,128)(2,1)S(1)} %collective-permute-done.14.refs_6_), channel_id=1, source_target_pairs={{0,1},{1,0},{2,3},{3,2},{4,5},{5,4},{6,7},{7,6},{8,9},{9,8},{10,11... | collective-permute-start | bytes 2359304 | tf_op jit(solution)/shard_map/ppermute | solution.py:36
  167.6 2.1 fusion
  169.8 0.5 collective-permute-start.19
  170.5 0.4 collective-permute-start.21
  171.1 2.5 %collective-permute-start.17 = (bf16[16,8192]{1,0:T(8,128)(2,1)S(1)}, bf16[16,8192]{1,0:T(8,128)(2,1)S(1)}, u32[]{:S(2)}, u32[]{:S(2)}) collective-permute-start(bf16[16,8192]{1,0:T(8,128)(2,1)S(1)} %slice.75), channel_id=1, source_target_pairs={{0,6},{1,7},{2,0},{3,1},{4,2},{5,3},{6,4},{7,5},{8,14},{9,15},{10,... | collective-permute-start | bytes 786440 | tf_op jit(solution)/shard_map/ppermute | solution.py:36
  173.7 5.6 %collective-permute-done.16.refs_8_ = bf16[16,8192]{1,0:T(8,128)(2,1)S(1)} collective-permute-done((bf16[16,8192]{1,0:T(8,128)(2,1)S(1)}, bf16[16,8192]{1,0:T(8,128)(2,1)S(1)}, u32[]{:S(2)}, u32[]{:S(2)}) %collective-permute-start.16) | collective-permute-done | bytes 262176 | tf_op jit(solution)/shard_map/ppermute | solution.py:36
  179.3 1.0 collective-permute-start.26
  180.6 0.6 broadcast_in_dim.20.refs_21_
  181.4 0.6 copy-done.19
  182.4 0.7 copy-done.24
  183.1 0.7 copy-done.25
  183.8 35.6 %project.1 = (bf16[1024,1024]{1,0:T(8,128)(2,1)}, bf16[1024,128]{1,0:T(8,128)(2,1)}, bf16[1024,128]{1,0:T(8,128)(2,1)}) custom-call(s32[8]{0:T(128)} %stack.35.owners, bf16[96,8192]{1,0:T(8,128)(2,1)} %convolution_convert_fusion.3.refs_0_, bf16[32,8192]{1,0:T(8,128)(2,1)} %copy-done.5, bf16[96,8192]{1,0:T(8,128)(2,1)} %collective-permute-done.10.refs_2_, ...), custom_call_target="tpu_custom_call" | custom-call | flops 21474836480 | bytes 45000000 | tf_op jit(solution)/shard_map/project/pallas_call | solution.py:115
  (114 shorter events, 3.8 us)
Async XLA Ops:
  7.2 58.5 %copy-start = (bf16[5120,320]{0,1:T(8,128)(2,1)S(1)}, bf16[5120,320]{0,1:T(8,128)(2,1)}, u32[]{:S(2)}) copy-start(bf16[5120,320]{0,1:T(8,128)(2,1)} %param.17) | copy-start | bytes 9830404
  7.2 11.0 %copy-start.12 = (s32[32]{0:T(128)S(1)}, s32[32]{0:T(128)}, u32[]{:S(2)}) copy-start(s32[32]{0:T(128)} %param.22) | copy-start | bytes 388
  7.2 176.6 %all-gather.2.cloned.1.call-start = ((), (), s32[]{:S(2)}) async-start(), calls=%async_computation.1 | async-start | bytes 22282240 | tf_op jit(solution)/shard_map/all_gather | solution.py:152
  22.1 20.3 %all-to-all-start = ((bf16[16,2,5248]{2,1,0:T(2,128)(2,1)}), bf16[16,2,5248]{2,1,0:T(2,128)(2,1)}, u32[]{:S(2)}, u32[]{:S(2)}) async-start(bf16[16,2,5248]{2,1,0:T(2,128)(2,1)} %reshape.91), calls=%async_computation | async-start | bytes 671744 | tf_op jit(solution)/shard_map/all_to_all | solution.py:158
  30.8 5.3 %copy-start.6 = (f32[8192]{0:T(1024)S(1)}, f32[8192]{0:T(1024)}, u32[]{:S(2)}) copy-start(f32[8192]{0:T(1024)} %param.25) | copy-start | bytes 98308
  34.8 1.3 copy-start.2
  44.2 8.9 %collective-permute-start = (bf16[32,5248]{1,0:T(8,128)(2,1)}, bf16[32,5248]{1,0:T(8,128)(2,1)S(1)}, u32[]{:S(2)}, u32[]{:S(2)}) collective-permute-start(bf16[32,5248]{1,0:T(8,128)(2,1)} %reshape.92), channel_id=1, source_target_pairs={{0,2},{1,3},{2,4},{3,5},{4,6},{5,7},{6,0},{7,1},{8,10},{9,11},{10,... | collective-permute-start | bytes 1007624 | tf_op jit(solution)/shard_map/ppermute | solution.py:36
  45.5 7.8 %collective-permute-start.1 = (bf16[32,5248]{1,0:T(8,128)(2,1)}, bf16[32,5248]{1,0:T(8,128)(2,1)S(1)}, u32[]{:S(2)}, u32[]{:S(2)}) collective-permute-start(bf16[32,5248]{1,0:T(8,128)(2,1)} %reshape.92), channel_id=1, source_target_pairs={{0,6},{1,7},{2,0},{3,1},{4,2},{5,3},{6,4},{7,5},{8,14},{9,15},{10,... | collective-permute-start | bytes 1007624 | tf_op jit(solution)/shard_map/ppermute | solution.py:36
  53.1 5.5 %collective-permute-start.2 = (bf16[16,5248]{1,0:T(8,128)(2,1)S(1)}, bf16[16,5248]{1,0:T(8,128)(2,1)S(1)}, u32[]{:S(2)}, u32[]{:S(2)}) collective-permute-start(bf16[16,5248]{1,0:T(8,128)(2,1)S(1)} %slice.49), channel_id=1, source_target_pairs={{0,2},{1,3},{2,4},{3,5},{4,6},{5,7},{6,0},{7,1},{8,10},{9,11},{10,... | collective-permute-start | bytes 503816 | tf_op jit(solution)/shard_map/ppermute | solution.py:36
  53.3 5.4 %collective-permute-start.3 = (bf16[16,5248]{1,0:T(8,128)(2,1)S(1)}, bf16[16,5248]{1,0:T(8,128)(2,1)S(1)}, u32[]{:S(2)}, u32[]{:S(2)}) collective-permute-start(bf16[16,5248]{1,0:T(8,128)(2,1)S(1)} %slice.64), channel_id=1, source_target_pairs={{0,6},{1,7},{2,0},{3,1},{4,2},{5,3},{6,4},{7,5},{8,14},{9,15},{10,... | collective-permute-start | bytes 503816 | tf_op jit(solution)/shard_map/ppermute | solution.py:36
  56.0 9.7 %copy-start.26 = (f32[320]{0:T(512)S(1)}, f32[320]{0:T(512)}, u32[]{:S(2)}) copy-start(f32[320]{0:T(512)} %param.18) | copy-start | bytes 3844
  58.7 6.8 %collective-permute-start.4 = (bf16[128,5248]{1,0:T(8,128)(2,1)S(1)}, bf16[128,5248]{1,0:T(8,128)(2,1)S(1)}, u32[]{:S(2)}, u32[]{:S(2)}) collective-permute-start(bf16[128,5248]{1,0:T(8,128)(2,1)S(1)} %get-tuple-element.32), channel_id=1, source_target_pairs={{0,1},{1,0},{2,3},{3,2},{4,5},{5,4},{6,7},{7,6},{8,9},{9,8},{10,11... | collective-permute-start | bytes 4030472 | tf_op jit(solution)/shard_map/ppermute | solution.py:36
  65.5 3.2 %slice-start = ((s8[5242880]{0:T(1024)(128)(4,1)}), s8[4194304]{0:T(1024)(128)(4,1)S(1)}, s32[]{:S(2)}) async-start(s8[5242880]{0:T(1024)(128)(4,1)} %bitcast.14), calls=%async_computation.2 | async-start | bytes 8388608
  65.7 1.7 copy-start.9
  65.7 3.3 %slice-start.1 = ((s8[5242880]{0:T(1024)(128)(4,1)}), s8[1048576]{0:T(1024)(128)(4,1)S(1)}, s32[]{:S(2)}) async-start(s8[5242880]{0:T(1024)(128)(4,1)} %bitcast.14), calls=%async_computation.3 | async-start | bytes 2097152
  71.6 14.1 %collective-permute-start.5 = (bf16[128,8192]{1,0:T(8,128)(2,1)}, bf16[128,8192]{1,0:T(8,128)(2,1)}, u32[]{:S(2)}, u32[]{:S(2)}) collective-permute-start(bf16[128,8192]{1,0:T(8,128)(2,1)} %convolution_convert_fusion.1), channel_id=1, source_target_pairs={{0,1},{1,0},{2,3},{3,2},{4,5},{5,4},{6,7},{7,6},{8,9},{9,8},{10,11... | collective-permute-start | bytes 6291464 | tf_op jit(solution)/shard_map/ppermute | solution.py:36
  77.2 47.8 %collective-permute-start.10 = (bf16[96,8192]{1,0:T(8,128)(2,1)}, bf16[96,8192]{1,0:T(8,128)(2,1)}, u32[]{:S(2)}, u32[]{:S(2)}) collective-permute-start(bf16[96,8192]{1,0:T(8,128)(2,1)} %convolution_convert_fusion.3.refs_0_), channel_id=1, source_target_pairs={{0,2},{1,3},{2,4},{3,5},{4,6},{5,7},{6,0},{7,1},{8,10},{9,11},{10,... | collective-permute-start | bytes 4718600 | tf_op jit(solution)/shard_map/ppermute | solution.py:36
  77.6 48.6 %collective-permute-start.12 = (bf16[96,8192]{1,0:T(8,128)(2,1)}, bf16[96,8192]{1,0:T(8,128)(2,1)}, u32[]{:S(2)}, u32[]{:S(2)}) collective-permute-start(bf16[96,8192]{1,0:T(8,128)(2,1)} %convolution_convert_fusion.3.refs_0_), channel_id=1, source_target_pairs={{0,6},{1,7},{2,0},{3,1},{4,2},{5,3},{6,4},{7,5},{8,14},{9,15},{10,... | collective-permute-start | bytes 4718600 | tf_op jit(solution)/shard_map/ppermute | solution.py:36
  80.2 89.6 %collective-permute-start.18 = (bf16[96,8192]{1,0:T(8,128)(2,1)}, bf16[96,8192]{1,0:T(8,128)(2,1)}, u32[]{:S(2)}, u32[]{:S(2)}) collective-permute-start(bf16[96,8192]{1,0:T(8,128)(2,1)} %convolution_convert_fusion.3.refs_0_), channel_id=1, source_target_pairs={{0,1},{1,0},{2,3},{3,2},{4,5},{5,4},{6,7},{7,6},{8,9},{9,8},{10,11... | collective-permute-start | bytes 4718600 | tf_op jit(solution)/shard_map/ppermute | solution.py:36
  87.8 33.0 %collective-permute-start.6 = (bf16[16,8192]{1,0:T(8,128)(2,1)S(1)}, bf16[16,8192]{1,0:T(8,128)(2,1)S(1)}, u32[]{:S(2)}, u32[]{:S(2)}) collective-permute-start(bf16[16,8192]{1,0:T(8,128)(2,1)S(1)} %get-tuple-element.24), channel_id=1, source_target_pairs={{0,2},{1,3},{2,4},{3,5},{4,6},{5,7},{6,0},{7,1},{8,10},{9,11},{10,... | collective-permute-start | bytes 786440 | tf_op jit(solution)/shard_map/ppermute | solution.py:36
  87.9 32.9 %collective-permute-start.8 = (bf16[16,8192]{1,0:T(8,128)(2,1)S(1)}, bf16[16,8192]{1,0:T(8,128)(2,1)S(1)}, u32[]{:S(2)}, u32[]{:S(2)}) collective-permute-start(bf16[16,8192]{1,0:T(8,128)(2,1)S(1)} %get-tuple-element.25), channel_id=1, source_target_pairs={{0,6},{1,7},{2,0},{3,1},{4,2},{5,3},{6,4},{7,5},{8,14},{9,15},{10,... | collective-permute-start | bytes 786440 | tf_op jit(solution)/shard_map/ppermute | solution.py:36
  91.0 46.6 %copy-start.3 = (bf16[128,8192]{1,0:T(8,128)(2,1)S(1)}, bf16[128,8192]{1,0:T(8,128)(2,1)}, u32[]{:S(2)}) copy-start(bf16[128,8192]{1,0:T(8,128)(2,1)} %copy-done.2) | copy-start | bytes 6291460
  91.0 46.6 %copy-start.4 = (f32[32,8192]{1,0:T(8,128)S(1)}, f32[32,8192]{1,0:T(8,128)}, u32[]{:S(2)}) copy-start(f32[32,8192]{1,0:T(8,128)} %fusion.7) | copy-start | bytes 3145732
  91.0 46.6 %copy-start.10 = (f32[8192]{0:T(1024)S(1)}, f32[8192]{0:T(1024)}, u32[]{:S(2)}) copy-start(f32[8192]{0:T(1024)} %param.20) | copy-start | bytes 98308
  120.9 14.3 %collective-permute-start.7 = (bf16[32,8192]{1,0:T(8,128)(2,1)S(1)}, bf16[32,8192]{1,0:T(8,128)(2,1)S(1)}, u32[]{:S(2)}, u32[]{:S(2)}) collective-permute-start(bf16[32,8192]{1,0:T(8,128)(2,1)S(1)} %get-tuple-element.22), channel_id=1, source_target_pairs={{0,2},{1,3},{2,4},{3,5},{4,6},{5,7},{6,0},{7,1},{8,10},{9,11},{10,... | collective-permute-start | bytes 1572872 | tf_op jit(solution)/shard_map/ppermute | solution.py:36
  121.6 16.0 %collective-permute-start.9 = (bf16[32,8192]{1,0:T(8,128)(2,1)S(1)}, bf16[32,8192]{1,0:T(8,128)(2,1)S(1)}, u32[]{:S(2)}, u32[]{:S(2)}) collective-permute-start(bf16[32,8192]{1,0:T(8,128)(2,1)S(1)} %get-tuple-element.23), channel_id=1, source_target_pairs={{0,6},{1,7},{2,0},{3,1},{4,2},{5,3},{6,4},{7,5},{8,14},{9,15},{10,... | collective-permute-start | bytes 1572872 | tf_op jit(solution)/shard_map/ppermute | solution.py:36
  126.1 25.8 %collective-permute-start.14 = (bf16[48,8192]{1,0:T(8,128)(2,1)S(1)}, bf16[48,8192]{1,0:T(8,128)(2,1)S(1)}, u32[]{:S(2)}, u32[]{:S(2)}) collective-permute-start(bf16[48,8192]{1,0:T(8,128)(2,1)S(1)} %slice.60), channel_id=1, source_target_pairs={{0,2},{1,3},{2,4},{3,5},{4,6},{5,7},{6,0},{7,1},{8,10},{9,11},{10,... | collective-permute-start | bytes 2359304 | tf_op jit(solution)/shard_map/ppermute | solution.py:36
  127.4 24.5 %collective-permute-start.15 = (bf16[48,8192]{1,0:T(8,128)(2,1)S(1)}, bf16[48,8192]{1,0:T(8,128)(2,1)S(1)}, u32[]{:S(2)}, u32[]{:S(2)}) collective-permute-start(bf16[48,8192]{1,0:T(8,128)(2,1)S(1)} %slice.74), channel_id=1, source_target_pairs={{0,6},{1,7},{2,0},{3,1},{4,2},{5,3},{6,4},{7,5},{8,14},{9,15},{10,... | collective-permute-start | bytes 2359304 | tf_op jit(solution)/shard_map/ppermute | solution.py:36
  135.2 35.7 %collective-permute-start.20 = (bf16[96,8192]{1,0:T(8,128)(2,1)}, bf16[96,8192]{1,0:T(8,128)(2,1)S(1)}, u32[]{:S(2)}, u32[]{:S(2)}) collective-permute-start(bf16[96,8192]{1,0:T(8,128)(2,1)} %collective-permute-done.10.refs_2_), channel_id=1, source_target_pairs={{0,1},{1,0},{2,3},{3,2},{4,5},{5,4},{6,7},{7,6},{8,9},{9,8},{10,11... | collective-permute-start | bytes 4718600 | tf_op jit(solution)/shard_map/ppermute | solution.py:36
  137.6 33.5 %collective-permute-start.22 = (bf16[96,8192]{1,0:T(8,128)(2,1)}, bf16[96,8192]{1,0:T(8,128)(2,1)S(1)}, u32[]{:S(2)}, u32[]{:S(2)}) collective-permute-start(bf16[96,8192]{1,0:T(8,128)(2,1)} %collective-permute-done.12.refs_4_), channel_id=1, source_target_pairs={{0,1},{1,0},{2,3},{3,2},{4,5},{5,4},{6,7},{7,6},{8,9},{9,8},{10,11... | collective-permute-start | bytes 4718600 | tf_op jit(solution)/shard_map/ppermute | solution.py:36
  138.8 31.0 %copy-start.5 = (bf16[32,8192]{1,0:T(8,128)(2,1)}, bf16[32,8192]{1,0:T(8,128)(2,1)S(1)}, u32[]{:S(2)}) copy-start(bf16[32,8192]{1,0:T(8,128)(2,1)S(1)} %fusion.14.refs_1_) | copy-start | bytes 1572868
  138.8 41.8 %copy-start.11 = (f32[1280]{0:T(1024)S(1)}, f32[1280]{0:T(1024)}, u32[]{:S(2)}) copy-start(f32[1280]{0:T(1024)} %param.27) | copy-start | bytes 15364
  151.9 17.8 %copy-start.15 = (bf16[48,8192]{1,0:T(8,128)(2,1)}, bf16[48,8192]{1,0:T(8,128)(2,1)S(1)}, u32[]{:S(2)}) copy-start(bf16[48,8192]{1,0:T(8,128)(2,1)S(1)} %collective-permute-done.14.refs_6_) | copy-start | bytes 2359300
  151.9 13.2 %collective-permute-start.11 = (bf16[32,8192]{1,0:T(8,128)(2,1)S(1)}, bf16[32,8192]{1,0:T(8,128)(2,1)S(1)}, u32[]{:S(2)}, u32[]{:S(2)}) collective-permute-start(bf16[32,8192]{1,0:T(8,128)(2,1)S(1)} %fusion.14.refs_1_), channel_id=1, source_target_pairs={{0,2},{1,3},{2,4},{3,5},{4,6},{5,7},{6,0},{7,1},{8,10},{9,11},{10,... | collective-permute-start | bytes 1572872 | tf_op jit(solution)/shard_map/ppermute | solution.py:36
  152.0 17.8 %copy-start.16 = (bf16[48,8192]{1,0:T(8,128)(2,1)}, bf16[48,8192]{1,0:T(8,128)(2,1)S(1)}, u32[]{:S(2)}) copy-start(bf16[48,8192]{1,0:T(8,128)(2,1)S(1)} %collective-permute-done.15.refs_7_) | copy-start | bytes 2359300
  152.0 15.5 %collective-permute-start.13 = (bf16[32,8192]{1,0:T(8,128)(2,1)S(1)}, bf16[32,8192]{1,0:T(8,128)(2,1)S(1)}, u32[]{:S(2)}, u32[]{:S(2)}) collective-permute-start(bf16[32,8192]{1,0:T(8,128)(2,1)S(1)} %fusion.14.refs_1_), channel_id=1, source_target_pairs={{0,6},{1,7},{2,0},{3,1},{4,2},{5,3},{6,4},{7,5},{8,14},{9,15},{10,... | collective-permute-start | bytes 1572872 | tf_op jit(solution)/shard_map/ppermute | solution.py:36
  165.2 5.4 %copy-start.7 = (bf16[32,8192]{1,0:T(8,128)(2,1)}, bf16[32,8192]{1,0:T(8,128)(2,1)S(1)}, u32[]{:S(2)}) copy-start(bf16[32,8192]{1,0:T(8,128)(2,1)S(1)} %collective-permute-done.11.refs_3_) | copy-start | bytes 1572868
  165.2 5.1 %collective-permute-start.24 = (bf16[48,8192]{1,0:T(8,128)(2,1)S(1)}, bf16[48,8192]{1,0:T(8,128)(2,1)S(1)}, u32[]{:S(2)}, u32[]{:S(2)}) collective-permute-start(bf16[48,8192]{1,0:T(8,128)(2,1)S(1)} %collective-permute-done.14.refs_6_), channel_id=1, source_target_pairs={{0,1},{1,0},{2,3},{3,2},{4,5},{5,4},{6,7},{7,6},{8,9},{9,8},{10,11... | collective-permute-start | bytes 2359304 | tf_op jit(solution)/shard_map/ppermute | solution.py:36
  167.5 3.4 %copy-start.8 = (bf16[32,8192]{1,0:T(8,128)(2,1)}, bf16[32,8192]{1,0:T(8,128)(2,1)S(1)}, u32[]{:S(2)}) copy-start(bf16[32,8192]{1,0:T(8,128)(2,1)S(1)} %collective-permute-done.13.refs_5_) | copy-start | bytes 1572868
  167.5 3.0 %collective-permute-start.25 = (bf16[48,8192]{1,0:T(8,128)(2,1)S(1)}, bf16[48,8192]{1,0:T(8,128)(2,1)S(1)}, u32[]{:S(2)}, u32[]{:S(2)}) collective-permute-start(bf16[48,8192]{1,0:T(8,128)(2,1)S(1)} %collective-permute-done.15.refs_7_), channel_id=1, source_target_pairs={{0,1},{1,0},{2,3},{3,2},{4,5},{5,4},{6,7},{7,6},{8,9},{9,8},{10,11... | collective-permute-start | bytes 2359304 | tf_op jit(solution)/shard_map/ppermute | solution.py:36
  169.8 11.4 %collective-permute-start.19 = (bf16[32,8192]{1,0:T(8,128)(2,1)S(1)}, bf16[32,8192]{1,0:T(8,128)(2,1)S(1)}, u32[]{:S(2)}, u32[]{:S(2)}) collective-permute-start(bf16[32,8192]{1,0:T(8,128)(2,1)S(1)} %fusion.14.refs_1_), channel_id=1, source_target_pairs={{0,1},{1,0},{2,3},{3,2},{4,5},{5,4},{6,7},{7,6},{8,9},{9,8},{10,11... | collective-permute-start | bytes 1572872 | tf_op jit(solution)/shard_map/ppermute | solution.py:36
  170.3 11.1 %copy-start.17 = (bf16[48,8192]{1,0:T(8,128)(2,1)}, bf16[48,8192]{1,0:T(8,128)(2,1)S(1)}, u32[]{:S(2)}) copy-start(bf16[48,8192]{1,0:T(8,128)(2,1)S(1)} %collective-permute-done.24.refs_16_) | copy-start | bytes 2359300
  170.3 9.0 %collective-permute-start.16 = (bf16[16,8192]{1,0:T(8,128)(2,1)S(1)}, bf16[16,8192]{1,0:T(8,128)(2,1)S(1)}, u32[]{:S(2)}, u32[]{:S(2)}) collective-permute-start(bf16[16,8192]{1,0:T(8,128)(2,1)S(1)} %slice.62), channel_id=1, source_target_pairs={{0,2},{1,3},{2,4},{3,5},{4,6},{5,7},{6,0},{7,1},{8,10},{9,11},{10,... | collective-permute-start | bytes 786440 | tf_op jit(solution)/shard_map/ppermute | solution.py:36
  170.5 10.9 %copy-start.18 = (bf16[48,8192]{1,0:T(8,128)(2,1)}, bf16[48,8192]{1,0:T(8,128)(2,1)S(1)}, u32[]{:S(2)}) copy-start(bf16[48,8192]{1,0:T(8,128)(2,1)S(1)} %collective-permute-done.25.refs_17_) | copy-start | bytes 2359300
  170.5 10.7 %collective-permute-start.21 = (bf16[32,8192]{1,0:T(8,128)(2,1)S(1)}, bf16[32,8192]{1,0:T(8,128)(2,1)S(1)}, u32[]{:S(2)}, u32[]{:S(2)}) collective-permute-start(bf16[32,8192]{1,0:T(8,128)(2,1)S(1)} %collective-permute-done.11.refs_3_), channel_id=1, source_target_pairs={{0,1},{1,0},{2,3},{3,2},{4,5},{5,4},{6,7},{7,6},{8,9},{9,8},{10,11... | collective-permute-start | bytes 1572872 | tf_op jit(solution)/shard_map/ppermute | solution.py:36
  170.9 10.3 %copy-start.13 = (bf16[96,8192]{1,0:T(8,128)(2,1)}, bf16[96,8192]{1,0:T(8,128)(2,1)S(1)}, u32[]{:S(2)}) copy-start(bf16[96,8192]{1,0:T(8,128)(2,1)S(1)} %collective-permute-done.20.refs_12_) | copy-start | bytes 4718596
  170.9 10.3 %collective-permute-start.23 = (bf16[32,8192]{1,0:T(8,128)(2,1)S(1)}, bf16[32,8192]{1,0:T(8,128)(2,1)S(1)}, u32[]{:S(2)}, u32[]{:S(2)}) collective-permute-start(bf16[32,8192]{1,0:T(8,128)(2,1)S(1)} %collective-permute-done.13.refs_5_), channel_id=1, source_target_pairs={{0,1},{1,0},{2,3},{3,2},{4,5},{5,4},{6,7},{7,6},{8,9},{9,8},{10,11... | collective-permute-start | bytes 1572872 | tf_op jit(solution)/shard_map/ppermute | solution.py:36
  171.1 10.3 %copy-start.14 = (bf16[96,8192]{1,0:T(8,128)(2,1)}, bf16[96,8192]{1,0:T(8,128)(2,1)S(1)}, u32[]{:S(2)}) copy-start(bf16[96,8192]{1,0:T(8,128)(2,1)S(1)} %collective-permute-done.22.refs_14_) | copy-start | bytes 4718596
  171.1 9.1 %collective-permute-start.17 = (bf16[16,8192]{1,0:T(8,128)(2,1)S(1)}, bf16[16,8192]{1,0:T(8,128)(2,1)S(1)}, u32[]{:S(2)}, u32[]{:S(2)}) collective-permute-start(bf16[16,8192]{1,0:T(8,128)(2,1)S(1)} %slice.75), channel_id=1, source_target_pairs={{0,6},{1,7},{2,0},{3,1},{4,2},{5,3},{6,4},{7,5},{8,14},{9,15},{10,... | collective-permute-start | bytes 786440 | tf_op jit(solution)/shard_map/ppermute | solution.py:36
  179.3 4.5 %copy-start.22 = (bf16[16,8192]{1,0:T(8,128)(2,1)}, bf16[16,8192]{1,0:T(8,128)(2,1)S(1)}, u32[]{:S(2)}) copy-start(bf16[16,8192]{1,0:T(8,128)(2,1)S(1)} %collective-permute-done.16.refs_8_) | copy-start | bytes 786436
  179.3 2.1 collective-permute-start.26
  180.3 1.2 copy-start.23
  180.3 2.1 collective-permute-start.27
  181.2 0.8 copy-start.19
  181.2 1.0 copy-start.20
  181.2 1.1 copy-start.21
  182.4 0.7 copy-start.24
  183.1 0.7 copy-start.25
  183.8 35.6 %copy-start.1 = (bf16[5120,320]{0,1:T(8,128)(2,1)S(1)}, bf16[5120,320]{0,1:T(8,128)(2,1)}, u32[]{:S(2)}) copy-start(bf16[5120,320]{0,1:T(8,128)(2,1)} %param.17) | copy-start | bytes 9830404
Sparse Core Ops, SparseCore 0:
  10.2 139.3 all-gather.1

commit v3 on v2

--- a/solution.py
+++ b/solution.py
@@ -1,3 +1,5 @@
+import functools
+
 import jax
 import jax.numpy as jnp
 from jax import lax
@@ -9,17 +11,11 @@
 HEAD_DIM = 128
 KEEP_SCALE = 1.0 / 0.9
 K_BLOCKS = 8
+TENSOR = 8
 
 UP = [(t, (t + 2) % 8) for t in range(8)]
 DOWN = [(t, (t - 2) % 8) for t in range(8)]
 ACROSS = [(t, t ^ 1) for t in range(8)]
-
-
-def layer_norm(inputs, gain, bias):
-    widened = inputs.astype(jnp.float32)
-    center = jnp.mean(widened, axis=-1, keepdims=True)
-    spread = jnp.mean((widened - center) * (widened - center), axis=-1, keepdims=True)
-    return (widened - center) * lax.rsqrt(spread + 1e-06) * gain + bias
 
 
 def rms_norm(inputs, gain):
@@ -45,19 +41,46 @@
     return shift(near[0][:half], UP), shift(near[1][half:], DOWN)
 
 
-def outgoing_rows(merged_in, image_counts, image_positions, rows_here, groups, tensor_devs):
+def outgoing_body(rows_here, groups, counts, patches, gain, shift_by, positions, out):
+    slots = out.shape[0]
+    width = patches.shape[1]
+    live = (counts[0, 0] + counts[0, 1] + counts[0, 2] + counts[0, 3]) // 4
+    widened = patches[...].astype(jnp.float32)
+    centered = widened - jnp.mean(widened, axis=-1, keepdims=True)
+    spread = jnp.mean(centered * centered, axis=-1, keepdims=True)
+    normed = (centered * lax.rsqrt(spread + 1e-06) * gain[...] + shift_by[...]).astype(jnp.bfloat16)
+
+    first = lax.broadcasted_iota(jnp.int32, (slots, slots), 0)
+    second = lax.broadcasted_iota(jnp.int32, (slots, slots), 1)
+    position = jnp.broadcast_to(positions[...], (slots, slots))
+    group = position // (rows_here * TENSOR)
+    row = position % rows_here + 1
+    mark = jnp.where(second < live, row, -row).astype(jnp.float32)
+    own_group = jnp.sum(jnp.where(first == second, group, 0).astype(jnp.float32), axis=1, keepdims=True)
+    earlier = (own_group == group.astype(jnp.float32)) & (first < second)
+    rank = jnp.sum(earlier.astype(jnp.float32), axis=0, keepdims=True)
+    chosen = group.astype(jnp.float32) * (slots // groups) + rank == first.astype(jnp.float32)
+    source = jnp.sum(jnp.where(chosen, second, 0).astype(jnp.float32), axis=1, keepdims=True)
+    marked = jnp.sum(jnp.where(chosen, mark, 0.0), axis=1, keepdims=True)
+    patch = lax.broadcasted_iota(jnp.int32, (slots, patches.shape[0]), 1).astype(jnp.float32)
+    for quarter in range(4):
+        pick = (patch == 4.0 * source + quarter).astype(jnp.bfloat16)
+        joined = jnp.dot(pick, normed, preferred_element_type=jnp.float32)
+        out[:, quarter * width : (quarter + 1) * width] = joined.astype(jnp.bfloat16)
+    out[:, 4 * width :] = jnp.broadcast_to(marked, (slots, 128)).astype(jnp.bfloat16)
+
+
+def outgoing_rows(patches, gain, shift_by, image_counts, image_positions, rows_here, groups):
     slots = image_positions.shape[0]
-    live_slots = jnp.sum(image_counts) // 4
-    usable = jnp.arange(slots, dtype=jnp.int32) < live_slots
-    group = image_positions // (rows_here * tensor_devs)
-    row = image_positions % rows_here
-    mark = jnp.where(usable, row + 1, -1 - row).astype(jnp.bfloat16)
-    order = jnp.arange(slots, dtype=jnp.int32)
-    earlier = (group[:, None] == group[None, :]) & (order[:, None] < order[None, :])
-    out_slot = group * (slots // groups) + jnp.sum(earlier.astype(jnp.int32), axis=0)
-    chooser = (out_slot[None, :] == order[:, None]).astype(jnp.bfloat16)
-    payload = jnp.concatenate([merged_in, jnp.broadcast_to(mark[:, None], (slots, 128))], axis=1)
-    return jnp.dot(chooser, payload, preferred_element_type=jnp.float32).astype(jnp.bfloat16)
+    vmem = pl.BlockSpec(memory_space=pltpu.VMEM)
+    return pl.pallas_call(
+        functools.partial(outgoing_body, rows_here, groups),
+        name="outgoing",
+        in_specs=[pl.BlockSpec(memory_space=pltpu.SMEM), vmem, vmem, vmem, vmem],
+        out_specs=vmem,
+        out_shape=jax.ShapeDtypeStruct((slots, 4 * patches.shape[1] + 128), jnp.bfloat16),
+        compiler_params=pltpu.CompilerParams(vmem_limit_bytes=16 * 1024 * 1024),
+    )(image_counts, patches, gain[None, :], shift_by[None, :], image_positions[None, :])
 
 
 def project_body(owners, *refs):
@@ -83,17 +106,15 @@
 
     for copy in copies(block):
         copy.wait()
-    product = jnp.dot(
-        rows[:, pl.ds(pl.multiple_of(block * step, step), step)], weight[...], preferred_element_type=jnp.float32
-    )
 
     @pl.when(block == 0)
     def _():
-        total[...] = product + bias[...]
-
-    @pl.when(block > 0)
-    def _():
-        total[...] += product
+        total[...] = jnp.broadcast_to(bias[...], total.shape)
+
+    span = pl.ds(pl.multiple_of(block * step, step), step)
+    half = rows.shape[0] // 2
+    for part in (slice(0, half), slice(half, 2 * half)):
+        total[part, :] += jnp.dot(rows[part, span], weight[...], preferred_element_type=jnp.float32)
 
     @pl.when(block == pl.num_programs(0) - 1)
     def _():
@@ -151,10 +172,9 @@
     rows_here, _ = text_embeds.shape
     weight = lax.all_gather(qkv_weight, "dp", axis=0, tiled=True)
 
-    patch_normed = layer_norm(patches, ln_gain, ln_bias).astype(jnp.bfloat16)
-    merged_in = patch_normed.reshape(-1, 4 * patches.shape[1])
-    slots, features = merged_in.shape
-    outgoing = outgoing_rows(merged_in, image_counts, image_positions, rows_here, groups, tensor_devs)
+    slots = image_positions.shape[0]
+    features = 4 * patches.shape[1]
+    outgoing = outgoing_rows(patches, ln_gain, ln_bias, image_counts, image_positions, rows_here, groups)
     arrived = lax.all_to_all(
         outgoing.reshape(groups, slots // groups, -1), "dp", split_axis=0, concat_axis=0, tiled=True
     ).reshape(slots, -1)
@@ -219,9 +239,16 @@
     owners = owners.astype(jnp.int32)
 
     x_far = gather_far((after(x_near[0], place, owners), x_near[1]))
-    t_far = gather_far((after(t_near[0], stream), t_near[1]))
-    pieces = [text_kept, token_normed, x_near[0], t_near[0], x_near[1], t_near[1], *x_far, *t_far]
-    pieces = pieces + [shift(piece, ACROSS) for piece in pieces]
+    early = [text_kept, *x_near, *x_far]
+    crossed = [shift(piece, ACROSS) for piece in early]
+    t_far = gather_far((after(t_near[0], stream, *crossed), t_near[1]))
+    late = [token_normed, *t_near, *t_far]
+    arrived_late = [shift(piece, ACROSS) for piece in late]
+    pieces = []
+    for kept_rows, slot_rows in ((early, late), (crossed, arrived_late)):
+        for whole in range(3):
+            pieces = pieces + [kept_rows[whole], slot_rows[whole]]
+        pieces = pieces + kept_rows[3:] + slot_rows[3:]
     queries, keys, values = project(owners, pieces, weight, qkv_bias, place)
     return (stream, queries, keys, values)
 

time: 227 us -> 206 us (0.907)
  waiting for transfers between devices: 75.6 us -> 64.6 us
  matrix products: 20.5 us -> 13.8 us
  other arithmetic: 18.7 us -> 13.4 us
  local copies, waits for them, and re-layouts: 16.1 us -> 19.6 us
  starting transfers between devices: 42.7 us -> 45.8 us
  between operations: 17.1 us -> 14.6 us
  Pallas kernels: 35.6 us -> 33.1 us
    ppermute x28, waiting for transfers between devices: 70.6 us -> 61.4 us  [shift(): return lax.ppermute(value, 'tensor', perm)]
    reduce_sum x4 -> x0, other arithmetic: 3.84 us -> none  [the longest x1 1.44 us: outgoing_rows(): live_slots = jnp.sum(image_counts) // 4]
    unnamed x62 -> x72, local copies, waits for them, and re-layouts: 6.45 us -> 10.2 us
    pallas_call x1, Pallas kernels: 35.6 us -> 32 us  [project(): pl.pallas_call(project_body, name='project', grid_spec=pltpu.PrefetchScal...]
    dot_general x1, matrix products: 3.82 us -> 0.45 us  [shards(): jnp.dot(lookup.astype(jnp.bfloat16), keep_mask.astype(jnp.bfloat16), pref...]
    ppermute x28, starting transfers between devices: 34 us -> 37.1 us  [shift(): return lax.ppermute(value, 'tensor', perm)]
  transfers between devices with their start and end apart: 30 -> 30, of which waited for: 11 -> 10; matrix products, arithmetic and copies ran while one was open for 22% -> 18% of each run, Pallas kernels for 0% -> 1%
where the time goes in v3:
time: 206 us; the launch traced here: 205 us
  waiting for transfers between devices  64.6 us (31%)
  starting transfers between devices  45.8 us (22%)
  Pallas kernels  33.1 us (16%)
  local copies, waits for them, and re-layouts  19.6 us (10%)
  between operations  14.6 us (7%)
  matrix products  13.8 us (7%)
  other arithmetic  13.4 us (7%)
    ppermute x28, waiting for transfers between devices, shift(): return lax.ppermute(value, 'tensor', perm)  61.4 us
    ppermute x28, starting transfers between devices, shift(): return lax.ppermute(value, 'tensor', perm)  37.1 us
    pallas_call x1, Pallas kernels, project(): pl.pallas_call(project_body, name='project', grid_spec=pltpu.PrefetchScal...  32 us
    unnamed x72, local copies, waits for them, and re-layouts  10.2 us
    all_to_all x1, starting transfers between devices, shards(): lax.all_to_all(outgoing.reshape(groups, slots // groups, -1), 'dp', split...  8.63 us
    reduce_sum x1, other arithmetic, rms_norm(): jnp.mean(widened * widened, axis=-1, keepdims=True) + 1e-06  4.43 us
  transfers between devices with their start and end apart: 30, of which 10 were waited for; matrix products, arithmetic and copies ran while one was open for 18% of the time, Pallas kernels for 1%

profile of v3, /device:TPU:1, one launch (start us, length us, event | category | flops | bytes accessed | tf_op | source)
XLA Modules:
  0.0 204.9 jit_solution(11161792105368053047)
XLA Ops:
  7.2 0.7 all-gather.2.cloned.1.call-update
  7.9 0.9 broadcast_in_dim.23.gain
  8.9 0.7 broadcast_in_dim.24.shift_by
  9.6 1.0 copy-done.3
  10.5 0.7 copy-done.4
  11.2 0.7 copy-done.5
  11.8 1.1 outgoing.1
  13.0 0.7 copy-done.2
  13.7 1.8 reshape.69
  15.5 8.6 %all-to-all-start = ((bf16[16,2,5248]{2,1,0:T(2,128)(2,1)}), bf16[16,2,5248]{2,1,0:T(2,128)(2,1)}, u32[]{:S(2)}, u32[]{:S(2)}) async-start(bf16[16,2,5248]{2,1,0:T(2,128)(2,1)} %reshape.69), calls=%async_computation | async-start | bytes 671744 | tf_op jit(solution)/shard_map/all_to_all | solution.py:178
  24.2 4.4 %fusion.2 = (f32[128]{0:T(128)S(1)}, bf16[128,8192]{1,0:T(8,128)(2,1)S(1)}) fusion(s32[128,8192]{1,0:T(8,128)} %param.24, bf16[128,8192]{1,0:T(8,128)(2,1)} %param.23), kind=kLoop, calls=%fused_computation.9 | loop fusion | flops 8388480 | bytes 8389120 | tf_op jit(solution)/shard_map/reduce_sum | solution.py:23
  28.7 1.3 copy-done.6
  30.0 2.0 fusion.4
  31.9 2.5 %all-to-all-done = bf16[16,2,5248]{2,1,0:T(2,128)(2,1)} async-done(((bf16[16,2,5248]{2,1,0:T(2,128)(2,1)}), bf16[16,2,5248]{2,1,0:T(2,128)(2,1)}, u32[]{:S(2)}, u32[]{:S(2)}) %all-to-all-start) | async-done | bytes 335904 | tf_op jit(solution)/shard_map/all_to_all | solution.py:178
  34.5 1.8 reshape.70
  36.3 1.3 collective-permute-start
  37.6 1.4 collective-permute-start.1
  39.0 0.8 fusion.35
  39.9 1.0 constant_dynamic-update-slice_fusion.4
  41.0 3.4 %convolution_convert_fusion.3.refs_0_ = bf16[96,8192]{1,0:T(8,128)(2,1)} fusion(bf16[128,8192]{1,0:T(8,128)(2,1)} %fusion.4, s32[128]{0:T(128)S(1)} %iota_subtract_fusion.1, pred[128]{0:T(512)(128)(4,1)S(1)} %not.16), kind=kOutput, calls=%fused_computation.3 | convolution fusion | flops 202137600 | bytes 3670656 | tf_op jit(solution)/shard_map/dot_general | solution.py:193
  44.6 2.7 %collective-permute-start.3 = (bf16[16,5248]{1,0:T(8,128)(2,1)S(1)}, bf16[16,5248]{1,0:T(8,128)(2,1)S(1)}, u32[]{:S(2)}, u32[]{:S(2)}) collective-permute-start(bf16[16,5248]{1,0:T(8,128)(2,1)S(1)} %slice.64), channel_id=1, source_target_pairs={{0,6},{1,7},{2,0},{3,1},{4,2},{5,3},{6,4},{7,5},{8,14},{9,15},{10,... | collective-permute-start | bytes 503816 | tf_op jit(solution)/shard_map/ppermute | solution.py:32
  47.5 2.9 %collective-permute-done.2 = bf16[16,5248]{1,0:T(8,128)(2,1)S(1)} collective-permute-done((bf16[16,5248]{1,0:T(8,128)(2,1)S(1)}, bf16[16,5248]{1,0:T(8,128)(2,1)S(1)}, u32[]{:S(2)}, u32[]{:S(2)}) %collective-permute-start.2) | collective-permute-done | bytes 167968 | tf_op jit(solution)/shard_map/ppermute | solution.py:32
  50.5 4.4 %collective-permute-start.4 = (bf16[128,5248]{1,0:T(8,128)(2,1)S(1)}, bf16[128,5248]{1,0:T(8,128)(2,1)S(1)}, u32[]{:S(2)}, u32[]{:S(2)}) collective-permute-start(bf16[128,5248]{1,0:T(8,128)(2,1)S(1)} %get-tuple-element.32), channel_id=1, source_target_pairs={{0,1},{1,0},{2,3},{3,2},{4,5},{5,4},{6,7},{7,6},{8,9},{9,8},{10,11... | collective-permute-start | bytes 4030472 | tf_op jit(solution)/shard_map/ppermute | solution.py:32
  54.8 2.7 %collective-permute-done.4 = bf16[128,5248]{1,0:T(8,128)(2,1)S(1)} collective-permute-done((bf16[128,5248]{1,0:T(8,128)(2,1)S(1)}, bf16[128,5248]{1,0:T(8,128)(2,1)S(1)}, u32[]{:S(2)}, u32[]{:S(2)}) %collective-permute-start.4) | collective-permute-done | bytes 1343520 | tf_op jit(solution)/shard_map/ppermute | solution.py:32
  57.8 1.7 fusion.18
  59.5 1.2 slice-done
  61.0 1.3 convolution_convert_fusion.1
  62.3 0.5 collective-permute-start.5
  62.8 0.7 stack.35.owners
  63.4 0.9 collective-permute-start.10
  64.3 2.1 %collective-permute-start.12 = (bf16[96,8192]{1,0:T(8,128)(2,1)}, bf16[96,8192]{1,0:T(8,128)(2,1)}, u32[]{:S(2)}, u32[]{:S(2)}) collective-permute-start(bf16[96,8192]{1,0:T(8,128)(2,1)} %convolution_convert_fusion.3.refs_0_), channel_id=1, source_target_pairs={{0,6},{1,7},{2,0},{3,1},{4,2},{5,3},{6,4},{7,5},{8,14},{9,15},{10,... | collective-permute-start | bytes 4718600 | tf_op jit(solution)/shard_map/ppermute | solution.py:32
  66.4 1.0 add_reduce_fusion
  67.7 3.8 %convolution_convert_fusion.2 = bf16[128,8192]{1,0:T(8,128)(2,1)S(1)} fusion(bf16[320,8192]{1,0:T(8,128)(2,1)} %param.19, bf16[256,320]{0,1:T(8,128)(2,1)S(1)} %fusion.18), kind=kOutput, calls=%fused_computation.2 | convolution fusion | flops 672137216 | bytes 7421952 | tf_op jit(solution)/shard_map/dot_general | solution.py:206
  71.7 2.2 %add_convert_fusion = bf16[128,8192]{1,0:T(8,128)(2,1)S(1)} fusion(bf16[128,8192]{1,0:T(8,128)(2,1)} %collective-permute-done.5, bf16[128,8192]{1,0:T(8,128)(2,1)S(1)} %convolution_convert_fusion.2), kind=kLoop, calls=%fused_computation.12 | loop fusion | flops 4194304 | bytes 6291456 | tf_op jit(solution)/shard_map/convert_element_type | solution.py:208
  74.2 2.7 %collective-permute-start.8 = (bf16[16,8192]{1,0:T(8,128)(2,1)S(1)}, bf16[16,8192]{1,0:T(8,128)(2,1)S(1)}, u32[]{:S(2)}, u32[]{:S(2)}) collective-permute-start(bf16[16,8192]{1,0:T(8,128)(2,1)S(1)} %get-tuple-element.25), channel_id=1, source_target_pairs={{0,6},{1,7},{2,0},{3,1},{4,2},{5,3},{6,4},{7,5},{8,14},{9,15},{10,... | collective-permute-start | bytes 786440 | tf_op jit(solution)/shard_map/ppermute | solution.py:32
  77.2 0.9 add_convert_fusion.4.refs_22_
  78.1 23.3 %collective-permute-done.10.refs_2_ = bf16[96,8192]{1,0:T(8,128)(2,1)} collective-permute-done((bf16[96,8192]{1,0:T(8,128)(2,1)}, bf16[96,8192]{1,0:T(8,128)(2,1)}, u32[]{:S(2)}, u32[]{:S(2)}) %collective-permute-start.10) | collective-permute-done | bytes 1572896 | tf_op jit(solution)/shard_map/ppermute | solution.py:32
  101.4 1.2 slice.60
  102.7 1.2 slice.74
  103.9 2.7 %collective-permute-start.15 = (bf16[48,8192]{1,0:T(8,128)(2,1)S(1)}, bf16[48,8192]{1,0:T(8,128)(2,1)S(1)}, u32[]{:S(2)}, u32[]{:S(2)}) collective-permute-start(bf16[48,8192]{1,0:T(8,128)(2,1)S(1)} %slice.74), channel_id=1, source_target_pairs={{0,6},{1,7},{2,0},{3,1},{4,2},{5,3},{6,4},{7,5},{8,14},{9,15},{10,... | collective-permute-start | bytes 2359304 | tf_op jit(solution)/shard_map/ppermute | solution.py:32
  107.1 0.7 collective-permute-start.7
  107.8 2.1 %collective-permute-start.9 = (bf16[32,8192]{1,0:T(8,128)(2,1)S(1)}, bf16[32,8192]{1,0:T(8,128)(2,1)S(1)}, u32[]{:S(2)}, u32[]{:S(2)}) collective-permute-start(bf16[32,8192]{1,0:T(8,128)(2,1)S(1)} %get-tuple-element.23), channel_id=1, source_target_pairs={{0,6},{1,7},{2,0},{3,1},{4,2},{5,3},{6,4},{7,5},{8,14},{9,15},{10,... | collective-permute-start | bytes 1572872 | tf_op jit(solution)/shard_map/ppermute | solution.py:32
  109.9 0.8 fusion.37
  111.2 0.9 copy-done.9
  112.1 1.8 collective-permute-start.16
  113.9 9.4 %collective-permute-done.14.refs_6_ = bf16[48,8192]{1,0:T(8,128)(2,1)S(1)} collective-permute-done((bf16[48,8192]{1,0:T(8,128)(2,1)S(1)}, bf16[48,8192]{1,0:T(8,128)(2,1)S(1)}, u32[]{:S(2)}, u32[]{:S(2)}) %collective-permute-start.14) | collective-permute-done | bytes 786464 | tf_op jit(solution)/shard_map/ppermute | solution.py:32
  123.3 2.0 collective-permute-start.17
  125.3 0.8 collective-permute-start.18
  126.1 8.4 %collective-permute-done.7 = bf16[32,8192]{1,0:T(8,128)(2,1)S(1)} collective-permute-done((bf16[32,8192]{1,0:T(8,128)(2,1)S(1)}, bf16[32,8192]{1,0:T(8,128)(2,1)S(1)}, u32[]{:S(2)}, u32[]{:S(2)}) %collective-permute-start.7) | collective-permute-done | bytes 524320 | tf_op jit(solution)/shard_map/ppermute | solution.py:32
  134.5 1.2 collective-permute-start.19
  135.7 1.0 fusion.12
  137.0 0.9 collective-permute-start.11
  137.9 2.6 %collective-permute-start.13 = (bf16[32,8192]{1,0:T(8,128)(2,1)S(1)}, bf16[32,8192]{1,0:T(8,128)(2,1)S(1)}, u32[]{:S(2)}, u32[]{:S(2)}) collective-permute-start(bf16[32,8192]{1,0:T(8,128)(2,1)S(1)} %fusion.14.refs_1_), channel_id=1, source_target_pairs={{0,6},{1,7},{2,0},{3,1},{4,2},{5,3},{6,4},{7,5},{8,14},{9,15},{10,... | collective-permute-start | bytes 1572872 | tf_op jit(solution)/shard_map/ppermute | solution.py:32
  140.5 2.1 %fusion = bf16[128,8192]{1,0:T(8,128)(2,1)} fusion(bf16[128,8192]{1,0:T(8,128)(2,1)S(1)} %copy-done.7, bf16[32,8192]{1,0:T(8,128)(2,1)S(1)} %get-tuple-element.39, pred[128]{0:T(512)(128)(4,1)S(1)} %fusion.36, s32[32]{0:T(128)S(1)} %fusion.35), kind=kOutput, calls=%fused_computation.4 | convolution fusion | flops 69210112 | bytes 4718848 | tf_op jit(solution)/shard_map/dot_general | solution.py:228
  142.9 9.6 %collective-permute-done.11.refs_3_ = bf16[32,8192]{1,0:T(8,128)(2,1)S(1)} collective-permute-done((bf16[32,8192]{1,0:T(8,128)(2,1)S(1)}, bf16[32,8192]{1,0:T(8,128)(2,1)S(1)}, u32[]{:S(2)}, u32[]{:S(2)}) %collective-permute-start.11) | collective-permute-done | bytes 524320 | tf_op jit(solution)/shard_map/ppermute | solution.py:32
  152.7 0.8 collective-permute-start.24
  153.6 2.9 %collective-permute-start.22 = (bf16[16,8192]{1,0:T(8,128)(2,1)S(1)}, bf16[16,8192]{1,0:T(8,128)(2,1)S(1)}, u32[]{:S(2)}, u32[]{:S(2)}) collective-permute-start(bf16[16,8192]{1,0:T(8,128)(2,1)S(1)} %slice.75), channel_id=1, source_target_pairs={{0,6},{1,7},{2,0},{3,1},{4,2},{5,3},{6,4},{7,5},{8,14},{9,15},{10,... | collective-permute-start | bytes 786440 | tf_op jit(solution)/shard_map/ppermute | solution.py:32
  156.5 4.5 %collective-permute-done.21.refs_8_ = bf16[16,8192]{1,0:T(8,128)(2,1)S(1)} collective-permute-done((bf16[16,8192]{1,0:T(8,128)(2,1)S(1)}, bf16[16,8192]{1,0:T(8,128)(2,1)S(1)}, u32[]{:S(2)}, u32[]{:S(2)}) %collective-permute-start.21) | collective-permute-done | bytes 262176 | tf_op jit(solution)/shard_map/ppermute | solution.py:32
  161.0 1.6 collective-permute-start.26
  163.0 0.6 broadcast_in_dim.32.refs_21_
  163.8 0.8 copy-done.26
  164.8 0.5 copy-done.29
  165.2 0.7 copy-done.30
  166.0 32.0 %project.1 = (bf16[1024,1024]{1,0:T(8,128)(2,1)}, bf16[1024,128]{1,0:T(8,128)(2,1)}, bf16[1024,128]{1,0:T(8,128)(2,1)}) custom-call(s32[8]{0:T(128)} %stack.35.owners, bf16[96,8192]{1,0:T(8,128)(2,1)} %convolution_convert_fusion.3.refs_0_, bf16[32,8192]{1,0:T(8,128)(2,1)} %copy-done.10, bf16[96,8192]{1,0:T(8,128)(2,1)} %collective-permute-done.10.refs_2_, ...), custom_call_target="tpu_custom_call" | custom-call | flops 21474836480 | bytes 45000000 | tf_op jit(solution)/shard_map/project/pallas_call | solution.py:136
  (115 shorter events, 4.8 us)
Async XLA Ops:
  7.2 50.5 %copy-start = (bf16[5120,320]{0,1:T(8,128)(2,1)S(1)}, bf16[5120,320]{0,1:T(8,128)(2,1)}, u32[]{:S(2)}) copy-start(bf16[5120,320]{0,1:T(8,128)(2,1)} %param.17) | copy-start | bytes 9830404
  7.2 158.8 %all-gather.2.cloned.1.call-start = ((), (), s32[]{:S(2)}) async-start(), calls=%async_computation.1 | async-start | bytes 22282240 | tf_op jit(solution)/shard_map/all_gather | solution.py:173
  9.6 1.0 copy-start.3
  10.5 0.7 copy-start.4
  11.2 0.7 copy-start.5
  13.0 0.7 copy-start.2
  15.5 18.9 %all-to-all-start = ((bf16[16,2,5248]{2,1,0:T(2,128)(2,1)}), bf16[16,2,5248]{2,1,0:T(2,128)(2,1)}, u32[]{:S(2)}, u32[]{:S(2)}) async-start(bf16[16,2,5248]{2,1,0:T(2,128)(2,1)} %reshape.69), calls=%async_computation | async-start | bytes 671744 | tf_op jit(solution)/shard_map/all_to_all | solution.py:178
  24.2 5.8 %copy-start.11 = (f32[8192]{0:T(1024)S(1)}, f32[8192]{0:T(1024)}, u32[]{:S(2)}) copy-start(f32[8192]{0:T(1024)} %param.25) | copy-start | bytes 98308
  28.6 1.3 copy-start.6
  36.3 8.2 %collective-permute-start = (bf16[32,5248]{1,0:T(8,128)(2,1)}, bf16[32,5248]{1,0:T(8,128)(2,1)S(1)}, u32[]{:S(2)}, u32[]{:S(2)}) collective-permute-start(bf16[32,5248]{1,0:T(8,128)(2,1)} %reshape.70), channel_id=1, source_target_pairs={{0,2},{1,3},{2,4},{3,5},{4,6},{5,7},{6,0},{7,1},{8,10},{9,11},{10,... | collective-permute-start | bytes 1007624 | tf_op jit(solution)/shard_map/ppermute | solution.py:32
  37.6 7.0 %collective-permute-start.1 = (bf16[32,5248]{1,0:T(8,128)(2,1)}, bf16[32,5248]{1,0:T(8,128)(2,1)S(1)}, u32[]{:S(2)}, u32[]{:S(2)}) collective-permute-start(bf16[32,5248]{1,0:T(8,128)(2,1)} %reshape.70), channel_id=1, source_target_pairs={{0,6},{1,7},{2,0},{3,1},{4,2},{5,3},{6,4},{7,5},{8,14},{9,15},{10,... | collective-permute-start | bytes 1007624 | tf_op jit(solution)/shard_map/ppermute | solution.py:32
  44.5 5.9 %collective-permute-start.2 = (bf16[16,5248]{1,0:T(8,128)(2,1)S(1)}, bf16[16,5248]{1,0:T(8,128)(2,1)S(1)}, u32[]{:S(2)}, u32[]{:S(2)}) collective-permute-start(bf16[16,5248]{1,0:T(8,128)(2,1)S(1)} %slice.49), channel_id=1, source_target_pairs={{0,2},{1,3},{2,4},{3,5},{4,6},{5,7},{6,0},{7,1},{8,10},{9,11},{10,... | collective-permute-start | bytes 503816 | tf_op jit(solution)/shard_map/ppermute | solution.py:32
  44.6 5.8 %collective-permute-start.3 = (bf16[16,5248]{1,0:T(8,128)(2,1)S(1)}, bf16[16,5248]{1,0:T(8,128)(2,1)S(1)}, u32[]{:S(2)}, u32[]{:S(2)}) collective-permute-start(bf16[16,5248]{1,0:T(8,128)(2,1)S(1)} %slice.64), channel_id=1, source_target_pairs={{0,6},{1,7},{2,0},{3,1},{4,2},{5,3},{6,4},{7,5},{8,14},{9,15},{10,... | collective-permute-start | bytes 503816 | tf_op jit(solution)/shard_map/ppermute | solution.py:32
  47.3 10.4 %copy-start.31 = (f32[320]{0:T(512)S(1)}, f32[320]{0:T(512)}, u32[]{:S(2)}) copy-start(f32[320]{0:T(512)} %param.18) | copy-start | bytes 3844
  50.5 7.1 %collective-permute-start.4 = (bf16[128,5248]{1,0:T(8,128)(2,1)S(1)}, bf16[128,5248]{1,0:T(8,128)(2,1)S(1)}, u32[]{:S(2)}, u32[]{:S(2)}) collective-permute-start(bf16[128,5248]{1,0:T(8,128)(2,1)S(1)} %get-tuple-element.32), channel_id=1, source_target_pairs={{0,1},{1,0},{2,3},{3,2},{4,5},{5,4},{6,7},{7,6},{8,9},{9,8},{10,11... | collective-permute-start | bytes 4030472 | tf_op jit(solution)/shard_map/ppermute | solution.py:32
  57.5 3.2 %slice-start = ((s8[5242880]{0:T(1024)(128)(4,1)}), s8[4194304]{0:T(1024)(128)(4,1)S(1)}, s32[]{:S(2)}) async-start(s8[5242880]{0:T(1024)(128)(4,1)} %bitcast.16), calls=%async_computation.2 | async-start | bytes 8388608
  57.7 1.7 copy-start.14
  57.7 3.3 %slice-start.1 = ((s8[5242880]{0:T(1024)(128)(4,1)}), s8[1048576]{0:T(1024)(128)(4,1)S(1)}, s32[]{:S(2)}) async-start(s8[5242880]{0:T(1024)(128)(4,1)} %bitcast.16), calls=%async_computation.3 | async-start | bytes 2097152
  62.3 9.4 %collective-permute-start.5 = (bf16[128,8192]{1,0:T(8,128)(2,1)S(1)}, bf16[128,8192]{1,0:T(8,128)(2,1)}, u32[]{:S(2)}, u32[]{:S(2)}) collective-permute-start(bf16[128,8192]{1,0:T(8,128)(2,1)S(1)} %convolution_convert_fusion.1), channel_id=1, source_target_pairs={{0,1},{1,0},{2,3},{3,2},{4,5},{5,4},{6,7},{7,6},{8,9},{9,8},{10,11... | collective-permute-start | bytes 6291464 | tf_op jit(solution)/shard_map/ppermute | solution.py:32
  63.4 38.0 %collective-permute-start.10 = (bf16[96,8192]{1,0:T(8,128)(2,1)}, bf16[96,8192]{1,0:T(8,128)(2,1)}, u32[]{:S(2)}, u32[]{:S(2)}) collective-permute-start(bf16[96,8192]{1,0:T(8,128)(2,1)} %convolution_convert_fusion.3.refs_0_), channel_id=1, source_target_pairs={{0,2},{1,3},{2,4},{3,5},{4,6},{5,7},{6,0},{7,1},{8,10},{9,11},{10,... | collective-permute-start | bytes 4718600 | tf_op jit(solution)/shard_map/ppermute | solution.py:32
  64.3 38.4 %collective-permute-start.12 = (bf16[96,8192]{1,0:T(8,128)(2,1)}, bf16[96,8192]{1,0:T(8,128)(2,1)}, u32[]{:S(2)}, u32[]{:S(2)}) collective-permute-start(bf16[96,8192]{1,0:T(8,128)(2,1)} %convolution_convert_fusion.3.refs_0_), channel_id=1, source_target_pairs={{0,6},{1,7},{2,0},{3,1},{4,2},{5,3},{6,4},{7,5},{8,14},{9,15},{10,... | collective-permute-start | bytes 4718600 | tf_op jit(solution)/shard_map/ppermute | solution.py:32
  73.9 33.1 %collective-permute-start.6 = (bf16[16,8192]{1,0:T(8,128)(2,1)S(1)}, bf16[16,8192]{1,0:T(8,128)(2,1)S(1)}, u32[]{:S(2)}, u32[]{:S(2)}) collective-permute-start(bf16[16,8192]{1,0:T(8,128)(2,1)S(1)} %get-tuple-element.24), channel_id=1, source_target_pairs={{0,2},{1,3},{2,4},{3,5},{4,6},{5,7},{6,0},{7,1},{8,10},{9,11},{10,... | collective-permute-start | bytes 786440 | tf_op jit(solution)/shard_map/ppermute | solution.py:32
  74.2 32.8 %collective-permute-start.8 = (bf16[16,8192]{1,0:T(8,128)(2,1)S(1)}, bf16[16,8192]{1,0:T(8,128)(2,1)S(1)}, u32[]{:S(2)}, u32[]{:S(2)}) collective-permute-start(bf16[16,8192]{1,0:T(8,128)(2,1)S(1)} %get-tuple-element.25), channel_id=1, source_target_pairs={{0,6},{1,7},{2,0},{3,1},{4,2},{5,3},{6,4},{7,5},{8,14},{9,15},{10,... | collective-permute-start | bytes 786440 | tf_op jit(solution)/shard_map/ppermute | solution.py:32
  78.1 32.6 %copy-start.8 = (s32[128,8192]{1,0:T(8,128)S(1)}, s32[128,8192]{1,0:T(8,128)}, u32[]{:S(2)}) copy-start(s32[128,8192]{1,0:T(8,128)} %param.24) | copy-start | bytes 12582916
  102.6 20.7 %collective-permute-start.14 = (bf16[48,8192]{1,0:T(8,128)(2,1)S(1)}, bf16[48,8192]{1,0:T(8,128)(2,1)S(1)}, u32[]{:S(2)}, u32[]{:S(2)}) collective-permute-start(bf16[48,8192]{1,0:T(8,128)(2,1)S(1)} %slice.60), channel_id=1, source_target_pairs={{0,2},{1,3},{2,4},{3,5},{4,6},{5,7},{6,0},{7,1},{8,10},{9,11},{10,... | collective-permute-start | bytes 2359304 | tf_op jit(solution)/shard_map/ppermute | solution.py:32
  103.9 21.4 %collective-permute-start.15 = (bf16[48,8192]{1,0:T(8,128)(2,1)S(1)}, bf16[48,8192]{1,0:T(8,128)(2,1)S(1)}, u32[]{:S(2)}, u32[]{:S(2)}) collective-permute-start(bf16[48,8192]{1,0:T(8,128)(2,1)S(1)} %slice.74), channel_id=1, source_target_pairs={{0,6},{1,7},{2,0},{3,1},{4,2},{5,3},{6,4},{7,5},{8,14},{9,15},{10,... | collective-permute-start | bytes 2359304 | tf_op jit(solution)/shard_map/ppermute | solution.py:32
  107.1 27.4 %collective-permute-start.7 = (bf16[32,8192]{1,0:T(8,128)(2,1)S(1)}, bf16[32,8192]{1,0:T(8,128)(2,1)S(1)}, u32[]{:S(2)}, u32[]{:S(2)}) collective-permute-start(bf16[32,8192]{1,0:T(8,128)(2,1)S(1)} %get-tuple-element.22), channel_id=1, source_target_pairs={{0,2},{1,3},{2,4},{3,5},{4,6},{5,7},{6,0},{7,1},{8,10},{9,11},{10,... | collective-permute-start | bytes 1572872 | tf_op jit(solution)/shard_map/ppermute | solution.py:32
  107.8 27.9 %collective-permute-start.9 = (bf16[32,8192]{1,0:T(8,128)(2,1)S(1)}, bf16[32,8192]{1,0:T(8,128)(2,1)S(1)}, u32[]{:S(2)}, u32[]{:S(2)}) collective-permute-start(bf16[32,8192]{1,0:T(8,128)(2,1)S(1)} %get-tuple-element.23), channel_id=1, source_target_pairs={{0,6},{1,7},{2,0},{3,1},{4,2},{5,3},{6,4},{7,5},{8,14},{9,15},{10,... | collective-permute-start | bytes 1572872 | tf_op jit(solution)/shard_map/ppermute | solution.py:32
  110.7 1.4 copy-start.9
  110.7 25.0 %copy-start.7 = (bf16[128,8192]{1,0:T(8,128)(2,1)S(1)}, bf16[128,8192]{1,0:T(8,128)(2,1)}, u32[]{:S(2)}) copy-start(bf16[128,8192]{1,0:T(8,128)(2,1)} %copy-done.6) | copy-start | bytes 6291460
  110.7 25.0 %copy-start.15 = (f32[8192]{0:T(1024)S(1)}, f32[8192]{0:T(1024)}, u32[]{:S(2)}) copy-start(f32[8192]{0:T(1024)} %param.20) | copy-start | bytes 98308
  112.1 24.8 %collective-permute-start.16 = (bf16[96,8192]{1,0:T(8,128)(2,1)S(1)}, bf16[96,8192]{1,0:T(8,128)(2,1)S(1)}, u32[]{:S(2)}, u32[]{:S(2)}) collective-permute-start(bf16[96,8192]{1,0:T(8,128)(2,1)S(1)} %copy-done.9), channel_id=1, source_target_pairs={{0,1},{1,0},{2,3},{3,2},{4,5},{5,4},{6,7},{7,6},{8,9},{9,8},{10,11... | collective-permute-start | bytes 4718600 | tf_op jit(solution)/shard_map/ppermute | solution.py:32
  123.3 13.4 %copy-start.20 = (bf16[48,8192]{1,0:T(8,128)(2,1)}, bf16[48,8192]{1,0:T(8,128)(2,1)S(1)}, u32[]{:S(2)}) copy-start(bf16[48,8192]{1,0:T(8,128)(2,1)S(1)} %collective-permute-done.14.refs_6_) | copy-start | bytes 2359300
  123.3 19.6 %collective-permute-start.17 = (bf16[96,8192]{1,0:T(8,128)(2,1)}, bf16[96,8192]{1,0:T(8,128)(2,1)S(1)}, u32[]{:S(2)}, u32[]{:S(2)}) collective-permute-start(bf16[96,8192]{1,0:T(8,128)(2,1)} %collective-permute-done.10.refs_2_), channel_id=1, source_target_pairs={{0,1},{1,0},{2,3},{3,2},{4,5},{5,4},{6,7},{7,6},{8,9},{9,8},{10,11... | collective-permute-start | bytes 4718600 | tf_op jit(solution)/shard_map/ppermute | solution.py:32
  125.3 11.4 %copy-start.21 = (bf16[48,8192]{1,0:T(8,128)(2,1)}, bf16[48,8192]{1,0:T(8,128)(2,1)S(1)}, u32[]{:S(2)}) copy-start(bf16[48,8192]{1,0:T(8,128)(2,1)S(1)} %collective-permute-done.15.refs_7_) | copy-start | bytes 2359300
  125.3 17.6 %collective-permute-start.18 = (bf16[96,8192]{1,0:T(8,128)(2,1)}, bf16[96,8192]{1,0:T(8,128)(2,1)S(1)}, u32[]{:S(2)}, u32[]{:S(2)}) collective-permute-start(bf16[96,8192]{1,0:T(8,128)(2,1)} %collective-permute-done.12.refs_4_), channel_id=1, source_target_pairs={{0,1},{1,0},{2,3},{3,2},{4,5},{5,4},{6,7},{7,6},{8,9},{9,8},{10,11... | collective-permute-start | bytes 4718600 | tf_op jit(solution)/shard_map/ppermute | solution.py:32
  134.5 3.4 %collective-permute-start.19 = (bf16[48,8192]{1,0:T(8,128)(2,1)S(1)}, bf16[48,8192]{1,0:T(8,128)(2,1)S(1)}, u32[]{:S(2)}, u32[]{:S(2)}) collective-permute-start(bf16[48,8192]{1,0:T(8,128)(2,1)S(1)} %collective-permute-done.14.refs_6_), channel_id=1, source_target_pairs={{0,1},{1,0},{2,3},{3,2},{4,5},{5,4},{6,7},{7,6},{8,9},{9,8},{10,11... | collective-permute-start | bytes 2359304 | tf_op jit(solution)/shard_map/ppermute | solution.py:32
  135.7 6.9 %collective-permute-start.20 = (bf16[48,8192]{1,0:T(8,128)(2,1)S(1)}, bf16[48,8192]{1,0:T(8,128)(2,1)S(1)}, u32[]{:S(2)}, u32[]{:S(2)}) collective-permute-start(bf16[48,8192]{1,0:T(8,128)(2,1)S(1)} %collective-permute-done.15.refs_7_), channel_id=1, source_target_pairs={{0,1},{1,0},{2,3},{3,2},{4,5},{5,4},{6,7},{7,6},{8,9},{9,8},{10,11... | collective-permute-start | bytes 2359304 | tf_op jit(solution)/shard_map/ppermute | solution.py:32
  136.9 15.6 %copy-start.10 = (bf16[32,8192]{1,0:T(8,128)(2,1)}, bf16[32,8192]{1,0:T(8,128)(2,1)S(1)}, u32[]{:S(2)}) copy-start(bf16[32,8192]{1,0:T(8,128)(2,1)S(1)} %fusion.14.refs_1_) | copy-start | bytes 1572868
  136.9 26.1 %copy-start.16 = (f32[1280]{0:T(1024)S(1)}, f32[1280]{0:T(1024)}, u32[]{:S(2)}) copy-start(f32[1280]{0:T(1024)} %param.27) | copy-start | bytes 15364
  136.9 15.6 %copy-start.17 = (bf16[96,8192]{1,0:T(8,128)(2,1)}, bf16[96,8192]{1,0:T(8,128)(2,1)S(1)}, u32[]{:S(2)}) copy-start(bf16[96,8192]{1,0:T(8,128)(2,1)S(1)} %collective-permute-done.16.refs_10_) | copy-start | bytes 4718596
  137.0 15.6 %collective-permute-start.11 = (bf16[32,8192]{1,0:T(8,128)(2,1)S(1)}, bf16[32,8192]{1,0:T(8,128)(2,1)S(1)}, u32[]{:S(2)}, u32[]{:S(2)}) collective-permute-start(bf16[32,8192]{1,0:T(8,128)(2,1)S(1)} %fusion.14.refs_1_), channel_id=1, source_target_pairs={{0,2},{1,3},{2,4},{3,5},{4,6},{5,7},{6,0},{7,1},{8,10},{9,11},{10,... | collective-permute-start | bytes 1572872 | tf_op jit(solution)/shard_map/ppermute | solution.py:32
  137.9 14.7 %copy-start.22 = (bf16[48,8192]{1,0:T(8,128)(2,1)}, bf16[48,8192]{1,0:T(8,128)(2,1)S(1)}, u32[]{:S(2)}) copy-start(bf16[48,8192]{1,0:T(8,128)(2,1)S(1)} %collective-permute-done.19.refs_16_) | copy-start | bytes 2359300
  137.9 15.5 %collective-permute-start.13 = (bf16[32,8192]{1,0:T(8,128)(2,1)S(1)}, bf16[32,8192]{1,0:T(8,128)(2,1)S(1)}, u32[]{:S(2)}, u32[]{:S(2)}) collective-permute-start(bf16[32,8192]{1,0:T(8,128)(2,1)S(1)} %fusion.14.refs_1_), channel_id=1, source_target_pairs={{0,6},{1,7},{2,0},{3,1},{4,2},{5,3},{6,4},{7,5},{8,14},{9,15},{10,... | collective-permute-start | bytes 1572872 | tf_op jit(solution)/shard_map/ppermute | solution.py:32
  142.6 21.2 %copy-start.23 = (bf16[48,8192]{1,0:T(8,128)(2,1)}, bf16[48,8192]{1,0:T(8,128)(2,1)S(1)}, u32[]{:S(2)}) copy-start(bf16[48,8192]{1,0:T(8,128)(2,1)S(1)} %collective-permute-done.20.refs_17_) | copy-start | bytes 2359300
  142.6 21.0 %collective-permute-start.23 = (bf16[32,8192]{1,0:T(8,128)(2,1)S(1)}, bf16[32,8192]{1,0:T(8,128)(2,1)S(1)}, u32[]{:S(2)}, u32[]{:S(2)}) collective-permute-start(bf16[32,8192]{1,0:T(8,128)(2,1)S(1)} %fusion.14.refs_1_), channel_id=1, source_target_pairs={{0,1},{1,0},{2,3},{3,2},{4,5},{5,4},{6,7},{7,6},{8,9},{9,8},{10,11... | collective-permute-start | bytes 1572872 | tf_op jit(solution)/shard_map/ppermute | solution.py:32
  142.9 20.7 %copy-start.18 = (bf16[96,8192]{1,0:T(8,128)(2,1)}, bf16[96,8192]{1,0:T(8,128)(2,1)S(1)}, u32[]{:S(2)}) copy-start(bf16[96,8192]{1,0:T(8,128)(2,1)S(1)} %collective-permute-done.17.refs_12_) | copy-start | bytes 4718596
  142.9 20.8 %copy-start.19 = (bf16[96,8192]{1,0:T(8,128)(2,1)}, bf16[96,8192]{1,0:T(8,128)(2,1)S(1)}, u32[]{:S(2)}) copy-start(bf16[96,8192]{1,0:T(8,128)(2,1)S(1)} %collective-permute-done.18.refs_14_) | copy-start | bytes 4718596
  152.5 11.1 %copy-start.12 = (bf16[32,8192]{1,0:T(8,128)(2,1)}, bf16[32,8192]{1,0:T(8,128)(2,1)S(1)}, u32[]{:S(2)}) copy-start(bf16[32,8192]{1,0:T(8,128)(2,1)S(1)} %collective-permute-done.11.refs_3_) | copy-start | bytes 1572868
  152.6 8.4 %collective-permute-start.21 = (bf16[16,8192]{1,0:T(8,128)(2,1)S(1)}, bf16[16,8192]{1,0:T(8,128)(2,1)S(1)}, u32[]{:S(2)}, u32[]{:S(2)}) collective-permute-start(bf16[16,8192]{1,0:T(8,128)(2,1)S(1)} %slice.62), channel_id=1, source_target_pairs={{0,2},{1,3},{2,4},{3,5},{4,6},{5,7},{6,0},{7,1},{8,10},{9,11},{10,... | collective-permute-start | bytes 786440 | tf_op jit(solution)/shard_map/ppermute | solution.py:32
  152.7 11.0 %collective-permute-start.24 = (bf16[32,8192]{1,0:T(8,128)(2,1)S(1)}, bf16[32,8192]{1,0:T(8,128)(2,1)S(1)}, u32[]{:S(2)}, u32[]{:S(2)}) collective-permute-start(bf16[32,8192]{1,0:T(8,128)(2,1)S(1)} %collective-permute-done.11.refs_3_), channel_id=1, source_target_pairs={{0,1},{1,0},{2,3},{3,2},{4,5},{5,4},{6,7},{7,6},{8,9},{9,8},{10,11... | collective-permute-start | bytes 1572872 | tf_op jit(solution)/shard_map/ppermute | solution.py:32
  153.4 10.2 %copy-start.13 = (bf16[32,8192]{1,0:T(8,128)(2,1)}, bf16[32,8192]{1,0:T(8,128)(2,1)S(1)}, u32[]{:S(2)}) copy-start(bf16[32,8192]{1,0:T(8,128)(2,1)S(1)} %collective-permute-done.13.refs_5_) | copy-start | bytes 1572868
  153.4 10.2 %collective-permute-start.25 = (bf16[32,8192]{1,0:T(8,128)(2,1)S(1)}, bf16[32,8192]{1,0:T(8,128)(2,1)S(1)}, u32[]{:S(2)}, u32[]{:S(2)}) collective-permute-start(bf16[32,8192]{1,0:T(8,128)(2,1)S(1)} %collective-permute-done.13.refs_5_), channel_id=1, source_target_pairs={{0,1},{1,0},{2,3},{3,2},{4,5},{5,4},{6,7},{7,6},{8,9},{9,8},{10,11... | collective-permute-start | bytes 1572872 | tf_op jit(solution)/shard_map/ppermute | solution.py:32
  153.6 9.0 %collective-permute-start.22 = (bf16[16,8192]{1,0:T(8,128)(2,1)S(1)}, bf16[16,8192]{1,0:T(8,128)(2,1)S(1)}, u32[]{:S(2)}, u32[]{:S(2)}) collective-permute-start(bf16[16,8192]{1,0:T(8,128)(2,1)S(1)} %slice.75), channel_id=1, source_target_pairs={{0,6},{1,7},{2,0},{3,1},{4,2},{5,3},{6,4},{7,5},{8,14},{9,15},{10,... | collective-permute-start | bytes 786440 | tf_op jit(solution)/shard_map/ppermute | solution.py:32
  161.0 4.9 %copy-start.27 = (bf16[16,8192]{1,0:T(8,128)(2,1)}, bf16[16,8192]{1,0:T(8,128)(2,1)S(1)}, u32[]{:S(2)}) copy-start(bf16[16,8192]{1,0:T(8,128)(2,1)S(1)} %collective-permute-done.21.refs_8_) | copy-start | bytes 786436
  161.0 2.7 %collective-permute-start.26 = (bf16[16,8192]{1,0:T(8,128)(2,1)S(1)}, bf16[16,8192]{1,0:T(8,128)(2,1)S(1)}, u32[]{:S(2)}, u32[]{:S(2)}) collective-permute-start(bf16[16,8192]{1,0:T(8,128)(2,1)S(1)} %collective-permute-done.21.refs_8_), channel_id=1, source_target_pairs={{0,1},{1,0},{2,3},{3,2},{4,5},{5,4},{6,7},{7,6},{8,9},{9,8},{10,11... | collective-permute-start | bytes 786440 | tf_op jit(solution)/shard_map/ppermute | solution.py:32
  162.6 1.2 copy-start.28
  162.6 1.9 collective-permute-start.27
  163.6 1.0 copy-start.24
  163.6 1.2 copy-start.25
  163.7 0.9 copy-start.26
  164.5 0.7 copy-start.29
  165.2 0.7 copy-start.30
  166.0 32.0 %copy-start.1 = (bf16[5120,320]{0,1:T(8,128)(2,1)S(1)}, bf16[5120,320]{0,1:T(8,128)(2,1)}, u32[]{:S(2)}) copy-start(bf16[5120,320]{0,1:T(8,128)(2,1)} %param.17) | copy-start | bytes 9830404
Sparse Core Ops, SparseCore 0:
  10.2 138.6 all-gather.1

commit v4 on v3

--- a/solution.py
+++ b/solution.py
@@ -159,7 +159,7 @@
         cost_estimate=pl.CostEstimate(
             flops=2 * total_rows * depth * width, bytes_accessed=45_000_000, transcendentals=0
         ),
-    )(owners, *pieces, weight, bias[None, :], place)
+    )(owners, *pieces, weight, bias, place)
 
 
 def shards(
@@ -238,18 +238,21 @@
     owners = jnp.stack([(base + step) & 7 for base in (device, device ^ 1) for step in (0, -2, 2, 4)])
     owners = owners.astype(jnp.int32)
 
-    x_far = gather_far((after(x_near[0], place, owners), x_near[1]))
+    bias = qkv_bias[None, :]
+    x_far = gather_far((after(x_near[0], place, owners, bias), x_near[1]))
     early = [text_kept, *x_near, *x_far]
     crossed = [shift(piece, ACROSS) for piece in early]
-    t_far = gather_far((after(t_near[0], stream, *crossed), t_near[1]))
+    t_far = gather_far((after(t_near[0], *crossed), t_near[1]))
     late = [token_normed, *t_near, *t_far]
-    arrived_late = [shift(piece, ACROSS) for piece in late]
+    arrived_late = [shift(piece, ACROSS) for piece in late[:3]]
+    last = after(t_far[0], stream, *arrived_late), after(t_far[1], stream, *arrived_late)
+    arrived_late = arrived_late + [shift(piece, ACROSS) for piece in last]
     pieces = []
     for kept_rows, slot_rows in ((early, late), (crossed, arrived_late)):
         for whole in range(3):
             pieces = pieces + [kept_rows[whole], slot_rows[whole]]
         pieces = pieces + kept_rows[3:] + slot_rows[3:]
-    queries, keys, values = project(owners, pieces, weight, qkv_bias, place)
+    queries, keys, values = project(owners, pieces, weight, bias, place)
     return (stream, queries, keys, values)
 
 

time: 206 us -> 208 us (level)
  waiting for transfers between devices: 64.6 us -> 66.8 us
    ppermute x28, waiting for transfers between devices: 61.4 us -> 63.5 us  [shift(): return lax.ppermute(value, 'tensor', perm)]
  transfers between devices with their start and end apart: 30 -> 30, of which waited for: 10 -> 11; matrix products, arithmetic and copies ran while one was open for 18% -> 19% of each run, Pallas kernels for 1% -> 1%
where the time goes in v4:
time: 208 us; the launch traced here: 207 us
  waiting for transfers between devices  66.8 us (32%)
  starting transfers between devices  45.7 us (22%)
  Pallas kernels  33.1 us (16%)
  local copies, waits for them, and re-layouts  18 us (9%)
  matrix products  15.1 us (7%)
  between operations  14.6 us (7%)
  other arithmetic  14.1 us (7%)
    ppermute x28, waiting for transfers between devices, shift(): return lax.ppermute(value, 'tensor', perm)  63.5 us
    ppermute x28, starting transfers between devices, shift(): return lax.ppermute(value, 'tensor', perm)  37 us
    pallas_call x1, Pallas kernels, project(): pl.pallas_call(project_body, name='project', grid_spec=pltpu.PrefetchScal...  32 us
    unnamed x72, local copies, waits for them, and re-layouts  8.75 us
    all_to_all x1, starting transfers between devices, shards(): lax.all_to_all(outgoing.reshape(groups, slots // groups, -1), 'dp', split...  8.63 us
    dot_general x1, matrix products, shards(): jnp.dot(hidden[:4 * slots], fc2_weight, preferred_element_type=jnp.float32)  5.1 us
    reduce_sum x1, other arithmetic, rms_norm(): jnp.mean(widened * widened, axis=-1, keepdims=True) + 1e-06  4.43 us
  transfers between devices with their start and end apart: 30, of which 11 were waited for; matrix products, arithmetic and copies ran while one was open for 19% of the time, Pallas kernels for 1%

profile of v4, /device:TPU:1, one launch (start us, length us, event | category | flops | bytes accessed | tf_op | source)
XLA Modules:
  0.0 207.4 jit_solution(4133643438402014545)
XLA Ops:
  7.2 0.7 all-gather.2.cloned.1.call-update
  7.9 0.9 broadcast_in_dim.23.gain
  8.9 0.7 broadcast_in_dim.24.shift_by
  9.6 1.0 copy-done.3
  10.5 0.7 copy-done.4
  11.2 0.7 copy-done.5
  11.8 1.1 outgoing.1
  13.0 0.7 copy-done.2
  13.7 1.8 reshape.69
  15.5 8.6 %all-to-all-start = ((bf16[16,2,5248]{2,1,0:T(2,128)(2,1)}), bf16[16,2,5248]{2,1,0:T(2,128)(2,1)}, u32[]{:S(2)}, u32[]{:S(2)}) async-start(bf16[16,2,5248]{2,1,0:T(2,128)(2,1)} %reshape.69), calls=%async_computation | async-start | bytes 671744 | tf_op jit(solution)/shard_map/all_to_all | solution.py:178
  24.2 4.4 %fusion.2 = (f32[128]{0:T(128)S(1)}, bf16[128,8192]{1,0:T(8,128)(2,1)S(1)}) fusion(s32[128,8192]{1,0:T(8,128)} %param.24, bf16[128,8192]{1,0:T(8,128)(2,1)} %param.23), kind=kLoop, calls=%fused_computation.9 | loop fusion | flops 8388480 | bytes 8389120 | tf_op jit(solution)/shard_map/reduce_sum | solution.py:23
  28.7 1.3 copy-done.6
  30.0 2.0 fusion.4
  31.9 2.5 %all-to-all-done = bf16[16,2,5248]{2,1,0:T(2,128)(2,1)} async-done(((bf16[16,2,5248]{2,1,0:T(2,128)(2,1)}), bf16[16,2,5248]{2,1,0:T(2,128)(2,1)}, u32[]{:S(2)}, u32[]{:S(2)}) %all-to-all-start) | async-done | bytes 335904 | tf_op jit(solution)/shard_map/all_to_all | solution.py:178
  34.5 1.8 reshape.70
  36.3 1.3 collective-permute-start
  37.6 1.4 collective-permute-start.1
  39.0 0.8 fusion.35
  39.9 1.0 constant_dynamic-update-slice_fusion.4
  41.1 3.4 %convolution_convert_fusion.3.refs_0_ = bf16[96,8192]{1,0:T(8,128)(2,1)} fusion(bf16[128,8192]{1,0:T(8,128)(2,1)} %fusion.4, s32[128]{0:T(128)S(1)} %iota_subtract_fusion.1, pred[128]{0:T(512)(128)(4,1)S(1)} %not.16), kind=kOutput, calls=%fused_computation.3 | convolution fusion | flops 202137600 | bytes 3670656 | tf_op jit(solution)/shard_map/dot_general | solution.py:193
  44.6 2.7 %collective-permute-start.3 = (bf16[16,5248]{1,0:T(8,128)(2,1)S(1)}, bf16[16,5248]{1,0:T(8,128)(2,1)S(1)}, u32[]{:S(2)}, u32[]{:S(2)}) collective-permute-start(bf16[16,5248]{1,0:T(8,128)(2,1)S(1)} %slice.64), channel_id=1, source_target_pairs={{0,6},{1,7},{2,0},{3,1},{4,2},{5,3},{6,4},{7,5},{8,14},{9,15},{10,... | collective-permute-start | bytes 503816 | tf_op jit(solution)/shard_map/ppermute | solution.py:32
  47.5 2.9 %collective-permute-done.2 = bf16[16,5248]{1,0:T(8,128)(2,1)S(1)} collective-permute-done((bf16[16,5248]{1,0:T(8,128)(2,1)S(1)}, bf16[16,5248]{1,0:T(8,128)(2,1)S(1)}, u32[]{:S(2)}, u32[]{:S(2)}) %collective-permute-start.2) | collective-permute-done | bytes 167968 | tf_op jit(solution)/shard_map/ppermute | solution.py:32
  50.5 4.4 %collective-permute-start.4 = (bf16[128,5248]{1,0:T(8,128)(2,1)S(1)}, bf16[128,5248]{1,0:T(8,128)(2,1)S(1)}, u32[]{:S(2)}, u32[]{:S(2)}) collective-permute-start(bf16[128,5248]{1,0:T(8,128)(2,1)S(1)} %get-tuple-element.36), channel_id=1, source_target_pairs={{0,1},{1,0},{2,3},{3,2},{4,5},{5,4},{6,7},{7,6},{8,9},{9,8},{10,11... | collective-permute-start | bytes 4030472 | tf_op jit(solution)/shard_map/ppermute | solution.py:32
  54.8 2.7 %collective-permute-done.4 = bf16[128,5248]{1,0:T(8,128)(2,1)S(1)} collective-permute-done((bf16[128,5248]{1,0:T(8,128)(2,1)S(1)}, bf16[128,5248]{1,0:T(8,128)(2,1)S(1)}, u32[]{:S(2)}, u32[]{:S(2)}) %collective-permute-start.4) | collective-permute-done | bytes 1343520 | tf_op jit(solution)/shard_map/ppermute | solution.py:32
  57.8 1.7 fusion.18
  59.5 1.2 slice-done
  61.0 1.3 convolution_convert_fusion.1
  62.8 0.6 broadcast_in_dim.32.refs_21_
  63.4 0.6 stack.35.owners
  64.0 0.9 collective-permute-start.10
  64.8 2.1 %collective-permute-start.12 = (bf16[96,8192]{1,0:T(8,128)(2,1)}, bf16[96,8192]{1,0:T(8,128)(2,1)}, u32[]{:S(2)}, u32[]{:S(2)}) collective-permute-start(bf16[96,8192]{1,0:T(8,128)(2,1)} %convolution_convert_fusion.3.refs_0_), channel_id=1, source_target_pairs={{0,6},{1,7},{2,0},{3,1},{4,2},{5,3},{6,4},{7,5},{8,14},{9,15},{10,... | collective-permute-start | bytes 4718600 | tf_op jit(solution)/shard_map/ppermute | solution.py:32
  67.0 5.1 %convolution_convert_fusion.2 = bf16[128,8192]{1,0:T(8,128)(2,1)} fusion(bf16[320,8192]{1,0:T(8,128)(2,1)} %param.19, bf16[256,320]{0,1:T(8,128)(2,1)S(1)} %fusion.18), kind=kOutput, calls=%fused_computation.2 | convolution fusion | flops 672137216 | bytes 7421952 | tf_op jit(solution)/shard_map/dot_general | solution.py:206
  72.1 1.0 add_reduce_fusion
  73.6 2.9 %add_convert_fusion = bf16[128,8192]{1,0:T(8,128)(2,1)S(1)} fusion(bf16[128,8192]{1,0:T(8,128)(2,1)} %collective-permute-done.5, bf16[128,8192]{1,0:T(8,128)(2,1)} %convolution_convert_fusion.2), kind=kLoop, calls=%fused_computation.12 | loop fusion | flops 4194304 | bytes 6291456 | tf_op jit(solution)/shard_map/convert_element_type | solution.py:208
  76.8 2.7 %collective-permute-start.8 = (bf16[16,8192]{1,0:T(8,128)(2,1)S(1)}, bf16[16,8192]{1,0:T(8,128)(2,1)S(1)}, u32[]{:S(2)}, u32[]{:S(2)}) collective-permute-start(bf16[16,8192]{1,0:T(8,128)(2,1)S(1)} %get-tuple-element.29), channel_id=1, source_target_pairs={{0,6},{1,7},{2,0},{3,1},{4,2},{5,3},{6,4},{7,5},{8,14},{9,15},{10,... | collective-permute-start | bytes 786440 | tf_op jit(solution)/shard_map/ppermute | solution.py:32
  79.8 0.9 add_convert_fusion.4.refs_22_
  80.7 21.2 %collective-permute-done.10.refs_2_ = bf16[96,8192]{1,0:T(8,128)(2,1)} collective-permute-done((bf16[96,8192]{1,0:T(8,128)(2,1)}, bf16[96,8192]{1,0:T(8,128)(2,1)}, u32[]{:S(2)}, u32[]{:S(2)}) %collective-permute-start.10) | collective-permute-done | bytes 1572896 | tf_op jit(solution)/shard_map/ppermute | solution.py:32
  101.9 1.2 slice.60
  103.2 1.2 slice.74
  104.4 2.7 %collective-permute-start.15 = (bf16[48,8192]{1,0:T(8,128)(2,1)S(1)}, bf16[48,8192]{1,0:T(8,128)(2,1)S(1)}, u32[]{:S(2)}, u32[]{:S(2)}) collective-permute-start(bf16[48,8192]{1,0:T(8,128)(2,1)S(1)} %slice.74), channel_id=1, source_target_pairs={{0,6},{1,7},{2,0},{3,1},{4,2},{5,3},{6,4},{7,5},{8,14},{9,15},{10,... | collective-permute-start | bytes 2359304 | tf_op jit(solution)/shard_map/ppermute | solution.py:32
  107.7 0.7 collective-permute-start.7
  108.3 2.1 collective-permute-start.9
  110.4 0.8 fusion.37
  111.7 0.9 copy-done.9
  112.6 1.8 collective-permute-start.16
  114.4 9.4 %collective-permute-done.14.refs_6_ = bf16[48,8192]{1,0:T(8,128)(2,1)S(1)} collective-permute-done((bf16[48,8192]{1,0:T(8,128)(2,1)S(1)}, bf16[48,8192]{1,0:T(8,128)(2,1)S(1)}, u32[]{:S(2)}, u32[]{:S(2)}) %collective-permute-start.14) | collective-permute-done | bytes 786464 | tf_op jit(solution)/shard_map/ppermute | solution.py:32
  123.8 2.0 collective-permute-start.17
  125.8 0.8 collective-permute-start.18
  126.6 8.4 %collective-permute-done.7 = bf16[32,8192]{1,0:T(8,128)(2,1)S(1)} collective-permute-done((bf16[32,8192]{1,0:T(8,128)(2,1)S(1)}, bf16[32,8192]{1,0:T(8,128)(2,1)S(1)}, u32[]{:S(2)}, u32[]{:S(2)}) %collective-permute-start.7) | collective-permute-done | bytes 524320 | tf_op jit(solution)/shard_map/ppermute | solution.py:32
  135.1 1.2 collective-permute-start.19
  136.2 1.0 fusion.12
  137.5 0.9 collective-permute-start.11
  138.4 2.5 %collective-permute-start.13 = (bf16[32,8192]{1,0:T(8,128)(2,1)S(1)}, bf16[32,8192]{1,0:T(8,128)(2,1)S(1)}, u32[]{:S(2)}, u32[]{:S(2)}) collective-permute-start(bf16[32,8192]{1,0:T(8,128)(2,1)S(1)} %fusion.14.refs_1_), channel_id=1, source_target_pairs={{0,6},{1,7},{2,0},{3,1},{4,2},{5,3},{6,4},{7,5},{8,14},{9,15},{10,... | collective-permute-start | bytes 1572872 | tf_op jit(solution)/shard_map/ppermute | solution.py:32
  141.3 11.7 %collective-permute-done.11.refs_3_ = bf16[32,8192]{1,0:T(8,128)(2,1)S(1)} collective-permute-done((bf16[32,8192]{1,0:T(8,128)(2,1)S(1)}, bf16[32,8192]{1,0:T(8,128)(2,1)S(1)}, u32[]{:S(2)}, u32[]{:S(2)}) %collective-permute-start.11) | collective-permute-done | bytes 524320 | tf_op jit(solution)/shard_map/ppermute | solution.py:32
  153.0 0.7 collective-permute-start.24
  153.8 2.7 %collective-permute-start.22 = (bf16[16,8192]{1,0:T(8,128)(2,1)S(1)}, bf16[16,8192]{1,0:T(8,128)(2,1)S(1)}, u32[]{:S(2)}, u32[]{:S(2)}) collective-permute-start(bf16[16,8192]{1,0:T(8,128)(2,1)S(1)} %slice.75), channel_id=1, source_target_pairs={{0,6},{1,7},{2,0},{3,1},{4,2},{5,3},{6,4},{7,5},{8,14},{9,15},{10,... | collective-permute-start | bytes 786440 | tf_op jit(solution)/shard_map/ppermute | solution.py:32
  156.7 2.1 %fusion = bf16[128,8192]{1,0:T(8,128)(2,1)} fusion(bf16[128,8192]{1,0:T(8,128)(2,1)S(1)} %copy-done.7, bf16[32,8192]{1,0:T(8,128)(2,1)S(1)} %get-tuple-element.43, pred[128]{0:T(512)(128)(4,1)S(1)} %fusion.36, s32[32]{0:T(128)S(1)} %fusion.35), kind=kOutput, calls=%fused_computation.4 | convolution fusion | flops 69210112 | bytes 4718848 | tf_op jit(solution)/shard_map/dot_general | solution.py:228
  158.9 3.4 %collective-permute-done.22.refs_9_ = bf16[16,8192]{1,0:T(8,128)(2,1)S(1)} collective-permute-done((bf16[16,8192]{1,0:T(8,128)(2,1)S(1)}, bf16[16,8192]{1,0:T(8,128)(2,1)S(1)}, u32[]{:S(2)}, u32[]{:S(2)}) %collective-permute-start.22) | collective-permute-done | bytes 262176 | tf_op jit(solution)/shard_map/ppermute | solution.py:32
  162.3 0.9 collective-permute-start.27
  163.2 2.3 %collective-permute-done.21.refs_8_ = bf16[16,8192]{1,0:T(8,128)(2,1)S(1)} collective-permute-done((bf16[16,8192]{1,0:T(8,128)(2,1)S(1)}, bf16[16,8192]{1,0:T(8,128)(2,1)S(1)}, u32[]{:S(2)}, u32[]{:S(2)}) %collective-permute-start.21) | collective-permute-done | bytes 262176 | tf_op jit(solution)/shard_map/ppermute | solution.py:32
  165.5 1.1 collective-permute-start.26
  166.7 1.1 collective-permute-done.26.refs_18_
  167.8 0.7 copy-done.30
  168.5 32.0 %project.1 = (bf16[1024,1024]{1,0:T(8,128)(2,1)}, bf16[1024,128]{1,0:T(8,128)(2,1)}, bf16[1024,128]{1,0:T(8,128)(2,1)}) custom-call(s32[8]{0:T(128)} %stack.35.owners, bf16[96,8192]{1,0:T(8,128)(2,1)} %convolution_convert_fusion.3.refs_0_, bf16[32,8192]{1,0:T(8,128)(2,1)} %copy-done.10, bf16[96,8192]{1,0:T(8,128)(2,1)} %collective-permute-done.10.refs_2_, ...), custom_call_target="tpu_custom_call" | custom-call | flops 21474836480 | bytes 45000000 | tf_op jit(solution)/shard_map/project/pallas_call | solution.py:136
  (115 shorter events, 4.6 us)
Async XLA Ops:
  7.2 50.6 %copy-start = (bf16[5120,320]{0,1:T(8,128)(2,1)S(1)}, bf16[5120,320]{0,1:T(8,128)(2,1)}, u32[]{:S(2)}) copy-start(bf16[5120,320]{0,1:T(8,128)(2,1)} %param.17) | copy-start | bytes 9830404
  7.2 161.3 %all-gather.2.cloned.1.call-start = ((), (), s32[]{:S(2)}) async-start(), calls=%async_computation.1 | async-start | bytes 22282240 | tf_op jit(solution)/shard_map/all_gather | solution.py:173
  9.6 1.0 copy-start.3
  10.5 0.7 copy-start.4
  11.2 0.7 copy-start.5
  13.0 0.7 copy-start.2
  15.5 18.9 %all-to-all-start = ((bf16[16,2,5248]{2,1,0:T(2,128)(2,1)}), bf16[16,2,5248]{2,1,0:T(2,128)(2,1)}, u32[]{:S(2)}, u32[]{:S(2)}) async-start(bf16[16,2,5248]{2,1,0:T(2,128)(2,1)} %reshape.69), calls=%async_computation | async-start | bytes 671744 | tf_op jit(solution)/shard_map/all_to_all | solution.py:178
  24.2 5.8 %copy-start.11 = (f32[8192]{0:T(1024)S(1)}, f32[8192]{0:T(1024)}, u32[]{:S(2)}) copy-start(f32[8192]{0:T(1024)} %param.25) | copy-start | bytes 98308
  28.6 1.3 copy-start.6
  36.3 8.2 %collective-permute-start = (bf16[32,5248]{1,0:T(8,128)(2,1)}, bf16[32,5248]{1,0:T(8,128)(2,1)S(1)}, u32[]{:S(2)}, u32[]{:S(2)}) collective-permute-start(bf16[32,5248]{1,0:T(8,128)(2,1)} %reshape.70), channel_id=1, source_target_pairs={{0,2},{1,3},{2,4},{3,5},{4,6},{5,7},{6,0},{7,1},{8,10},{9,11},{10,... | collective-permute-start | bytes 1007624 | tf_op jit(solution)/shard_map/ppermute | solution.py:32
  37.6 7.0 %collective-permute-start.1 = (bf16[32,5248]{1,0:T(8,128)(2,1)}, bf16[32,5248]{1,0:T(8,128)(2,1)S(1)}, u32[]{:S(2)}, u32[]{:S(2)}) collective-permute-start(bf16[32,5248]{1,0:T(8,128)(2,1)} %reshape.70), channel_id=1, source_target_pairs={{0,6},{1,7},{2,0},{3,1},{4,2},{5,3},{6,4},{7,5},{8,14},{9,15},{10,... | collective-permute-start | bytes 1007624 | tf_op jit(solution)/shard_map/ppermute | solution.py:32
  44.5 5.9 %collective-permute-start.2 = (bf16[16,5248]{1,0:T(8,128)(2,1)S(1)}, bf16[16,5248]{1,0:T(8,128)(2,1)S(1)}, u32[]{:S(2)}, u32[]{:S(2)}) collective-permute-start(bf16[16,5248]{1,0:T(8,128)(2,1)S(1)} %slice.49), channel_id=1, source_target_pairs={{0,2},{1,3},{2,4},{3,5},{4,6},{5,7},{6,0},{7,1},{8,10},{9,11},{10,... | collective-permute-start | bytes 503816 | tf_op jit(solution)/shard_map/ppermute | solution.py:32
  44.6 5.8 %collective-permute-start.3 = (bf16[16,5248]{1,0:T(8,128)(2,1)S(1)}, bf16[16,5248]{1,0:T(8,128)(2,1)S(1)}, u32[]{:S(2)}, u32[]{:S(2)}) collective-permute-start(bf16[16,5248]{1,0:T(8,128)(2,1)S(1)} %slice.64), channel_id=1, source_target_pairs={{0,6},{1,7},{2,0},{3,1},{4,2},{5,3},{6,4},{7,5},{8,14},{9,15},{10,... | collective-permute-start | bytes 503816 | tf_op jit(solution)/shard_map/ppermute | solution.py:32
  47.3 10.4 %copy-start.31 = (f32[320]{0:T(512)S(1)}, f32[320]{0:T(512)}, u32[]{:S(2)}) copy-start(f32[320]{0:T(512)} %param.18) | copy-start | bytes 3844
  50.5 7.1 %collective-permute-start.4 = (bf16[128,5248]{1,0:T(8,128)(2,1)S(1)}, bf16[128,5248]{1,0:T(8,128)(2,1)S(1)}, u32[]{:S(2)}, u32[]{:S(2)}) collective-permute-start(bf16[128,5248]{1,0:T(8,128)(2,1)S(1)} %get-tuple-element.36), channel_id=1, source_target_pairs={{0,1},{1,0},{2,3},{3,2},{4,5},{5,4},{6,7},{7,6},{8,9},{9,8},{10,11... | collective-permute-start | bytes 4030472 | tf_op jit(solution)/shard_map/ppermute | solution.py:32
  57.5 3.2 %slice-start = ((s8[5242880]{0:T(1024)(128)(4,1)}), s8[4194304]{0:T(1024)(128)(4,1)S(1)}, s32[]{:S(2)}) async-start(s8[5242880]{0:T(1024)(128)(4,1)} %bitcast.16), calls=%async_computation.2 | async-start | bytes 8388608
  57.7 1.7 copy-start.14
  57.7 3.3 %slice-start.1 = ((s8[5242880]{0:T(1024)(128)(4,1)}), s8[1048576]{0:T(1024)(128)(4,1)S(1)}, s32[]{:S(2)}) async-start(s8[5242880]{0:T(1024)(128)(4,1)} %bitcast.16), calls=%async_computation.3 | async-start | bytes 2097152
  61.0 1.8 copy-start.16
  62.3 11.3 %collective-permute-start.5 = (bf16[128,8192]{1,0:T(8,128)(2,1)S(1)}, bf16[128,8192]{1,0:T(8,128)(2,1)}, u32[]{:S(2)}, u32[]{:S(2)}) collective-permute-start(bf16[128,8192]{1,0:T(8,128)(2,1)S(1)} %convolution_convert_fusion.1), channel_id=1, source_target_pairs={{0,1},{1,0},{2,3},{3,2},{4,5},{5,4},{6,7},{7,6},{8,9},{9,8},{10,11... | collective-permute-start | bytes 6291464 | tf_op jit(solution)/shard_map/ppermute | solution.py:32
  64.0 38.0 %collective-permute-start.10 = (bf16[96,8192]{1,0:T(8,128)(2,1)}, bf16[96,8192]{1,0:T(8,128)(2,1)}, u32[]{:S(2)}, u32[]{:S(2)}) collective-permute-start(bf16[96,8192]{1,0:T(8,128)(2,1)} %convolution_convert_fusion.3.refs_0_), channel_id=1, source_target_pairs={{0,2},{1,3},{2,4},{3,5},{4,6},{5,7},{6,0},{7,1},{8,10},{9,11},{10,... | collective-permute-start | bytes 4718600 | tf_op jit(solution)/shard_map/ppermute | solution.py:32
  64.8 38.4 %collective-permute-start.12 = (bf16[96,8192]{1,0:T(8,128)(2,1)}, bf16[96,8192]{1,0:T(8,128)(2,1)}, u32[]{:S(2)}, u32[]{:S(2)}) collective-permute-start(bf16[96,8192]{1,0:T(8,128)(2,1)} %convolution_convert_fusion.3.refs_0_), channel_id=1, source_target_pairs={{0,6},{1,7},{2,0},{3,1},{4,2},{5,3},{6,4},{7,5},{8,14},{9,15},{10,... | collective-permute-start | bytes 4718600 | tf_op jit(solution)/shard_map/ppermute | solution.py:32
  76.5 31.0 %collective-permute-start.6 = (bf16[16,8192]{1,0:T(8,128)(2,1)S(1)}, bf16[16,8192]{1,0:T(8,128)(2,1)S(1)}, u32[]{:S(2)}, u32[]{:S(2)}) collective-permute-start(bf16[16,8192]{1,0:T(8,128)(2,1)S(1)} %get-tuple-element.28), channel_id=1, source_target_pairs={{0,2},{1,3},{2,4},{3,5},{4,6},{5,7},{6,0},{7,1},{8,10},{9,11},{10,... | collective-permute-start | bytes 786440 | tf_op jit(solution)/shard_map/ppermute | solution.py:32
  76.8 30.7 %collective-permute-start.8 = (bf16[16,8192]{1,0:T(8,128)(2,1)S(1)}, bf16[16,8192]{1,0:T(8,128)(2,1)S(1)}, u32[]{:S(2)}, u32[]{:S(2)}) collective-permute-start(bf16[16,8192]{1,0:T(8,128)(2,1)S(1)} %get-tuple-element.29), channel_id=1, source_target_pairs={{0,6},{1,7},{2,0},{3,1},{4,2},{5,3},{6,4},{7,5},{8,14},{9,15},{10,... | collective-permute-start | bytes 786440 | tf_op jit(solution)/shard_map/ppermute | solution.py:32
  80.7 30.5 %copy-start.8 = (s32[128,8192]{1,0:T(8,128)S(1)}, s32[128,8192]{1,0:T(8,128)}, u32[]{:S(2)}) copy-start(s32[128,8192]{1,0:T(8,128)} %param.24) | copy-start | bytes 12582916
  103.1 20.7 %collective-permute-start.14 = (bf16[48,8192]{1,0:T(8,128)(2,1)S(1)}, bf16[48,8192]{1,0:T(8,128)(2,1)S(1)}, u32[]{:S(2)}, u32[]{:S(2)}) collective-permute-start(bf16[48,8192]{1,0:T(8,128)(2,1)S(1)} %slice.60), channel_id=1, source_target_pairs={{0,2},{1,3},{2,4},{3,5},{4,6},{5,7},{6,0},{7,1},{8,10},{9,11},{10,... | collective-permute-start | bytes 2359304 | tf_op jit(solution)/shard_map/ppermute | solution.py:32
  104.4 21.4 %collective-permute-start.15 = (bf16[48,8192]{1,0:T(8,128)(2,1)S(1)}, bf16[48,8192]{1,0:T(8,128)(2,1)S(1)}, u32[]{:S(2)}, u32[]{:S(2)}) collective-permute-start(bf16[48,8192]{1,0:T(8,128)(2,1)S(1)} %slice.74), channel_id=1, source_target_pairs={{0,6},{1,7},{2,0},{3,1},{4,2},{5,3},{6,4},{7,5},{8,14},{9,15},{10,... | collective-permute-start | bytes 2359304 | tf_op jit(solution)/shard_map/ppermute | solution.py:32
  107.7 27.4 %collective-permute-start.7 = (bf16[32,8192]{1,0:T(8,128)(2,1)S(1)}, bf16[32,8192]{1,0:T(8,128)(2,1)S(1)}, u32[]{:S(2)}, u32[]{:S(2)}) collective-permute-start(bf16[32,8192]{1,0:T(8,128)(2,1)S(1)} %get-tuple-element.26), channel_id=1, source_target_pairs={{0,2},{1,3},{2,4},{3,5},{4,6},{5,7},{6,0},{7,1},{8,10},{9,11},{10,... | collective-permute-start | bytes 1572872 | tf_op jit(solution)/shard_map/ppermute | solution.py:32
  108.3 27.9 %collective-permute-start.9 = (bf16[32,8192]{1,0:T(8,128)(2,1)S(1)}, bf16[32,8192]{1,0:T(8,128)(2,1)S(1)}, u32[]{:S(2)}, u32[]{:S(2)}) collective-permute-start(bf16[32,8192]{1,0:T(8,128)(2,1)S(1)} %get-tuple-element.27), channel_id=1, source_target_pairs={{0,6},{1,7},{2,0},{3,1},{4,2},{5,3},{6,4},{7,5},{8,14},{9,15},{10,... | collective-permute-start | bytes 1572872 | tf_op jit(solution)/shard_map/ppermute | solution.py:32
  111.2 1.4 copy-start.9
  111.2 25.0 %copy-start.7 = (bf16[128,8192]{1,0:T(8,128)(2,1)S(1)}, bf16[128,8192]{1,0:T(8,128)(2,1)}, u32[]{:S(2)}) copy-start(bf16[128,8192]{1,0:T(8,128)(2,1)} %copy-done.6) | copy-start | bytes 6291460
  111.2 25.0 %copy-start.15 = (f32[8192]{0:T(1024)S(1)}, f32[8192]{0:T(1024)}, u32[]{:S(2)}) copy-start(f32[8192]{0:T(1024)} %param.20) | copy-start | bytes 98308
  112.6 24.8 %collective-permute-start.16 = (bf16[96,8192]{1,0:T(8,128)(2,1)S(1)}, bf16[96,8192]{1,0:T(8,128)(2,1)S(1)}, u32[]{:S(2)}, u32[]{:S(2)}) collective-permute-start(bf16[96,8192]{1,0:T(8,128)(2,1)S(1)} %copy-done.9), channel_id=1, source_target_pairs={{0,1},{1,0},{2,3},{3,2},{4,5},{5,4},{6,7},{7,6},{8,9},{9,8},{10,11... | collective-permute-start | bytes 4718600 | tf_op jit(solution)/shard_map/ppermute | solution.py:32
  123.8 13.4 %copy-start.20 = (bf16[48,8192]{1,0:T(8,128)(2,1)}, bf16[48,8192]{1,0:T(8,128)(2,1)S(1)}, u32[]{:S(2)}) copy-start(bf16[48,8192]{1,0:T(8,128)(2,1)S(1)} %collective-permute-done.14.refs_6_) | copy-start | bytes 2359300
  123.8 30.0 %collective-permute-start.17 = (bf16[96,8192]{1,0:T(8,128)(2,1)}, bf16[96,8192]{1,0:T(8,128)(2,1)S(1)}, u32[]{:S(2)}, u32[]{:S(2)}) collective-permute-start(bf16[96,8192]{1,0:T(8,128)(2,1)} %collective-permute-done.10.refs_2_), channel_id=1, source_target_pairs={{0,1},{1,0},{2,3},{3,2},{4,5},{5,4},{6,7},{7,6},{8,9},{9,8},{10,11... | collective-permute-start | bytes 4718600 | tf_op jit(solution)/shard_map/ppermute | solution.py:32
  125.8 11.4 %copy-start.21 = (bf16[48,8192]{1,0:T(8,128)(2,1)}, bf16[48,8192]{1,0:T(8,128)(2,1)S(1)}, u32[]{:S(2)}) copy-start(bf16[48,8192]{1,0:T(8,128)(2,1)S(1)} %collective-permute-done.15.refs_7_) | copy-start | bytes 2359300
  125.8 30.7 %collective-permute-start.18 = (bf16[96,8192]{1,0:T(8,128)(2,1)}, bf16[96,8192]{1,0:T(8,128)(2,1)S(1)}, u32[]{:S(2)}, u32[]{:S(2)}) collective-permute-start(bf16[96,8192]{1,0:T(8,128)(2,1)} %collective-permute-done.12.refs_4_), channel_id=1, source_target_pairs={{0,1},{1,0},{2,3},{3,2},{4,5},{5,4},{6,7},{7,6},{8,9},{9,8},{10,11... | collective-permute-start | bytes 4718600 | tf_op jit(solution)/shard_map/ppermute | solution.py:32
  135.1 3.3 %collective-permute-start.19 = (bf16[48,8192]{1,0:T(8,128)(2,1)S(1)}, bf16[48,8192]{1,0:T(8,128)(2,1)S(1)}, u32[]{:S(2)}, u32[]{:S(2)}) collective-permute-start(bf16[48,8192]{1,0:T(8,128)(2,1)S(1)} %collective-permute-done.14.refs_6_), channel_id=1, source_target_pairs={{0,1},{1,0},{2,3},{3,2},{4,5},{5,4},{6,7},{7,6},{8,9},{9,8},{10,11... | collective-permute-start | bytes 2359304 | tf_op jit(solution)/shard_map/ppermute | solution.py:32
  136.2 4.7 %collective-permute-start.20 = (bf16[48,8192]{1,0:T(8,128)(2,1)S(1)}, bf16[48,8192]{1,0:T(8,128)(2,1)S(1)}, u32[]{:S(2)}, u32[]{:S(2)}) collective-permute-start(bf16[48,8192]{1,0:T(8,128)(2,1)S(1)} %collective-permute-done.15.refs_7_), channel_id=1, source_target_pairs={{0,1},{1,0},{2,3},{3,2},{4,5},{5,4},{6,7},{7,6},{8,9},{9,8},{10,11... | collective-permute-start | bytes 2359304 | tf_op jit(solution)/shard_map/ppermute | solution.py:32
  137.4 21.4 %copy-start.10 = (bf16[32,8192]{1,0:T(8,128)(2,1)}, bf16[32,8192]{1,0:T(8,128)(2,1)S(1)}, u32[]{:S(2)}) copy-start(bf16[32,8192]{1,0:T(8,128)(2,1)S(1)} %fusion.14.refs_1_) | copy-start | bytes 1572868
  137.4 21.4 %copy-start.17 = (bf16[96,8192]{1,0:T(8,128)(2,1)}, bf16[96,8192]{1,0:T(8,128)(2,1)S(1)}, u32[]{:S(2)}) copy-start(bf16[96,8192]{1,0:T(8,128)(2,1)S(1)} %collective-permute-done.16.refs_10_) | copy-start | bytes 4718596
  137.5 15.5 %collective-permute-start.11 = (bf16[32,8192]{1,0:T(8,128)(2,1)S(1)}, bf16[32,8192]{1,0:T(8,128)(2,1)S(1)}, u32[]{:S(2)}, u32[]{:S(2)}) collective-permute-start(bf16[32,8192]{1,0:T(8,128)(2,1)S(1)} %fusion.14.refs_1_), channel_id=1, source_target_pairs={{0,2},{1,3},{2,4},{3,5},{4,6},{5,7},{6,0},{7,1},{8,10},{9,11},{10,... | collective-permute-start | bytes 1572872 | tf_op jit(solution)/shard_map/ppermute | solution.py:32
  138.4 20.4 %copy-start.22 = (bf16[48,8192]{1,0:T(8,128)(2,1)}, bf16[48,8192]{1,0:T(8,128)(2,1)S(1)}, u32[]{:S(2)}) copy-start(bf16[48,8192]{1,0:T(8,128)(2,1)S(1)} %collective-permute-done.19.refs_16_) | copy-start | bytes 2359300
  138.4 15.3 %collective-permute-start.13 = (bf16[32,8192]{1,0:T(8,128)(2,1)S(1)}, bf16[32,8192]{1,0:T(8,128)(2,1)S(1)}, u32[]{:S(2)}, u32[]{:S(2)}) collective-permute-start(bf16[32,8192]{1,0:T(8,128)(2,1)S(1)} %fusion.14.refs_1_), channel_id=1, source_target_pairs={{0,6},{1,7},{2,0},{3,1},{4,2},{5,3},{6,4},{7,5},{8,14},{9,15},{10,... | collective-permute-start | bytes 1572872 | tf_op jit(solution)/shard_map/ppermute | solution.py:32
  140.9 25.7 %copy-start.23 = (bf16[48,8192]{1,0:T(8,128)(2,1)}, bf16[48,8192]{1,0:T(8,128)(2,1)S(1)}, u32[]{:S(2)}) copy-start(bf16[48,8192]{1,0:T(8,128)(2,1)S(1)} %collective-permute-done.20.refs_17_) | copy-start | bytes 2359300
  140.9 17.9 %collective-permute-start.23 = (bf16[32,8192]{1,0:T(8,128)(2,1)S(1)}, bf16[32,8192]{1,0:T(8,128)(2,1)S(1)}, u32[]{:S(2)}, u32[]{:S(2)}) collective-permute-start(bf16[32,8192]{1,0:T(8,128)(2,1)S(1)} %fusion.14.refs_1_), channel_id=1, source_target_pairs={{0,1},{1,0},{2,3},{3,2},{4,5},{5,4},{6,7},{7,6},{8,9},{9,8},{10,11... | collective-permute-start | bytes 1572872 | tf_op jit(solution)/shard_map/ppermute | solution.py:32
  153.0 5.9 %copy-start.12 = (bf16[32,8192]{1,0:T(8,128)(2,1)}, bf16[32,8192]{1,0:T(8,128)(2,1)S(1)}, u32[]{:S(2)}) copy-start(bf16[32,8192]{1,0:T(8,128)(2,1)S(1)} %collective-permute-done.11.refs_3_) | copy-start | bytes 1572868
  153.0 9.3 %collective-permute-start.24 = (bf16[32,8192]{1,0:T(8,128)(2,1)S(1)}, bf16[32,8192]{1,0:T(8,128)(2,1)S(1)}, u32[]{:S(2)}, u32[]{:S(2)}) collective-permute-start(bf16[32,8192]{1,0:T(8,128)(2,1)S(1)} %collective-permute-done.11.refs_3_), channel_id=1, source_target_pairs={{0,1},{1,0},{2,3},{3,2},{4,5},{5,4},{6,7},{7,6},{8,9},{9,8},{10,11... | collective-permute-start | bytes 1572872 | tf_op jit(solution)/shard_map/ppermute | solution.py:32
  153.7 5.2 %copy-start.13 = (bf16[32,8192]{1,0:T(8,128)(2,1)}, bf16[32,8192]{1,0:T(8,128)(2,1)S(1)}, u32[]{:S(2)}) copy-start(bf16[32,8192]{1,0:T(8,128)(2,1)S(1)} %collective-permute-done.13.refs_5_) | copy-start | bytes 1572868
  153.7 8.5 %collective-permute-start.25 = (bf16[32,8192]{1,0:T(8,128)(2,1)S(1)}, bf16[32,8192]{1,0:T(8,128)(2,1)S(1)}, u32[]{:S(2)}, u32[]{:S(2)}) collective-permute-start(bf16[32,8192]{1,0:T(8,128)(2,1)S(1)} %collective-permute-done.13.refs_5_), channel_id=1, source_target_pairs={{0,1},{1,0},{2,3},{3,2},{4,5},{5,4},{6,7},{7,6},{8,9},{9,8},{10,11... | collective-permute-start | bytes 1572872 | tf_op jit(solution)/shard_map/ppermute | solution.py:32
  153.8 5.0 %copy-start.18 = (bf16[96,8192]{1,0:T(8,128)(2,1)}, bf16[96,8192]{1,0:T(8,128)(2,1)S(1)}, u32[]{:S(2)}) copy-start(bf16[96,8192]{1,0:T(8,128)(2,1)S(1)} %collective-permute-done.17.refs_12_) | copy-start | bytes 4718596
  153.8 8.4 %collective-permute-start.22 = (bf16[16,8192]{1,0:T(8,128)(2,1)S(1)}, bf16[16,8192]{1,0:T(8,128)(2,1)S(1)}, u32[]{:S(2)}, u32[]{:S(2)}) collective-permute-start(bf16[16,8192]{1,0:T(8,128)(2,1)S(1)} %slice.75), channel_id=1, source_target_pairs={{0,6},{1,7},{2,0},{3,1},{4,2},{5,3},{6,4},{7,5},{8,14},{9,15},{10,... | collective-permute-start | bytes 786440 | tf_op jit(solution)/shard_map/ppermute | solution.py:32
  156.6 8.9 %copy-start.19 = (bf16[96,8192]{1,0:T(8,128)(2,1)}, bf16[96,8192]{1,0:T(8,128)(2,1)S(1)}, u32[]{:S(2)}) copy-start(bf16[96,8192]{1,0:T(8,128)(2,1)S(1)} %collective-permute-done.18.refs_14_) | copy-start | bytes 4718596
  156.6 8.9 %collective-permute-start.21 = (bf16[16,8192]{1,0:T(8,128)(2,1)S(1)}, bf16[16,8192]{1,0:T(8,128)(2,1)S(1)}, u32[]{:S(2)}, u32[]{:S(2)}) collective-permute-start(bf16[16,8192]{1,0:T(8,128)(2,1)S(1)} %slice.62), channel_id=1, source_target_pairs={{0,2},{1,3},{2,4},{3,5},{4,6},{5,7},{6,0},{7,1},{8,10},{9,11},{10,... | collective-permute-start | bytes 786440 | tf_op jit(solution)/shard_map/ppermute | solution.py:32
  158.9 7.7 %copy-start.24 = (bf16[32,8192]{1,0:T(8,128)(2,1)}, bf16[32,8192]{1,0:T(8,128)(2,1)S(1)}, u32[]{:S(2)}) copy-start(bf16[32,8192]{1,0:T(8,128)(2,1)S(1)} %collective-permute-done.23.refs_11_) | copy-start | bytes 1572868
  162.3 4.4 %copy-start.27 = (bf16[16,8192]{1,0:T(8,128)(2,1)}, bf16[16,8192]{1,0:T(8,128)(2,1)S(1)}, u32[]{:S(2)}) copy-start(bf16[16,8192]{1,0:T(8,128)(2,1)S(1)} %collective-permute-done.22.refs_9_) | copy-start | bytes 786436
  162.3 4.4 %copy-start.25 = (bf16[32,8192]{1,0:T(8,128)(2,1)}, bf16[32,8192]{1,0:T(8,128)(2,1)S(1)}, u32[]{:S(2)}) copy-start(bf16[32,8192]{1,0:T(8,128)(2,1)S(1)} %collective-permute-done.24.refs_13_) | copy-start | bytes 1572868
  162.3 4.4 %copy-start.26 = (bf16[32,8192]{1,0:T(8,128)(2,1)}, bf16[32,8192]{1,0:T(8,128)(2,1)S(1)}, u32[]{:S(2)}) copy-start(bf16[32,8192]{1,0:T(8,128)(2,1)S(1)} %collective-permute-done.25.refs_15_) | copy-start | bytes 1572868
  162.3 4.4 %collective-permute-start.27 = (bf16[16,8192]{1,0:T(8,128)(2,1)S(1)}, bf16[16,8192]{1,0:T(8,128)(2,1)S(1)}, u32[]{:S(2)}, u32[]{:S(2)}) collective-permute-start(bf16[16,8192]{1,0:T(8,128)(2,1)S(1)} %collective-permute-done.22.refs_9_), channel_id=1, source_target_pairs={{0,1},{1,0},{2,3},{3,2},{4,5},{5,4},{6,7},{7,6},{8,9},{9,8},{10,11... | collective-permute-start | bytes 786440 | tf_op jit(solution)/shard_map/ppermute | solution.py:32
  165.5 1.2 copy-start.28
  165.5 2.3 %collective-permute-start.26 = (bf16[16,8192]{1,0:T(8,128)(2,1)S(1)}, bf16[16,8192]{1,0:T(8,128)(2,1)S(1)}, u32[]{:S(2)}, u32[]{:S(2)}) collective-permute-start(bf16[16,8192]{1,0:T(8,128)(2,1)S(1)} %collective-permute-done.21.refs_8_), channel_id=1, source_target_pairs={{0,1},{1,0},{2,3},{3,2},{4,5},{5,4},{6,7},{7,6},{8,9},{9,8},{10,11... | collective-permute-start | bytes 786440 | tf_op jit(solution)/shard_map/ppermute | solution.py:32
  166.7 1.8 copy-start.29
  167.8 0.7 copy-start.30
  168.5 32.0 %copy-start.1 = (bf16[5120,320]{0,1:T(8,128)(2,1)S(1)}, bf16[5120,320]{0,1:T(8,128)(2,1)}, u32[]{:S(2)}) copy-start(bf16[5120,320]{0,1:T(8,128)(2,1)} %param.17) | copy-start | bytes 9830404
Sparse Core Ops, SparseCore 0:
  10.2 138.6 all-gather.1
